TPU v7x, 32 devices: a whole 2x2x4 slice. The times are simulated.
32 devices in a mesh: dp: 4 (over y, x), expert: 8 (over z, core).
Axes of the slice: x: 2, y: 2, z: 4, core: 2. Of those that a mesh axis runs over, the one named last changes fastest.
Arguments:
- tokens: bfloat16 [4096, 2048], P(('dp', 'expert')), may hold values from -6 to 6
- expert_ids: int32 [4096, 2], P(('dp', 'expert')), may hold values from 0 to 7, all different within a row; in each aligned block of 128 rows (0 to 127, 128 to 255, ...) at most 40 rows name the same one
- gate_units: int32 [4096, 2], P(('dp', 'expert')), may hold values from 64 to 1023
- capacity: int32 [8], replicated, may hold values from 512 to 1535
- w_gate: bfloat16 [8, 2048, 1408], P('expert', None, 'dp'), may hold values from -0.125 to 0.125
- w_up: bfloat16 [8, 2048, 1408], P('expert', None, 'dp'), may hold values from -0.125 to 0.125
- w_down: bfloat16 [8, 2048, 1408], P('expert', None, 'dp'), may hold values from -0.15625 to 0.15625
Outputs:
- mixed: bfloat16 [4096, 2048], P(('dp', 'expert'))
Inputs may be any that keep to these rules, and one draw needn't show every extreme that they name: `expert_ids`: each row names two different experts; of one device's 128 rows (aligned blocks) no expert is named more than 40 times.
All inputs are finite; a program needn't handle non-finite values.
Results may differ from a plain program's by a relative error of at most 0.0057.
Values may be sent and summed in bfloat16 or wider, within the bound.
No kernel may reach another device: no remote copies, remote signals or barrier semaphores. Data moves between devices by JAX's collectives and lax.ppermute only.
A program may use at most 128 MiB of HBM per device.

v0:
```python
import jax
import jax.numpy as jnp
from jax import lax
from jax.sharding import PartitionSpec as P


def prefix(shard, axis, combine, identity):
    length, here = (lax.axis_size(axis), lax.axis_index(axis))
    everything = lax.all_gather(shard, axis)
    start = jnp.broadcast_to(jnp.asarray(identity, shard.dtype), shard.shape)

    def step(k, before):
        reached = k < here
        new = combine(before, everything[k])
        return jnp.where(reached, new, before)

    return lax.fori_loop(0, length, step, start)


def expert_rows(rows, gate_w, up_w, down_w):
    gate = jnp.dot(rows, gate_w, preferred_element_type=jnp.float32)
    up = jnp.dot(rows, up_w, preferred_element_type=jnp.float32)
    hidden = (jax.nn.silu(gate) * up).astype(jnp.bfloat16)
    return lax.dot_general(
        hidden, down_w, (((1,), (1,)), ((), ())), preferred_element_type=jnp.float32
    )


def add_counts(earlier, later):
    return earlier + later


def local(tokens, expert_ids, gate_units, capacity, w_gate, w_up, w_down):
    tok_rows = tokens.shape[0]
    width = tokens.shape[1]
    n_experts = capacity.shape[0]
    most = max(2, 5 * tok_rows // (2 * n_experts))
    slots_all = n_experts * most
    flat = expert_ids.reshape(-1)
    onehot = (flat[:, None] == jnp.arange(n_experts, dtype=jnp.int32)[None, :]).astype(jnp.int32)
    local_rank = jnp.sum((jnp.cumsum(onehot, axis=0) - onehot) * onehot, axis=1)
    counts = jnp.sum(onehot, axis=0)
    offsets = prefix(counts, ("dp", "expert"), add_counts, jnp.zeros_like(counts))
    global_slot = jnp.sum(onehot * offsets[None, :], axis=1) + local_rank
    limit = jnp.sum(onehot * capacity[None, :], axis=1)
    kept = global_slot < limit
    weight = jnp.where(kept, gate_units.reshape(-1).astype(jnp.float32) / 1024.0, jnp.float32(0.0))
    send_slot = flat * most + local_rank
    chosen = (send_slot[None, :] == jnp.arange(slots_all, dtype=jnp.int32)[:, None]) & kept[None, :]
    placing = jnp.sum(chosen.reshape(slots_all, tok_rows, 2).astype(jnp.int32), axis=2).astype(
        jnp.bfloat16
    )
    outgoing = jnp.dot(placing, tokens, preferred_element_type=jnp.float32).astype(jnp.bfloat16)
    outgoing = outgoing.reshape(n_experts, most, width)
    arrived = lax.all_to_all(outgoing, "expert", split_axis=0, concat_axis=0, tiled=True).reshape(
        slots_all, width
    )
    produced = expert_rows(
        arrived,
        lax.all_gather(w_gate, "dp", axis=2, tiled=True)[0],
        lax.all_gather(w_up, "dp", axis=2, tiled=True)[0],
        lax.all_gather(w_down, "dp", axis=2, tiled=True)[0],
    )
    answer = produced.astype(jnp.bfloat16).reshape(n_experts, most, width)
    back = lax.all_to_all(answer, "expert", split_axis=0, concat_axis=0, tiled=True).reshape(
        slots_all, width
    )
    picked = back[send_slot].astype(jnp.float32) * weight[:, None]
    mixed = jnp.sum(picked.reshape(tok_rows, 2, width), axis=1)
    return mixed.astype(jnp.bfloat16)


def solution(mesh):
    return jax.shard_map(
        local,
        mesh=mesh,
        in_specs=(
            P(("dp", "expert"), None),
            P(("dp", "expert"), None),
            P(("dp", "expert"), None),
            P(),
            P("expert", None, "dp"),
            P("expert", None, "dp"),
            P("expert", None, "dp"),
        ),
        out_specs=P(("dp", "expert"), None),
        check_vma=False,
    )
```

profile of v0, /device:TPU:0, one launch (start us, length us, event | category | flops | bytes accessed | tf_op | source)
XLA Modules:
  0.0 275.7 jit_solution(2728513415111079550)
XLA Ops:
  6.5 0.0 copy-start
  6.5 0.0 all-gather.5.cloned.1.call-start
  6.5 0.7 all-gather.5.cloned.1.call-update
  7.3 0.0 copy-start.1
  7.3 0.0 copy-start.3
  7.3 0.0 copy-start.2
  7.3 0.0 all-gather.7.cloned.1.call-start
  7.3 0.7 all-gather.7.cloned.1.call-update
  8.0 0.0 all-gather.9.cloned.1.call-start
  8.1 0.7 all-gather.9.cloned.1.call-update
  8.8 0.0 copy-done.1
  8.8 0.1 copy.23
  8.9 0.1 eq.39
  9.1 0.1 eq.43
  9.2 0.1 convert_reduce_fusion.1
  9.3 0.2 dynamic-update-slice
  9.6 42.6 %all-reduce = s32[256]{0:T(256)S(1)} all-reduce(s32[256]{0:T(256)S(1)} %dynamic-update-slice), channel_id=2, replica_groups=mesh['dp'=4,'expert'=8] {'dp','expert'}, use_global_device_ids=true, to_apply=%add | all-reduce | flops 256 | bytes 2048
  52.1 0.1 reshape.134
  52.2 0.6 reduce-window.6
  52.8 0.2 slice_reduce_fusion
  53.1 1.3 while.14
  54.4 0.0 copy-done.3
  54.4 0.1 select_reduce_fusion.1
  54.5 0.1 reduce_sum.63
  54.6 0.1 copy.28
  54.7 0.2 reduce_sum.66
  54.8 0.1 copy.27
  54.9 0.2 reduce_sum.68
  55.1 0.1 copy.29
  55.2 0.1 copy.26
  55.2 0.0 copy-done.2
  55.3 0.0 copy-done
  55.3 0.5 convolution_convert_fusion
  55.8 35.6 %all_to_all.10 = bf16[8,40,2048]{2,1,0:T(8,128)(2,1)S(1)} all-to-all(bf16[8,40,2048]{2,1,0:T(8,128)(2,1)S(1)} %bitcast.35), channel_id=1, replica_groups=mesh['dp'=4,'expert'=8] {'expert'}, dimensions={0} | all-to-all | bytes 2621440 | tf_op jit(solution)/shard_map/all_to_all | solution.py:55
  91.4 0.0 all-gather.5.cloned.1.call-done
  91.4 6.1 %fusion.4 = f32[320,1408]{1,0:T(8,128)} fusion(bf16[320,2048]{1,0:T(8,128)(2,1)S(1)} %bitcast.36, bf16[1,2048,1408]{1,2,0:T(8,128)(2,1)} %all-gather.5.cloned.1.call-done), kind=kOutput, calls=%fused_computation.7 | convolution fusion | flops 1845493760 | bytes 8880128 | tf_op jit(solution)/shard_map/dot_general | solution.py:21
  97.5 48.3 %all-gather.7.cloned.1.call-done = bf16[1,2048,1408]{1,2,0:T(8,128)(2,1)} async-done(((bf16[1,2048,352]{1,2,0:T(8,128)(2,1)}), bf16[1,2048,1408]{1,2,0:T(8,128)(2,1)}) %all-gather.7.cloned.1.call-update) | async-done | bytes 5767184 | tf_op jit(solution)/shard_map/all_gather | solution.py:61
  145.8 67.5 %all-gather.9.cloned.1.call-done = bf16[1,2048,1408]{1,2,0:T(8,128)(2,1)} async-done(((bf16[1,2048,352]{1,2,0:T(8,128)(2,1)}), bf16[1,2048,1408]{1,2,0:T(8,128)(2,1)}) %all-gather.9.cloned.1.call-update) | async-done | bytes 5767184 | tf_op jit(solution)/shard_map/all_gather | solution.py:62
  213.4 10.3 %fusion.9 = bf16[320,2048]{1,0:T(8,128)(2,1)} fusion(bf16[1,2048,1408]{1,2,0:T(8,128)(2,1)} %all-gather.9.cloned.1.call-done, bf16[320,2048]{1,0:T(8,128)(2,1)S(1)} %bitcast.37, bf16[1,2048,1408]{1,2,0:T(8,128)(2,1)} %all-gather.7.cloned.1.call-done, f32[320,1408]{1,0:T(8,128)} %fusion.4), kind=kOutput, calls=%fused_computation.10 | convolution fusion | flops 3694346240 | bytes 15958016 | tf_op jit(solution)/shard_map/dot_general | solution.py:24
  223.7 4.6 %all-to-all-start.1 = ((bf16[8,40,2048]{2,1,0:T(8,128)(2,1)}), bf16[8,40,2048]{2,1,0:T(8,128)(2,1)S(1)}, u32[]{:S(2)}, u32[]{:S(2)}) async-start(bf16[8,40,2048]{2,1,0:T(8,128)(2,1)} %bitcast.7), calls=%async_computation.1 | async-start | bytes 2621440 | tf_op jit(solution)/shard_map/all_to_all | solution.py:65
  228.3 0.1 mul.68
  228.4 0.1 copy.30
  228.5 31.9 %all-to-all-done.1 = bf16[8,40,2048]{2,1,0:T(8,128)(2,1)S(1)} async-done(((bf16[8,40,2048]{2,1,0:T(8,128)(2,1)}), bf16[8,40,2048]{2,1,0:T(8,128)(2,1)S(1)}, u32[]{:S(2)}, u32[]{:S(2)}) %all-to-all-start.1) | async-done | bytes 1310752 | tf_op jit(solution)/shard_map/all_to_all | solution.py:65
  260.5 2.3 gather_fusion
  262.8 2.4 reshape.125
  265.2 4.0 %multiply_reduce_fusion = bf16[128,2048]{1,0:T(8,128)(2,1)} fusion(f32[128,2,2048]{2,1,0:T(2,128)S(1)} %reshape.125, f32[128,2]{1,0:T(8,128)S(1)} %copy.30), kind=kLoop, calls=%fused_computation.13 | loop fusion | flops 786432 | bytes 2622464 | tf_op jit(solution)/shard_map/reduce_sum | solution.py:69
  (42 shorter events, 0.7 us)
Async XLA Ops:
  6.5 48.8 %copy-start = (bf16[128,2048]{1,0:T(8,128)(2,1)S(1)}, bf16[128,2048]{1,0:T(8,128)(2,1)}, u32[]{:S(2)}) copy-start(bf16[128,2048]{1,0:T(8,128)(2,1)} %param.9) | copy-start | bytes 1572868
  6.5 84.9 %all-gather.5.cloned.1.call-start = ((), (), s32[]{:S(2)}) async-start(), calls=%async_computation.2 | async-start | bytes 7208960 | tf_op jit(solution)/shard_map/all_gather | solution.py:60
  7.3 1.5 copy-start.1
  7.3 47.1 %copy-start.3 = (s32[8]{0:T(128)S(1)}, s32[8]{0:T(128)}, u32[]{:S(2)}) copy-start(s32[8]{0:T(128)} %param.12) | copy-start | bytes 100
  7.3 47.9 %copy-start.2 = (s32[128,2]{0,1:T(2,128)S(1)}, s32[128,2]{0,1:T(2,128)}, u32[]{:S(2)}) copy-start(s32[128,2]{0,1:T(2,128)} %param.11) | copy-start | bytes 3076
  7.3 138.6 %all-gather.7.cloned.1.call-start = ((), (), s32[]{:S(2)}) async-start(), calls=%async_computation.3 | async-start | bytes 7208960 | tf_op jit(solution)/shard_map/all_gather | solution.py:61
  8.0 205.4 %all-gather.9.cloned.1.call-start = ((), (), s32[]{:S(2)}) async-start(), calls=%async_computation.4 | async-start | bytes 7208960 | tf_op jit(solution)/shard_map/all_gather | solution.py:62
  223.7 36.8 %all-to-all-start.1 = ((bf16[8,40,2048]{2,1,0:T(8,128)(2,1)}), bf16[8,40,2048]{2,1,0:T(8,128)(2,1)S(1)}, u32[]{:S(2)}, u32[]{:S(2)}) async-start(bf16[8,40,2048]{2,1,0:T(8,128)(2,1)} %bitcast.7), calls=%async_computation.1 | async-start | bytes 2621440 | tf_op jit(solution)/shard_map/all_to_all | solution.py:65
Sparse Core Ops, SparseCore 0:
  9.2 69.0 all-gather.4
  80.1 65.6 all-gather.6
  147.7 65.6 all-gather.8
where the time goes:
time: 276 us
  waiting for transfers between devices  150 us (54%)
  blocking collectives  78.1 us (28%)
  matrix products  16.9 us (6%)
  between operations  13.3 us (5%)
  local copies, waits for them, and re-layouts  6.6 us (2%)
  other arithmetic  5.55 us (2%)
  starting transfers between devices  4.68 us (2%)
    all_gather x1, waiting for transfers between devices, local(): lax.all_gather(w_down, 'dp', axis=2, tiled=True)[0]  67.5 us
    all_gather x1, waiting for transfers between devices, local(): lax.all_gather(w_up, 'dp', axis=2, tiled=True)[0]  48.3 us
    unnamed x1, blocking collectives  42.6 us
    all_to_all x1, blocking collectives, local(): lax.all_to_all(outgoing, 'expert', split_axis=0, concat_axis=0, tiled=True)  35.6 us
    all_to_all x1, waiting for transfers between devices, local(): lax.all_to_all(answer, 'expert', split_axis=0, concat_axis=0, tiled=True)  31.9 us
    dot_general x1, matrix products, expert_rows(): lax.dot_general(hidden, down_w, (((1,), (1,)), ((), ())), preferred_eleme...  10.3 us
    dot_general x1, matrix products, expert_rows(): gate = jnp.dot(rows, gate_w, preferred_element_type=jnp.float32)  6.11 us
  transfers between devices with their start and end apart: 4, of which 3 were waited for; matrix products, arithmetic and copies ran while one was open for 4% of the time, Pallas kernels for 0%

commit v1 on v0

v1 whole, which is shorter than its diff:
```python
import jax
import jax.numpy as jnp
from jax import lax
from jax.sharding import PartitionSpec as P

BF16 = jnp.bfloat16
F32 = jnp.float32
AXES = ("dp", "expert")


def far_first(n):
    return sorted(range(1, n), key=lambda k: (-(k // 2), k))


def pair_permute(values, n_dp, n_exp, weights_side):
    pairs = []
    for d in range(n_dp):
        for e in range(n_exp):
            high = (e % 2 == 0) == weights_side
            partner = d ^ (n_dp // 2) if high else d ^ 1
            pairs.append((d * n_exp + e, partner * n_exp + e))
    return lax.ppermute(values, AXES, pairs)


def few(n):
    return n - 1 <= 16


def expert_exchange(blocks):
    n = lax.axis_size("expert")
    if not few(n):
        place = jnp.arange(n, dtype=jnp.int32) ^ lax.axis_index("expert")
        there = lax.all_to_all(jnp.stack(blocks)[place], "expert", 0, 0, tiled=True)[place]
        return [there[k] for k in range(n)]
    out = [blocks[0]] + [None] * (n - 1)
    for k in far_first(n):
        out[k] = lax.ppermute(blocks[k], "expert", [(i, i ^ k) for i in range(n)])
    return out


def earlier_counts(counts, late):
    n = lax.axis_size("dp") * lax.axis_size("expert")
    me = lax.axis_index(AXES)
    total, before = counts, jnp.zeros_like(counts)
    step = 1
    while step < n:
        if step == lax.axis_size("expert"):
            total, _ = lax.optimization_barrier((total, late))
        other = lax.ppermute(total, AXES, [(i, i ^ step) for i in range(n)])
        before = before + jnp.where((me & step) != 0, other, 0)
        total = total + other
        step *= 2
    return before


def dot(a, b):
    return jnp.dot(a, b, preferred_element_type=F32)


def hidden_of(rows, gate_w, up_w):
    return (jax.nn.silu(dot(rows, gate_w)) * dot(rows, up_w)).astype(BF16)


def down(hidden, w):
    return lax.dot_general(hidden, w, (((1,), (1,)), ((), ())), preferred_element_type=F32)


def layer(tokens, expert_ids, gate_units, capacity, w_gate, w_up, w_down):
    n_dp, n_exp = lax.axis_size("dp"), lax.axis_size("expert")
    tok_rows, width = tokens.shape
    n_experts = capacity.shape[0]
    most = max(2, 5 * tok_rows // (2 * n_experts))
    me = lax.axis_index("expert")
    wg, wu, wd = w_gate[0], w_up[0], w_down[0]
    wg2 = pair_permute(wg, n_dp, n_exp, True)
    wu2 = pair_permute(wu, n_dp, n_exp, True)
    wd2 = pair_permute(wd, n_dp, n_exp, True)

    places = jnp.arange(n_experts, dtype=jnp.int32)
    away = expert_ids ^ me
    named = away[:, :, None] == places[None, None, :]
    once = jnp.any(named, axis=1)
    t = jnp.arange(tok_rows, dtype=jnp.int32)
    lower = (t[:, None] > t[None, :]).astype(BF16)
    rank = dot(lower, once.astype(BF16)).astype(jnp.int32)
    slot = jnp.where(once, rank, most).T
    chosen = slot[:, None, :] == jnp.arange(most, dtype=jnp.int32)[None, :, None]
    chosen = chosen.reshape(n_experts * most, tok_rows)
    outgoing = dot(chosen.astype(BF16), tokens).astype(BF16).reshape(n_experts, most, width)

    arrived = jnp.concatenate(expert_exchange([outgoing[k] for k in range(n_experts)]), axis=0)
    theirs = pair_permute(arrived, n_dp, n_exp, False)

    part_theirs = down(hidden_of(theirs, wg, wu), wd) + down(hidden_of(theirs, wg2, wu2), wd2)
    returned = pair_permute(part_theirs.astype(BF16), n_dp, n_exp, False)
    part_own = down(hidden_of(arrived, wg, wu), wd) + down(hidden_of(arrived, wg2, wu2), wd2)
    answer = (part_own + returned.astype(F32)).astype(BF16).reshape(n_experts, most, width)
    back = jnp.concatenate(expert_exchange([answer[k] for k in range(n_experts)]), axis=0)

    counts = jnp.sum((expert_ids[:, :, None] == places).astype(jnp.int32), axis=(0, 1))
    counts, _ = lax.optimization_barrier((counts, arrived[0, 0]))
    room = capacity - earlier_counts(counts, answer[0, 0, 0])
    room_of = jnp.sum(jnp.where(expert_ids[:, :, None] == places, room, 0), axis=2)
    rank_of = jnp.sum(jnp.where(named, rank[:, None, :], 0), axis=2)
    units = jnp.where(rank_of < room_of, gate_units, 0)
    unit_at = jnp.sum(jnp.where(named, units[:, :, None], 0), axis=1)
    high = (unit_at // 8 * 8).astype(F32) / 1024.0
    low = (unit_at % 8).astype(F32) / 1024.0

    picks = chosen.reshape(n_experts, most, tok_rows)
    high_at = jnp.where(picks, high.T[:, None, :], 0.0).astype(BF16).reshape(n_experts * most, tok_rows)
    low_at = jnp.where(picks, low.T[:, None, :], 0.0).astype(BF16).reshape(n_experts * most, tok_rows)
    across = (((0,), (0,)), ((), ()))
    mixed = lax.dot_general(high_at, back, across, preferred_element_type=F32)
    mixed = mixed + lax.dot_general(low_at, back, across, preferred_element_type=F32)
    return mixed.astype(BF16)


def solution(mesh):
    return jax.shard_map(
        layer,
        mesh=mesh,
        in_specs=(
            P(AXES, None),
            P(AXES, None),
            P(AXES, None),
            P(),
            P("expert", None, "dp"),
            P("expert", None, "dp"),
            P("expert", None, "dp"),
        ),
        out_specs=P(AXES, None),
        check_vma=False,
    )
```

time: 276 us -> 183 us (0.66)
  blocking collectives: 78.1 us -> 0 us
  waiting for transfers between devices: 150 us -> 106 us
  starting transfers between devices: 4.68 us -> 30.3 us
  matrix products: 16.9 us -> 37.3 us
  between operations: 13.3 us -> 0.18 us
  other arithmetic: 5.55 us -> 1.26 us
    all_gather x3 -> x0, waiting for transfers between devices: 116 us -> none  [the longest x1 67.5 us: local(): lax.all_gather(w_down, 'dp', axis=2, tiled=True)[0]]
    ppermute x0 -> x24, waiting for transfers between devices: none -> 106 us  [the longest x5 55.5 us: earlier_counts(): other = lax.ppermute(total, AXES, [(i, i ^ step) for i in range(n)])]
    unnamed x1 -> x0, blocking collectives: 42.6 us -> none
    all_to_all x1 -> x0, blocking collectives: 35.6 us -> none  [local(): lax.all_to_all(outgoing, 'expert', split_axis=0, concat_axis=0, tiled=True)]
    all_to_all x1 -> x0, waiting for transfers between devices: 31.9 us -> none  [local(): lax.all_to_all(answer, 'expert', split_axis=0, concat_axis=0, tiled=True)]
    ppermute x0 -> x24, starting transfers between devices: none -> 30.3 us  [the longest x14 20.8 us: expert_exchange(): out[k] = lax.ppermute(blocks[k], 'expert', [(i, i ^ k) for i in range(n)])]
    dot_general x3 -> x12, matrix products: 16.9 us -> 37.3 us  [the longest x4 21.3 us: down(): lax.dot_general(hidden, w, (((1,), (1,)), ((), ())), preferred_element_ty...]
    all_to_all x1 -> x0, starting transfers between devices: 4.61 us -> none  [local(): lax.all_to_all(answer, 'expert', split_axis=0, concat_axis=0, tiled=True)]
  transfers between devices with their start and end apart: 4 -> 24, of which waited for: 3 -> 9; matrix products, arithmetic and copies ran while one was open for 4% -> 16% of each run, Pallas kernels for 0% -> 0%
where the time goes in v1:
time: 183 us; the launch traced here: 182 us
  waiting for transfers between devices  106 us (58%)
  matrix products  37.3 us (20%)
  starting transfers between devices  30.3 us (17%)
  local copies, waits for them, and re-layouts  7.18 us (4%)
    ppermute x5, waiting for transfers between devices, earlier_counts(): other = lax.ppermute(total, AXES, [(i, i ^ step) for i in range(n)])  55.5 us
    ppermute x14, waiting for transfers between devices, expert_exchange(): out[k] = lax.ppermute(blocks[k], 'expert', [(i, i ^ k) for i in range(n)])  46.2 us
    dot_general x4, matrix products, down(): lax.dot_general(hidden, w, (((1,), (1,)), ((), ())), preferred_element_ty...  21.3 us
    ppermute x14, starting transfers between devices, expert_exchange(): out[k] = lax.ppermute(blocks[k], 'expert', [(i, i ^ k) for i in range(n)])  20.8 us
    dot_general x6, matrix products, dot(): return jnp.dot(a, b, preferred_element_type=F32)  14.3 us
    ppermute x5, starting transfers between devices, pair_permute(): return lax.ppermute(values, AXES, pairs)  6.59 us
    ppermute x5, waiting for transfers between devices, pair_permute(): return lax.ppermute(values, AXES, pairs)  4.18 us
    unnamed x20, local copies, waits for them, and re-layouts  4.13 us
  transfers between devices with their start and end apart: 24, of which 9 were waited for; matrix products, arithmetic and copies ran while one was open for 16% of the time, Pallas kernels for 0%

profile of v1, /device:TPU:0, one launch (start us, length us, event | category | flops | bytes accessed | tf_op | source)
XLA Modules:
  0.0 182.1 jit_solution(7958559847258245405)
XLA Ops:
  0.0 0.7 broadcast_xor_fusion
  0.8 0.1 convolution_convert_fusion.1
  1.1 0.5 convolution_convert_fusion
  1.6 0.8 fusion.49
  2.4 0.5 collective-permute-start.5
  2.9 4.7 %collective-permute-start.11 = (bf16[40,2048]{1,0:T(8,128)(2,1)S(1)}, bf16[40,2048]{1,0:T(8,128)(2,1)S(1)}, u32[]{:S(2)}, u32[]{:S(2)}) collective-permute-start(bf16[40,2048]{1,0:T(8,128)(2,1)S(1)} %get-tuple-element.13), channel_id=1, source_target_pairs={{0,7},{1,6},{2,5},{3,4},{4,3},{5,2},{6,1},{7,0},{8,15},{9,14},{10,... | collective-permute-start | bytes 491528 | tf_op jit(solution)/shard_map/ppermute | solution.py:37
  7.6 0.3 collective-permute-start.9
  8.0 2.3 %collective-permute-start.8 = (bf16[40,2048]{1,0:T(8,128)(2,1)S(1)}, bf16[40,2048]{1,0:T(8,128)(2,1)S(1)}, u32[]{:S(2)}, u32[]{:S(2)}) collective-permute-start(bf16[40,2048]{1,0:T(8,128)(2,1)S(1)} %get-tuple-element.16), channel_id=1, source_target_pairs={{0,4},{1,5},{2,6},{3,7},{4,0},{5,1},{6,2},{7,3},{8,12},{9,13},{10,... | collective-permute-start | bytes 491528 | tf_op jit(solution)/shard_map/ppermute | solution.py:37
  10.3 1.7 collective-permute-start.6
  12.0 0.7 constant_dynamic-update-slice_fusion.6
  12.7 13.0 %collective-permute-done.6 = bf16[40,2048]{1,0:T(8,128)(2,1)S(1)} collective-permute-done((bf16[40,2048]{1,0:T(8,128)(2,1)S(1)}, bf16[40,2048]{1,0:T(8,128)(2,1)S(1)}, u32[]{:S(2)}, u32[]{:S(2)}) %collective-permute-start.6) | collective-permute-done | bytes 163872 | tf_op jit(solution)/shard_map/ppermute | solution.py:37
  25.7 1.5 collective-permute-start.7
  27.2 0.7 constant_dynamic-update-slice_fusion.5
  27.9 10.6 %collective-permute-done.7 = bf16[40,2048]{1,0:T(8,128)(2,1)S(1)} collective-permute-done((bf16[40,2048]{1,0:T(8,128)(2,1)S(1)}, bf16[40,2048]{1,0:T(8,128)(2,1)S(1)}, u32[]{:S(2)}, u32[]{:S(2)}) %collective-permute-start.7) | collective-permute-done | bytes 163872 | tf_op jit(solution)/shard_map/ppermute | solution.py:37
  38.5 0.7 constant_dynamic-update-slice_fusion.4
  39.1 0.7 constant_dynamic-update-slice_fusion.3
  39.8 0.7 constant_dynamic-update-slice_fusion.2
  40.5 0.7 constant_dynamic-update-slice_fusion.1
  41.2 0.7 constant_dynamic-update-slice_fusion
  41.9 1.5 collective-permute-start.15
  43.3 1.5 collective-permute-start.12
  45.1 0.6 collective-permute-start.14
  45.6 1.5 collective-permute-start.13
  47.3 3.5 %collective-permute-done.1 = s32[8]{0:T(128)S(1)} collective-permute-done((s32[8]{0:T(128)S(1)}, s32[8]{0:T(128)S(1)}, u32[]{:S(2)}, u32[]{:S(2)}) %collective-permute-start.1) | collective-permute-done | bytes 64 | tf_op jit(solution)/shard_map/ppermute | solution.py:49
  50.8 4.5 %collective-permute-done.2 = s32[8]{0:T(128)S(1)} collective-permute-done((s32[8]{0:T(128)S(1)}, s32[8]{0:T(128)S(1)}, u32[]{:S(2)}, u32[]{:S(2)}) %collective-permute-start.2) | collective-permute-done | bytes 64 | tf_op jit(solution)/shard_map/ppermute | solution.py:49
  55.3 0.5 collective-permute-start.3
  55.8 17.4 %collective-permute-done.3 = s32[8]{0:T(128)S(1)} collective-permute-done((s32[8]{0:T(128)S(1)}, s32[8]{0:T(128)S(1)}, u32[]{:S(2)}, u32[]{:S(2)}) %collective-permute-start.3) | collective-permute-done | bytes 64 | tf_op jit(solution)/shard_map/ppermute | solution.py:49
  73.2 2.2 %collective-permute-start.4 = (s32[8]{0:T(128)S(1)}, s32[8]{0:T(128)S(1)}, u32[]{:S(2)}, u32[]{:S(2)}) collective-permute-start(s32[8]{0:T(128)S(1)} %add.68), channel_id=1, source_target_pairs={{0,16},{1,17},{2,18},{3,19},{4,20},{5,21},{6,22},{7,23},{8,24},{9,... | collective-permute-start | bytes 104 | tf_op jit(solution)/shard_map/ppermute | solution.py:49
  75.4 30.1 %collective-permute-done.4 = s32[8]{0:T(128)S(1)} collective-permute-done((s32[8]{0:T(128)S(1)}, s32[8]{0:T(128)S(1)}, u32[]{:S(2)}, u32[]{:S(2)}) %collective-permute-start.4) | collective-permute-done | bytes 64 | tf_op jit(solution)/shard_map/ppermute | solution.py:49
  105.6 3.4 %fusion.40 = f32[320,352]{1,0:T(8,128)} fusion(bf16[320,2048]{1,0:T(8,128)(2,1)} %collective-permute-done.15, bf16[1,2048,352]{1,2,0:T(8,128)(2,1)} %param.11), kind=kOutput, calls=%fused_computation.82 | convolution fusion | flops 461373440 | bytes 3203072 | tf_op jit(solution)/shard_map/dot_general | solution.py:57
  109.0 3.5 %fusion.55 = f32[320,352]{1,0:T(8,128)} fusion(bf16[320,2048]{1,0:T(8,128)(2,1)} %collective-permute-done.15, bf16[2048,352]{0,1:T(8,128)(2,1)} %collective-permute-done.12), kind=kOutput, calls=%fused_computation.95 | convolution fusion | flops 461373440 | bytes 3203072 | tf_op jit(solution)/shard_map/dot_general | solution.py:57
  112.4 5.5 %fusion.5 = f32[320,2048]{1,0:T(8,128)} fusion(f32[320,352]{1,0:T(8,128)} %fusion.40, bf16[1,2048,352]{1,2,0:T(8,128)(2,1)} %param.13, bf16[320,2048]{1,0:T(8,128)(2,1)} %collective-permute-done.15, bf16[1,2048,352]{1,2,0:T(8,128)(2,1)} %param.12), kind=kOutput, calls=%fused_computation.14 | convolution fusion | flops 923422720 | bytes 7266304 | tf_op jit(solution)/shard_map/dot_general | solution.py:65
  117.9 5.0 %fusion.2 = bf16[320,2048]{1,0:T(8,128)(2,1)} fusion(f32[320,2048]{1,0:T(8,128)} %fusion.5, bf16[2048,352]{0,1:T(8,128)(2,1)S(1)} %collective-permute-done.14, f32[320,352]{1,0:T(8,128)} %fusion.55, bf16[320,2048]{1,0:T(8,128)(2,1)} %collective-permute-done.15, bf16[2048,352]{0,1:T(8,128)(2,1)S(1)} %collective-permute-done.13), kind=kOutput, calls=%fused_computation.5 | convolution fusion | flops 924733440 | bytes 8577024 | tf_op jit(solution)/shard_map/dot_general | solution.py:65
  122.9 1.5 collective-permute-start.16
  124.4 3.4 %fusion.42 = f32[320,352]{1,0:T(8,128)} fusion(bf16[320,2048]{1,0:T(8,128)(2,1)} %constant_dynamic-update-slice_fusion, bf16[1,2048,352]{1,2,0:T(8,128)(2,1)} %param.11), kind=kOutput, calls=%fused_computation.84 | convolution fusion | flops 461373440 | bytes 3203072 | tf_op jit(solution)/shard_map/dot_general | solution.py:57
  127.8 5.5 %fusion.4 = f32[320,2048]{1,0:T(8,128)} fusion(f32[320,352]{1,0:T(8,128)} %fusion.42, bf16[1,2048,352]{1,2,0:T(8,128)(2,1)} %param.13, bf16[320,2048]{1,0:T(8,128)(2,1)} %constant_dynamic-update-slice_fusion, bf16[1,2048,352]{1,2,0:T(8,128)(2,1)} %param.12), kind=kOutput, calls=%fused_computation.13 | convolution fusion | flops 923422720 | bytes 7266304 | tf_op jit(solution)/shard_map/dot_general | solution.py:65
  133.3 3.4 %fusion.54 = f32[320,352]{1,0:T(8,128)} fusion(bf16[320,2048]{1,0:T(8,128)(2,1)} %constant_dynamic-update-slice_fusion, bf16[2048,352]{0,1:T(8,128)(2,1)} %collective-permute-done.12), kind=kOutput, calls=%fused_computation.94 | convolution fusion | flops 461373440 | bytes 3203072 | tf_op jit(solution)/shard_map/dot_general | solution.py:57
  136.7 4.2 %collective-permute-done.16 = bf16[320,2048]{1,0:T(8,128)(2,1)} collective-permute-done((bf16[320,2048]{1,0:T(8,128)(2,1)}, bf16[320,2048]{1,0:T(8,128)(2,1)}, u32[]{:S(2)}, u32[]{:S(2)}) %collective-permute-start.16) | collective-permute-done | bytes 1310752 | tf_op jit(solution)/shard_map/ppermute | solution.py:22
  140.9 5.4 %fusion.1 = bf16[320,2048]{1,0:T(8,128)(2,1)} fusion(f32[320,2048]{1,0:T(8,128)} %fusion.4, bf16[2048,352]{0,1:T(8,128)(2,1)S(1)} %collective-permute-done.14, bf16[320,2048]{1,0:T(8,128)(2,1)} %collective-permute-done.16, f32[320,352]{1,0:T(8,128)} %fusion.54, bf16[320,2048]{1,0:T(8,128)(2,1)} %constant_dynamic-update-slice_fusion, ...), kind=kOutput, calls=%fused_computation.4 | convolution fusion | flops 926044160 | bytes 9887744 | tf_op jit(solution)/shard_map/dot_general | solution.py:65
  146.2 1.5 fusion.48
  147.7 1.8 collective-permute-start.17
  149.7 3.4 %collective-permute-start.22 = (bf16[40,2048]{1,0:T(8,128)(2,1)S(1)}, bf16[40,2048]{1,0:T(8,128)(2,1)S(1)}, u32[]{:S(2)}, u32[]{:S(2)}) collective-permute-start(bf16[40,2048]{1,0:T(8,128)(2,1)S(1)} %get-tuple-element.6), channel_id=1, source_target_pairs={{0,6},{1,7},{2,4},{3,5},{4,2},{5,3},{6,0},{7,1},{8,14},{9,15},{10,... | collective-permute-start | bytes 491528 | tf_op jit(solution)/shard_map/ppermute | solution.py:37
  153.1 2.7 %collective-permute-start.20 = (bf16[40,2048]{1,0:T(8,128)(2,1)S(1)}, bf16[40,2048]{1,0:T(8,128)(2,1)S(1)}, u32[]{:S(2)}, u32[]{:S(2)}) collective-permute-start(bf16[40,2048]{1,0:T(8,128)(2,1)S(1)} %get-tuple-element.8), channel_id=1, source_target_pairs={{0,4},{1,5},{2,6},{3,7},{4,0},{5,1},{6,2},{7,3},{8,12},{9,13},{10,... | collective-permute-start | bytes 491528 | tf_op jit(solution)/shard_map/ppermute | solution.py:37
  155.9 11.9 %collective-permute-done.18 = bf16[40,2048]{1,0:T(8,128)(2,1)S(1)} collective-permute-done((bf16[40,2048]{1,0:T(8,128)(2,1)S(1)}, bf16[40,2048]{1,0:T(8,128)(2,1)S(1)}, u32[]{:S(2)}, u32[]{:S(2)}) %collective-permute-start.18) | collective-permute-done | bytes 163872 | tf_op jit(solution)/shard_map/ppermute | solution.py:37
  167.8 1.7 collective-permute-start.19
  169.5 10.8 %collective-permute-done.19 = bf16[40,2048]{1,0:T(8,128)(2,1)S(1)} collective-permute-done((bf16[40,2048]{1,0:T(8,128)(2,1)S(1)}, bf16[40,2048]{1,0:T(8,128)(2,1)S(1)}, u32[]{:S(2)}, u32[]{:S(2)}) %collective-permute-start.19) | collective-permute-done | bytes 163872 | tf_op jit(solution)/shard_map/ppermute | solution.py:37
  180.4 0.5 fusion.56
  180.9 1.3 fusion.3
  (54 shorter events, 1.0 us)
Async XLA Ops:
  0.0 1.1 copy-start
  2.4 42.4 %copy-start.1 = (s32[128,2]{0,1:T(2,128)S(1)}, s32[128,2]{0,1:T(2,128)}, u32[]{:S(2)}) copy-start(s32[128,2]{0,1:T(2,128)} %param.8) | copy-start | bytes 3076
  2.4 103.1 %copy-start.3 = (s32[8]{0:T(128)S(1)}, s32[8]{0:T(128)}, u32[]{:S(2)}) copy-start(s32[8]{0:T(128)} %param.10) | copy-start | bytes 100
  2.4 7.8 %collective-permute-start.5 = (bf16[40,2048]{1,0:T(8,128)(2,1)S(1)}, bf16[40,2048]{1,0:T(8,128)(2,1)S(1)}, u32[]{:S(2)}, u32[]{:S(2)}) collective-permute-start(bf16[40,2048]{1,0:T(8,128)(2,1)S(1)} %get-tuple-element.19), channel_id=1, source_target_pairs={{0,1},{1,0},{2,3},{3,2},{4,5},{5,4},{6,7},{7,6},{8,9},{9,8},{10,11... | collective-permute-start | bytes 491528 | tf_op jit(solution)/shard_map/ppermute | solution.py:37
  2.9 38.2 %collective-permute-start.11 = (bf16[40,2048]{1,0:T(8,128)(2,1)S(1)}, bf16[40,2048]{1,0:T(8,128)(2,1)S(1)}, u32[]{:S(2)}, u32[]{:S(2)}) collective-permute-start(bf16[40,2048]{1,0:T(8,128)(2,1)S(1)} %get-tuple-element.13), channel_id=1, source_target_pairs={{0,7},{1,6},{2,5},{3,4},{4,3},{5,2},{6,1},{7,0},{8,15},{9,14},{10,... | collective-permute-start | bytes 491528 | tf_op jit(solution)/shard_map/ppermute | solution.py:37
  7.6 32.9 %collective-permute-start.10 = (bf16[40,2048]{1,0:T(8,128)(2,1)S(1)}, bf16[40,2048]{1,0:T(8,128)(2,1)S(1)}, u32[]{:S(2)}, u32[]{:S(2)}) collective-permute-start(bf16[40,2048]{1,0:T(8,128)(2,1)S(1)} %get-tuple-element.14), channel_id=1, source_target_pairs={{0,6},{1,7},{2,4},{3,5},{4,2},{5,3},{6,0},{7,1},{8,14},{9,15},{10,... | collective-permute-start | bytes 491528 | tf_op jit(solution)/shard_map/ppermute | solution.py:37
  7.6 32.2 %collective-permute-start.9 = (bf16[40,2048]{1,0:T(8,128)(2,1)S(1)}, bf16[40,2048]{1,0:T(8,128)(2,1)S(1)}, u32[]{:S(2)}, u32[]{:S(2)}) collective-permute-start(bf16[40,2048]{1,0:T(8,128)(2,1)S(1)} %get-tuple-element.15), channel_id=1, source_target_pairs={{0,5},{1,4},{2,7},{3,6},{4,1},{5,0},{6,3},{7,2},{8,13},{9,12},{10,... | collective-permute-start | bytes 491528 | tf_op jit(solution)/shard_map/ppermute | solution.py:37
  8.0 31.2 %collective-permute-start.8 = (bf16[40,2048]{1,0:T(8,128)(2,1)S(1)}, bf16[40,2048]{1,0:T(8,128)(2,1)S(1)}, u32[]{:S(2)}, u32[]{:S(2)}) collective-permute-start(bf16[40,2048]{1,0:T(8,128)(2,1)S(1)} %get-tuple-element.16), channel_id=1, source_target_pairs={{0,4},{1,5},{2,6},{3,7},{4,0},{5,1},{6,2},{7,3},{8,12},{9,13},{10,... | collective-permute-start | bytes 491528 | tf_op jit(solution)/shard_map/ppermute | solution.py:37
  10.3 15.4 %collective-permute-start.6 = (bf16[40,2048]{1,0:T(8,128)(2,1)S(1)}, bf16[40,2048]{1,0:T(8,128)(2,1)S(1)}, u32[]{:S(2)}, u32[]{:S(2)}) collective-permute-start(bf16[40,2048]{1,0:T(8,128)(2,1)S(1)} %get-tuple-element.18), channel_id=1, source_target_pairs={{0,2},{1,3},{2,0},{3,1},{4,6},{5,7},{6,4},{7,5},{8,10},{9,11},{10,... | collective-permute-start | bytes 491528 | tf_op jit(solution)/shard_map/ppermute | solution.py:37
  25.7 12.8 %collective-permute-start.7 = (bf16[40,2048]{1,0:T(8,128)(2,1)S(1)}, bf16[40,2048]{1,0:T(8,128)(2,1)S(1)}, u32[]{:S(2)}, u32[]{:S(2)}) collective-permute-start(bf16[40,2048]{1,0:T(8,128)(2,1)S(1)} %get-tuple-element.17), channel_id=1, source_target_pairs={{0,3},{1,2},{2,1},{3,0},{4,7},{5,6},{6,5},{7,4},{8,11},{9,10},{10,... | collective-permute-start | bytes 491528 | tf_op jit(solution)/shard_map/ppermute | solution.py:37
  41.9 63.7 %collective-permute-start.15 = (bf16[320,2048]{1,0:T(8,128)(2,1)}, bf16[320,2048]{1,0:T(8,128)(2,1)}, u32[]{:S(2)}, u32[]{:S(2)}) collective-permute-start(bf16[320,2048]{1,0:T(8,128)(2,1)} %constant_dynamic-update-slice_fusion), channel_id=1, source_target_pairs={{0,8},{1,17},{2,10},{3,19},{4,12},{5,21},{6,14},{7,23},{8,0},{9,25... | collective-permute-start | bytes 3932168 | tf_op jit(solution)/shard_map/ppermute | solution.py:22
  43.3 65.6 %collective-permute-start.12 = (bf16[2048,352]{0,1:T(8,128)(2,1)}, bf16[2048,352]{0,1:T(8,128)(2,1)}, u32[]{:S(2)}, u32[]{:S(2)}) collective-permute-start(bf16[2048,352]{0,1:T(8,128)(2,1)} %bitcast.4), channel_id=1, source_target_pairs={{0,16},{1,9},{2,18},{3,11},{4,20},{5,13},{6,22},{7,15},{8,24},{9,1... | collective-permute-start | bytes 4325384 | tf_op jit(solution)/shard_map/ppermute | solution.py:22
  45.0 2.2 %collective-permute-start = (s32[8]{0:T(128)S(1)}, s32[8]{0:T(128)S(1)}, u32[]{:S(2)}, u32[]{:S(2)}) collective-permute-start(s32[8]{0:T(128)S(1)} %convert_reduce_fusion), channel_id=1, source_target_pairs={{0,1},{1,0},{2,3},{3,2},{4,5},{5,4},{6,7},{7,6},{8,9},{9,8},{10,11... | collective-permute-start | bytes 104 | tf_op jit(solution)/shard_map/ppermute | solution.py:49
  45.1 72.9 %collective-permute-start.14 = (bf16[2048,352]{0,1:T(8,128)(2,1)}, bf16[2048,352]{0,1:T(8,128)(2,1)S(1)}, u32[]{:S(2)}, u32[]{:S(2)}) collective-permute-start(bf16[2048,352]{0,1:T(8,128)(2,1)} %bitcast.6), channel_id=1, source_target_pairs={{0,16},{1,9},{2,18},{3,11},{4,20},{5,13},{6,22},{7,15},{8,24},{9,1... | collective-permute-start | bytes 4325384 | tf_op jit(solution)/shard_map/ppermute | solution.py:22
  45.6 72.3 %collective-permute-start.13 = (bf16[2048,352]{0,1:T(8,128)(2,1)}, bf16[2048,352]{0,1:T(8,128)(2,1)S(1)}, u32[]{:S(2)}, u32[]{:S(2)}) collective-permute-start(bf16[2048,352]{0,1:T(8,128)(2,1)} %bitcast.5), channel_id=1, source_target_pairs={{0,16},{1,9},{2,18},{3,11},{4,20},{5,13},{6,22},{7,15},{8,24},{9,1... | collective-permute-start | bytes 4325384 | tf_op jit(solution)/shard_map/ppermute | solution.py:22
  47.2 3.6 %collective-permute-start.1 = (s32[8]{0:T(128)S(1)}, s32[8]{0:T(128)S(1)}, u32[]{:S(2)}, u32[]{:S(2)}) collective-permute-start(s32[8]{0:T(128)S(1)} %add.62), channel_id=1, source_target_pairs={{0,2},{1,3},{2,0},{3,1},{4,6},{5,7},{6,4},{7,5},{8,10},{9,11},{10,... | collective-permute-start | bytes 104 | tf_op jit(solution)/shard_map/ppermute | solution.py:49
  50.8 4.5 %collective-permute-start.2 = (s32[8]{0:T(128)S(1)}, s32[8]{0:T(128)S(1)}, u32[]{:S(2)}, u32[]{:S(2)}) collective-permute-start(s32[8]{0:T(128)S(1)} %add.64), channel_id=1, source_target_pairs={{0,4},{1,5},{2,6},{3,7},{4,0},{5,1},{6,2},{7,3},{8,12},{9,13},{10,... | collective-permute-start | bytes 104 | tf_op jit(solution)/shard_map/ppermute | solution.py:49
  55.3 17.9 %collective-permute-start.3 = (s32[8]{0:T(128)S(1)}, s32[8]{0:T(128)S(1)}, u32[]{:S(2)}, u32[]{:S(2)}) collective-permute-start(s32[8]{0:T(128)S(1)} %add.66), channel_id=1, source_target_pairs={{0,8},{1,9},{2,10},{3,11},{4,12},{5,13},{6,14},{7,15},{8,0},{9,1},... | collective-permute-start | bytes 104 | tf_op jit(solution)/shard_map/ppermute | solution.py:49
  73.2 32.3 %collective-permute-start.4 = (s32[8]{0:T(128)S(1)}, s32[8]{0:T(128)S(1)}, u32[]{:S(2)}, u32[]{:S(2)}) collective-permute-start(s32[8]{0:T(128)S(1)} %add.68), channel_id=1, source_target_pairs={{0,16},{1,17},{2,18},{3,19},{4,20},{5,21},{6,22},{7,23},{8,24},{9,... | collective-permute-start | bytes 104 | tf_op jit(solution)/shard_map/ppermute | solution.py:49
  117.9 6.5 %copy-start.2 = (s32[128,2]{0,1:T(2,128)S(1)}, s32[128,2]{0,1:T(2,128)}, u32[]{:S(2)}) copy-start(s32[128,2]{0,1:T(2,128)} %param.9) | copy-start | bytes 3076
  122.9 17.9 %collective-permute-start.16 = (bf16[320,2048]{1,0:T(8,128)(2,1)}, bf16[320,2048]{1,0:T(8,128)(2,1)}, u32[]{:S(2)}, u32[]{:S(2)}) collective-permute-start(bf16[320,2048]{1,0:T(8,128)(2,1)} %fusion.2), channel_id=1, source_target_pairs={{0,8},{1,17},{2,10},{3,19},{4,12},{5,21},{6,14},{7,23},{8,0},{9,25... | collective-permute-start | bytes 3932168 | tf_op jit(solution)/shard_map/ppermute | solution.py:22
  147.7 8.2 %collective-permute-start.17 = (bf16[40,2048]{1,0:T(8,128)(2,1)S(1)}, bf16[40,2048]{1,0:T(8,128)(2,1)S(1)}, u32[]{:S(2)}, u32[]{:S(2)}) collective-permute-start(bf16[40,2048]{1,0:T(8,128)(2,1)S(1)} %get-tuple-element.11), channel_id=1, source_target_pairs={{0,1},{1,0},{2,3},{3,2},{4,5},{5,4},{6,7},{7,6},{8,9},{9,8},{10,11... | collective-permute-start | bytes 491528 | tf_op jit(solution)/shard_map/ppermute | solution.py:37
  149.6 30.8 %collective-permute-start.23 = (bf16[40,2048]{1,0:T(8,128)(2,1)S(1)}, bf16[40,2048]{1,0:T(8,128)(2,1)S(1)}, u32[]{:S(2)}, u32[]{:S(2)}) collective-permute-start(bf16[40,2048]{1,0:T(8,128)(2,1)S(1)} %get-tuple-element.5), channel_id=1, source_target_pairs={{0,7},{1,6},{2,5},{3,4},{4,3},{5,2},{6,1},{7,0},{8,15},{9,14},{10,... | collective-permute-start | bytes 491528 | tf_op jit(solution)/shard_map/ppermute | solution.py:37
  149.7 30.6 %collective-permute-start.22 = (bf16[40,2048]{1,0:T(8,128)(2,1)S(1)}, bf16[40,2048]{1,0:T(8,128)(2,1)S(1)}, u32[]{:S(2)}, u32[]{:S(2)}) collective-permute-start(bf16[40,2048]{1,0:T(8,128)(2,1)S(1)} %get-tuple-element.6), channel_id=1, source_target_pairs={{0,6},{1,7},{2,4},{3,5},{4,2},{5,3},{6,0},{7,1},{8,14},{9,15},{10,... | collective-permute-start | bytes 491528 | tf_op jit(solution)/shard_map/ppermute | solution.py:37
  153.1 27.2 %collective-permute-start.21 = (bf16[40,2048]{1,0:T(8,128)(2,1)S(1)}, bf16[40,2048]{1,0:T(8,128)(2,1)S(1)}, u32[]{:S(2)}, u32[]{:S(2)}) collective-permute-start(bf16[40,2048]{1,0:T(8,128)(2,1)S(1)} %get-tuple-element.7), channel_id=1, source_target_pairs={{0,5},{1,4},{2,7},{3,6},{4,1},{5,0},{6,3},{7,2},{8,13},{9,12},{10,... | collective-permute-start | bytes 491528 | tf_op jit(solution)/shard_map/ppermute | solution.py:37
  153.1 27.1 %collective-permute-start.20 = (bf16[40,2048]{1,0:T(8,128)(2,1)S(1)}, bf16[40,2048]{1,0:T(8,128)(2,1)S(1)}, u32[]{:S(2)}, u32[]{:S(2)}) collective-permute-start(bf16[40,2048]{1,0:T(8,128)(2,1)S(1)} %get-tuple-element.8), channel_id=1, source_target_pairs={{0,4},{1,5},{2,6},{3,7},{4,0},{5,1},{6,2},{7,3},{8,12},{9,13},{10,... | collective-permute-start | bytes 491528 | tf_op jit(solution)/shard_map/ppermute | solution.py:37
  155.9 11.9 %collective-permute-start.18 = (bf16[40,2048]{1,0:T(8,128)(2,1)S(1)}, bf16[40,2048]{1,0:T(8,128)(2,1)S(1)}, u32[]{:S(2)}, u32[]{:S(2)}) collective-permute-start(bf16[40,2048]{1,0:T(8,128)(2,1)S(1)} %get-tuple-element.10), channel_id=1, source_target_pairs={{0,2},{1,3},{2,0},{3,1},{4,6},{5,7},{6,4},{7,5},{8,10},{9,11},{10,... | collective-permute-start | bytes 491528 | tf_op jit(solution)/shard_map/ppermute | solution.py:37
  167.8 12.5 %collective-permute-start.19 = (bf16[40,2048]{1,0:T(8,128)(2,1)S(1)}, bf16[40,2048]{1,0:T(8,128)(2,1)S(1)}, u32[]{:S(2)}, u32[]{:S(2)}) collective-permute-start(bf16[40,2048]{1,0:T(8,128)(2,1)S(1)} %get-tuple-element.9), channel_id=1, source_target_pairs={{0,3},{1,2},{2,1},{3,0},{4,7},{5,6},{6,5},{7,4},{8,11},{9,10},{10,... | collective-permute-start | bytes 491528 | tf_op jit(solution)/shard_map/ppermute | solution.py:37

commit v2 on v1

--- a/solution.py
+++ b/solution.py
@@ -1,15 +1,24 @@
 import jax
 import jax.numpy as jnp
 from jax import lax
+from jax.experimental import pallas as pl
+from jax.experimental.pallas import tpu as pltpu
 from jax.sharding import PartitionSpec as P
 
 BF16 = jnp.bfloat16
 F32 = jnp.float32
 AXES = ("dp", "expert")
-
-
-def far_first(n):
-    return sorted(range(1, n), key=lambda k: (-(k // 2), k))
+VMEM_LIMIT = 8 << 20
+BOTH_LAST = (((1,), (1,)), ((), ()))
+BOTH_FIRST = (((0,), (0,)), ((), ()))
+
+
+def few(n):
+    return n - 1 <= 16
+
+
+def near_far(n):
+    return list(range(n // 2)), list(range(n // 2, n))
 
 
 def pair_permute(values, n_dp, n_exp, weights_side):
@@ -22,10 +31,6 @@
     return lax.ppermute(values, AXES, pairs)
 
 
-def few(n):
-    return n - 1 <= 16
-
-
 def expert_exchange(blocks):
     n = lax.axis_size("expert")
     if not few(n):
@@ -33,7 +38,7 @@
         there = lax.all_to_all(jnp.stack(blocks)[place], "expert", 0, 0, tiled=True)[place]
         return [there[k] for k in range(n)]
     out = [blocks[0]] + [None] * (n - 1)
-    for k in far_first(n):
+    for k in range(1, n):
         out[k] = lax.ppermute(blocks[k], "expert", [(i, i ^ k) for i in range(n)])
     return out
 
@@ -57,12 +62,70 @@
     return jnp.dot(a, b, preferred_element_type=F32)
 
 
-def hidden_of(rows, gate_w, up_w):
-    return (jax.nn.silu(dot(rows, gate_w)) * dot(rows, up_w)).astype(BF16)
-
-
-def down(hidden, w):
-    return lax.dot_general(hidden, w, (((1,), (1,)), ((), ())), preferred_element_type=F32)
+def kernel_call(body, shapes, operands, flops):
+    spec = pl.BlockSpec(memory_space=pltpu.VMEM)
+    single = not isinstance(shapes, (list, tuple))
+    moved = sum(x.size * x.dtype.itemsize for x in operands)
+    return pl.pallas_call(
+        body,
+        out_shape=shapes if single else tuple(shapes),
+        in_specs=[spec] * len(operands),
+        out_specs=spec if single else tuple([spec] * len(shapes)),
+        compiler_params=pltpu.CompilerParams(vmem_limit_bytes=VMEM_LIMIT),
+        cost_estimate=pl.CostEstimate(flops=flops, bytes_accessed=moved, transcendentals=0),
+    )(*operands)
+
+
+def join(blocks):
+    if len(blocks) > 16:
+        return jnp.concatenate(blocks, axis=0)
+    rows, width = blocks[0].shape
+
+    def body(*refs):
+        for i, ref in enumerate(refs[:-1]):
+            refs[-1][i * rows : (i + 1) * rows, :] = ref[...]
+
+    shape = jax.ShapeDtypeStruct((rows * len(blocks), width), blocks[0].dtype)
+    return kernel_call(body, shape, blocks, 0)
+
+
+def hidden_of(rows, gate_t, up_t):
+    def body(rows_ref, gate_ref, up_ref, out_ref):
+        gate = lax.dot_general(rows_ref[...], gate_ref[...], BOTH_LAST, preferred_element_type=F32)
+        up = lax.dot_general(rows_ref[...], up_ref[...], BOTH_LAST, preferred_element_type=F32)
+        out_ref[...] = (gate / (1.0 + jnp.exp(-gate)) * up).astype(BF16)
+
+    units = gate_t.shape[0]
+    shape = jax.ShapeDtypeStruct((rows.shape[0], units), BF16)
+    return kernel_call(body, shape, (rows, gate_t, up_t), 4 * rows.size * units)
+
+
+def down(hidden, down_t, hidden2, down2_t, dtype):
+    width = down_t.shape[1]
+    step = min(width, 512)
+
+    def body(h_ref, w_ref, h2_ref, w2_ref, out_ref):
+        for at in range(0, width, step):
+            part = dot(h_ref[...], w_ref[:, at : at + step]) + dot(h2_ref[...], w2_ref[:, at : at + step])
+            out_ref[:, at : at + step] = part.astype(out_ref.dtype)
+
+    shape = jax.ShapeDtypeStruct((hidden.shape[0], width), dtype)
+    return kernel_call(body, shape, (hidden, down_t, hidden2, down2_t), 4 * hidden.size * width)
+
+
+def add_and_split(own, returned, count):
+    rows, width = own.shape[0] // count, own.shape[1]
+    if count > 16:
+        total = (own + returned.astype(F32)).astype(BF16).reshape(count, rows, width)
+        return [total[k] for k in range(count)]
+
+    def body(own_ref, returned_ref, *out_refs):
+        for k, ref in enumerate(out_refs):
+            part = slice(k * rows, (k + 1) * rows)
+            ref[...] = (own_ref[part, :] + returned_ref[part, :].astype(F32)).astype(BF16)
+
+    shapes = [jax.ShapeDtypeStruct((rows, width), BF16)] * count
+    return list(kernel_call(body, shapes, (own, returned), own.size))
 
 
 def layer(tokens, expert_ids, gate_units, capacity, w_gate, w_up, w_down):
@@ -71,7 +134,8 @@
     n_experts = capacity.shape[0]
     most = max(2, 5 * tok_rows // (2 * n_experts))
     me = lax.axis_index("expert")
-    wg, wu, wd = w_gate[0], w_up[0], w_down[0]
+    near, far = near_far(n_experts)
+    wg, wu, wd = w_gate[0].T, w_up[0].T, w_down[0].T
     wg2 = pair_permute(wg, n_dp, n_exp, True)
     wu2 = pair_permute(wu, n_dp, n_exp, True)
     wd2 = pair_permute(wd, n_dp, n_exp, True)
@@ -88,32 +152,64 @@
     chosen = chosen.reshape(n_experts * most, tok_rows)
     outgoing = dot(chosen.astype(BF16), tokens).astype(BF16).reshape(n_experts, most, width)
 
-    arrived = jnp.concatenate(expert_exchange([outgoing[k] for k in range(n_experts)]), axis=0)
-    theirs = pair_permute(arrived, n_dp, n_exp, False)
-
-    part_theirs = down(hidden_of(theirs, wg, wu), wd) + down(hidden_of(theirs, wg2, wu2), wd2)
-    returned = pair_permute(part_theirs.astype(BF16), n_dp, n_exp, False)
-    part_own = down(hidden_of(arrived, wg, wu), wd) + down(hidden_of(arrived, wg2, wu2), wd2)
-    answer = (part_own + returned.astype(F32)).astype(BF16).reshape(n_experts, most, width)
-    back = jnp.concatenate(expert_exchange([answer[k] for k in range(n_experts)]), axis=0)
+    arrived = expert_exchange([outgoing[k] for k in range(n_experts)])
+    own_near = join([arrived[k] for k in near])
+    theirs_near = pair_permute(own_near, n_dp, n_exp, False)
+    own_far = join([arrived[k] for k in far])
+    theirs_far = pair_permute(own_far, n_dp, n_exp, False)
+
+    def hidden_pair(rows):
+        return hidden_of(rows, wg, wu), hidden_of(rows, wg2, wu2)
+
+    def partial(pair, dtype):
+        return down(pair[0], wd, pair[1], wd2, dtype)
+
+    h_own_near = hidden_pair(own_near)
+    h_own_far = hidden_pair(own_far)
+    h_near = hidden_pair(theirs_near)
+    h_far = hidden_pair(theirs_far)
+    back_far = pair_permute(partial(h_far, BF16), n_dp, n_exp, False)
+    back_near = pair_permute(partial(h_near, BF16), n_dp, n_exp, False)
+    own_far_part = partial(h_own_far, F32)
+    own_near_part = partial(h_own_near, F32)
+    answer_far = add_and_split(own_far_part, back_far, len(far))
+    answer_near = add_and_split(own_near_part, back_near, len(near))
+    back = expert_exchange(answer_near + answer_far)
 
     counts = jnp.sum((expert_ids[:, :, None] == places).astype(jnp.int32), axis=(0, 1))
-    counts, _ = lax.optimization_barrier((counts, arrived[0, 0]))
-    room = capacity - earlier_counts(counts, answer[0, 0, 0])
+    counts, _ = lax.optimization_barrier((counts, own_far[0, 0]))
+    room = capacity - earlier_counts(counts, answer_far[0][0, 0])
     room_of = jnp.sum(jnp.where(expert_ids[:, :, None] == places, room, 0), axis=2)
     rank_of = jnp.sum(jnp.where(named, rank[:, None, :], 0), axis=2)
     units = jnp.where(rank_of < room_of, gate_units, 0)
     unit_at = jnp.sum(jnp.where(named, units[:, :, None], 0), axis=1)
     high = (unit_at // 8 * 8).astype(F32) / 1024.0
     low = (unit_at % 8).astype(F32) / 1024.0
-
     picks = chosen.reshape(n_experts, most, tok_rows)
     high_at = jnp.where(picks, high.T[:, None, :], 0.0).astype(BF16).reshape(n_experts * most, tok_rows)
     low_at = jnp.where(picks, low.T[:, None, :], 0.0).astype(BF16).reshape(n_experts * most, tok_rows)
-    across = (((0,), (0,)), ((), ()))
-    mixed = lax.dot_general(high_at, back, across, preferred_element_type=F32)
-    mixed = mixed + lax.dot_general(low_at, back, across, preferred_element_type=F32)
-    return mixed.astype(BF16)
+
+    def mix(high_ref, low_ref, *refs):
+        joined, out_ref = refs[-1], refs[-2]
+        for k, ref in enumerate(refs[:-2]):
+            joined[k * most : (k + 1) * most, :] = ref[...]
+        mixed = lax.dot_general(high_ref[...], joined[...], BOTH_FIRST, preferred_element_type=F32)
+        mixed += lax.dot_general(low_ref[...], joined[...], BOTH_FIRST, preferred_element_type=F32)
+        out_ref[...] = mixed.astype(BF16)
+
+    if not few(n_experts):
+        back = [jnp.concatenate(back, axis=0)]
+        most = most * n_experts
+    spec = pl.BlockSpec(memory_space=pltpu.VMEM)
+    return pl.pallas_call(
+        mix,
+        out_shape=jax.ShapeDtypeStruct((tok_rows, width), BF16),
+        in_specs=[spec] * (2 + len(back)),
+        out_specs=spec,
+        scratch_shapes=[pltpu.VMEM((len(back) * most, width), BF16)],
+        compiler_params=pltpu.CompilerParams(vmem_limit_bytes=VMEM_LIMIT),
+        name="mix",
+    )(high_at, low_at, *back)
 
 
 def solution(mesh):

time: 183 us -> 117 us (0.64)
  waiting for transfers between devices: 106 us -> 49 us
  matrix products: 37.3 us -> 0.63 us
  Pallas kernels: 0 us -> 33.5 us
  local copies, waits for them, and re-layouts: 7.18 us -> 0.28 us
  starting transfers between devices: 30.3 us -> 32.2 us
    ppermute x5, waiting for transfers between devices: 55.5 us -> 11.8 us  [earlier_counts(): other = lax.ppermute(total, AXES, [(i, i ^ step) for i in range(n)])]
    pallas_call x0 -> x17, Pallas kernels: none -> 33.5 us  [the longest x16 31.9 us: kernel_call(): pl.pallas_call(body, out_shape=shapes if single else tuple(shapes), in_sp...]
    dot_general x6 -> x0, matrix products: 23 us -> none  [the longest x4 21.3 us: down(): lax.dot_general(hidden, w, (((1,), (1,)), ((), ())), preferred_element_ty...]
    dot_general x6 -> x2, matrix products: 14.3 us -> 0.63 us  [dot(): return jnp.dot(a, b, preferred_element_type=F32)]
    ppermute x14, waiting for transfers between devices: 46.2 us -> 37.1 us  [expert_exchange(): out[k] = lax.ppermute(blocks[k], 'expert', [(i, i ^ k) for i in range(n)])]
    ppermute x5 -> x7, waiting for transfers between devices: 4.18 us -> 0.02 us  [pair_permute(): return lax.ppermute(values, AXES, pairs)]
    unnamed x20 -> x14, local copies, waits for them, and re-layouts: 4.13 us -> 0.04 us
    ppermute x5 -> x7, starting transfers between devices: 6.59 us -> 10.1 us  [pair_permute(): return lax.ppermute(values, AXES, pairs)]
  transfers between devices with their start and end apart: 24 -> 26, of which waited for: 9 -> 14; matrix products, arithmetic and copies ran while one was open for 16% -> 2% of each run, Pallas kernels for 0% -> 27%
where the time goes in v2:
time: 117 us
  waiting for transfers between devices  49 us (42%)
  Pallas kernels  33.5 us (29%)
  starting transfers between devices  32.2 us (28%)
  other arithmetic  1.19 us (1%)
    ppermute x14, waiting for transfers between devices, expert_exchange(): out[k] = lax.ppermute(blocks[k], 'expert', [(i, i ^ k) for i in range(n)])  37.1 us
    pallas_call x16, Pallas kernels, kernel_call(): pl.pallas_call(body, out_shape=shapes if single else tuple(shapes), in_sp...  31.9 us
    ppermute x14, starting transfers between devices, expert_exchange(): out[k] = lax.ppermute(blocks[k], 'expert', [(i, i ^ k) for i in range(n)])  18 us
    ppermute x5, waiting for transfers between devices, earlier_counts(): other = lax.ppermute(total, AXES, [(i, i ^ step) for i in range(n)])  11.8 us
    ppermute x7, starting transfers between devices, pair_permute(): return lax.ppermute(values, AXES, pairs)  10.1 us
    ppermute x5, starting transfers between devices, earlier_counts(): other = lax.ppermute(total, AXES, [(i, i ^ step) for i in range(n)])  4.05 us
  transfers between devices with their start and end apart: 26, of which 14 were waited for; matrix products, arithmetic and copies ran while one was open for 2% of the time, Pallas kernels for 27%

profile of v2, /device:TPU:0, one launch (start us, length us, event | category | flops | bytes accessed | tf_op | source)
XLA Modules:
  0.0 117.0 jit_solution(12879089935821873968)
XLA Ops:
  0.0 3.0 %collective-permute-start.8 = (bf16[352,2048]{1,0:T(8,128)(2,1)}, bf16[352,2048]{1,0:T(8,128)(2,1)}, u32[]{:S(2)}, u32[]{:S(2)}) collective-permute-start(bf16[352,2048]{1,0:T(8,128)(2,1)} %bitcast.54), channel_id=1, source_target_pairs={{0,16},{1,9},{2,18},{3,11},{4,20},{5,13},{6,22},{7,15},{8,24},{9,1... | collective-permute-start | bytes 4325384 | tf_op jit(solution)/shard_map/ppermute | solution.py:31
  3.1 2.0 %collective-permute-start.10 = (bf16[352,2048]{1,0:T(8,128)(2,1)}, bf16[352,2048]{1,0:T(8,128)(2,1)}, u32[]{:S(2)}, u32[]{:S(2)}) collective-permute-start(bf16[352,2048]{1,0:T(8,128)(2,1)} %bitcast.64), channel_id=1, source_target_pairs={{0,16},{1,9},{2,18},{3,11},{4,20},{5,13},{6,22},{7,15},{8,24},{9,1... | collective-permute-start | bytes 4325384 | tf_op jit(solution)/shard_map/ppermute | solution.py:31
  5.0 0.7 broadcast_xor_fusion
  6.1 0.5 convolution_convert_fusion
  6.8 2.2 %collective-permute-start.19 = (bf16[40,2048]{1,0:T(8,128)(2,1)S(1)}, bf16[40,2048]{1,0:T(8,128)(2,1)S(1)}, u32[]{:S(2)}, u32[]{:S(2)}) collective-permute-start(bf16[40,2048]{1,0:T(8,128)(2,1)S(1)} %get-tuple-element.21), channel_id=1, source_target_pairs={{0,7},{1,6},{2,5},{3,4},{4,3},{5,2},{6,1},{7,0},{8,15},{9,14},{10,... | collective-permute-start | bytes 491528 | tf_op jit(solution)/shard_map/ppermute | solution.py:42
  9.1 1.6 %collective-permute-start = (s32[8]{0:T(128)S(1)}, s32[8]{0:T(128)S(1)}, u32[]{:S(2)}, u32[]{:S(2)}) collective-permute-start(s32[8]{0:T(128)S(1)} %convert_reduce_fusion), channel_id=1, source_target_pairs={{0,1},{1,0},{2,3},{3,2},{4,5},{5,4},{6,7},{7,6},{8,9},{9,8},{10,11... | collective-permute-start | bytes 104 | tf_op jit(solution)/shard_map/ppermute | solution.py:54
  10.7 0.8 collective-permute-done
  11.6 3.6 %collective-permute-done.1 = s32[8]{0:T(128)S(1)} collective-permute-done((s32[8]{0:T(128)S(1)}, s32[8]{0:T(128)S(1)}, u32[]{:S(2)}, u32[]{:S(2)}) %collective-permute-start.1) | collective-permute-done | bytes 64 | tf_op jit(solution)/shard_map/ppermute | solution.py:54
  15.1 0.7 collective-permute-start.18
  15.8 1.8 %collective-permute-start.17 = (bf16[40,2048]{1,0:T(8,128)(2,1)S(1)}, bf16[40,2048]{1,0:T(8,128)(2,1)S(1)}, u32[]{:S(2)}, u32[]{:S(2)}) collective-permute-start(bf16[40,2048]{1,0:T(8,128)(2,1)S(1)} %get-tuple-element.23), channel_id=1, source_target_pairs={{0,5},{1,4},{2,7},{3,6},{4,1},{5,0},{6,3},{7,2},{8,13},{9,12},{10,... | collective-permute-start | bytes 491528 | tf_op jit(solution)/shard_map/ppermute | solution.py:42
  17.6 6.3 %collective-permute-done.18.refs_2_ = bf16[40,2048]{1,0:T(8,128)(2,1)S(1)} collective-permute-done((bf16[40,2048]{1,0:T(8,128)(2,1)S(1)}, bf16[40,2048]{1,0:T(8,128)(2,1)S(1)}, u32[]{:S(2)}, u32[]{:S(2)}) %collective-permute-start.18) | collective-permute-done | bytes 163872 | tf_op jit(solution)/shard_map/ppermute | solution.py:42
  23.9 5.5 %collective-permute-start.16 = (bf16[40,2048]{1,0:T(8,128)(2,1)S(1)}, bf16[40,2048]{1,0:T(8,128)(2,1)S(1)}, u32[]{:S(2)}, u32[]{:S(2)}) collective-permute-start(bf16[40,2048]{1,0:T(8,128)(2,1)S(1)} %get-tuple-element.24), channel_id=1, source_target_pairs={{0,4},{1,5},{2,6},{3,7},{4,0},{5,1},{6,2},{7,3},{8,12},{9,13},{10,... | collective-permute-start | bytes 491528 | tf_op jit(solution)/shard_map/ppermute | solution.py:42
  29.4 3.1 %collective-permute-done.17.refs_1_ = bf16[40,2048]{1,0:T(8,128)(2,1)S(1)} collective-permute-done((bf16[40,2048]{1,0:T(8,128)(2,1)S(1)}, bf16[40,2048]{1,0:T(8,128)(2,1)S(1)}, u32[]{:S(2)}, u32[]{:S(2)}) %collective-permute-start.17) | collective-permute-done | bytes 163872 | tf_op jit(solution)/shard_map/ppermute | solution.py:42
  32.4 6.9 %collective-permute-done.16.refs_0_ = bf16[40,2048]{1,0:T(8,128)(2,1)S(1)} collective-permute-done((bf16[40,2048]{1,0:T(8,128)(2,1)S(1)}, bf16[40,2048]{1,0:T(8,128)(2,1)S(1)}, u32[]{:S(2)}, u32[]{:S(2)}) %collective-permute-start.16) | collective-permute-done | bytes 163872 | tf_op jit(solution)/shard_map/ppermute | solution.py:42
  39.4 0.9 shard_map.81.rows_ref
  40.3 3.5 %collective-permute-done.2 = s32[8]{0:T(128)S(1)} collective-permute-done((s32[8]{0:T(128)S(1)}, s32[8]{0:T(128)S(1)}, u32[]{:S(2)}, u32[]{:S(2)}) %collective-permute-start.2) | collective-permute-done | bytes 64 | tf_op jit(solution)/shard_map/ppermute | solution.py:54
  43.8 1.2 collective-permute-start.20
  45.0 5.3 %collective-permute-done.6.refs_2_ = bf16[40,2048]{1,0:T(8,128)(2,1)S(1)} collective-permute-done((bf16[40,2048]{1,0:T(8,128)(2,1)S(1)}, bf16[40,2048]{1,0:T(8,128)(2,1)S(1)}, u32[]{:S(2)}, u32[]{:S(2)}) %collective-permute-start.6) | collective-permute-done | bytes 163872 | tf_op jit(solution)/shard_map/ppermute | solution.py:42
  50.3 1.4 %collective-permute-done.5.refs_1_ = bf16[40,2048]{1,0:T(8,128)(2,1)S(1)} collective-permute-done((bf16[40,2048]{1,0:T(8,128)(2,1)S(1)}, bf16[40,2048]{1,0:T(8,128)(2,1)S(1)}, u32[]{:S(2)}, u32[]{:S(2)}) %collective-permute-start.5) | collective-permute-done | bytes 163872 | tf_op jit(solution)/shard_map/ppermute | solution.py:42
  51.7 0.9 collective-permute-start.3
  52.6 0.9 shard_map.73.rows_ref
  53.5 3.9 %collective-permute-done.3 = s32[8]{0:T(128)S(1)} collective-permute-done((s32[8]{0:T(128)S(1)}, s32[8]{0:T(128)S(1)}, u32[]{:S(2)}, u32[]{:S(2)}) %collective-permute-start.3) | collective-permute-done | bytes 64 | tf_op jit(solution)/shard_map/ppermute | solution.py:54
  57.3 1.7 %collective-permute-start.11 = (bf16[160,2048]{1,0:T(8,128)(2,1)}, bf16[160,2048]{1,0:T(8,128)(2,1)}, u32[]{:S(2)}, u32[]{:S(2)}) collective-permute-start(bf16[160,2048]{1,0:T(8,128)(2,1)} %shard_map.73.rows_ref), channel_id=1, source_target_pairs={{0,8},{1,17},{2,10},{3,19},{4,12},{5,21},{6,14},{7,23},{8,0},{9,25... | collective-permute-start | bytes 1966088 | tf_op jit(solution)/shard_map/ppermute | solution.py:31
  59.1 1.6 %collective-permute-start.4 = (s32[8]{0:T(128)S(1)}, s32[8]{0:T(128)S(1)}, u32[]{:S(2)}, u32[]{:S(2)}) collective-permute-start(s32[8]{0:T(128)S(1)} %add.43), channel_id=1, source_target_pairs={{0,16},{1,17},{2,18},{3,19},{4,20},{5,21},{6,22},{7,23},{8,24},{9,... | collective-permute-start | bytes 104 | tf_op jit(solution)/shard_map/ppermute | solution.py:54
  60.7 2.2 %shard_map.85.h_ref = bf16[160,352]{1,0:T(8,128)(2,1)S(1)} custom-call(bf16[160,2048]{1,0:T(8,128)(2,1)} %collective-permute-done.20.rows_ref, bf16[352,2048]{1,0:T(8,128)(2,1)S(1)} %bitcast.55, bf16[352,2048]{1,0:T(8,128)(2,1)S(1)} %bitcast.60), custom_call_target="tpu_custom_call" | custom-call | flops 461373440 | bytes 3538944 | tf_op jit(solution)/shard_map/pallas_call | solution.py:69
  62.9 3.2 %shard_map.86.h2_ref = bf16[160,352]{1,0:T(8,128)(2,1)S(1)} custom-call(bf16[160,2048]{1,0:T(8,128)(2,1)} %collective-permute-done.20.rows_ref, bf16[352,2048]{1,0:T(8,128)(2,1)} %collective-permute-done.8.gate_ref, bf16[352,2048]{1,0:T(8,128)(2,1)} %collective-permute-done.9.up_ref), custom_call_target="tpu_custom_call" | custom-call | flops 461373440 | bytes 3538944 | tf_op jit(solution)/shard_map/pallas_call | solution.py:69
  66.1 2.2 %shard_map.87 = bf16[160,2048]{1,0:T(8,128)(2,1)S(1)} custom-call(bf16[160,352]{1,0:T(8,128)(2,1)S(1)} %shard_map.85.h_ref, bf16[352,2048]{1,0:T(8,128)(2,1)S(1)} %bitcast.65, bf16[160,352]{1,0:T(8,128)(2,1)S(1)} %shard_map.86.h2_ref, bf16[352,2048]{1,0:T(8,128)(2,1)} %collective-permute-done.10.w2_ref), custom_call_target="tpu_custom_call" | custom-call | flops 461373440 | bytes 3108864 | tf_op jit(solution)/shard_map/pallas_call | solution.py:69
  68.4 0.6 collective-permute-start.21
  69.0 2.2 %shard_map.77.h_ref = bf16[160,352]{1,0:T(8,128)(2,1)S(1)} custom-call(bf16[160,2048]{1,0:T(8,128)(2,1)} %collective-permute-done.11.rows_ref, bf16[352,2048]{1,0:T(8,128)(2,1)S(1)} %bitcast.56, bf16[352,2048]{1,0:T(8,128)(2,1)S(1)} %bitcast.61), custom_call_target="tpu_custom_call" | custom-call | flops 461373440 | bytes 3538944 | tf_op jit(solution)/shard_map/pallas_call | solution.py:69
  71.2 3.1 %shard_map.78.h2_ref = bf16[160,352]{1,0:T(8,128)(2,1)S(1)} custom-call(bf16[160,2048]{1,0:T(8,128)(2,1)} %collective-permute-done.11.rows_ref, bf16[352,2048]{1,0:T(8,128)(2,1)} %collective-permute-done.8.gate_ref, bf16[352,2048]{1,0:T(8,128)(2,1)} %collective-permute-done.9.up_ref), custom_call_target="tpu_custom_call" | custom-call | flops 461373440 | bytes 3538944 | tf_op jit(solution)/shard_map/pallas_call | solution.py:69
  74.3 2.2 %shard_map.79 = bf16[160,2048]{1,0:T(8,128)(2,1)S(1)} custom-call(bf16[160,352]{1,0:T(8,128)(2,1)S(1)} %shard_map.77.h_ref, bf16[352,2048]{1,0:T(8,128)(2,1)S(1)} %bitcast.66, bf16[160,352]{1,0:T(8,128)(2,1)S(1)} %shard_map.78.h2_ref, bf16[352,2048]{1,0:T(8,128)(2,1)} %collective-permute-done.10.w2_ref), custom_call_target="tpu_custom_call" | custom-call | flops 461373440 | bytes 3108864 | tf_op jit(solution)/shard_map/pallas_call | solution.py:69
  76.5 1.6 %collective-permute-start.12 = (bf16[160,2048]{1,0:T(8,128)(2,1)S(1)}, bf16[160,2048]{1,0:T(8,128)(2,1)S(1)}, u32[]{:S(2)}, u32[]{:S(2)}) collective-permute-start(bf16[160,2048]{1,0:T(8,128)(2,1)S(1)} %shard_map.79), channel_id=1, source_target_pairs={{0,8},{1,17},{2,10},{3,19},{4,12},{5,21},{6,14},{7,23},{8,0},{9,25... | collective-permute-start | bytes 1966088 | tf_op jit(solution)/shard_map/ppermute | solution.py:31
  78.1 2.2 %shard_map.82.h_ref = bf16[160,352]{1,0:T(8,128)(2,1)S(1)} custom-call(bf16[160,2048]{1,0:T(8,128)(2,1)} %shard_map.81.rows_ref, bf16[352,2048]{1,0:T(8,128)(2,1)S(1)} %bitcast.57, bf16[352,2048]{1,0:T(8,128)(2,1)S(1)} %bitcast.62), custom_call_target="tpu_custom_call" | custom-call | flops 461373440 | bytes 3538944 | tf_op jit(solution)/shard_map/pallas_call | solution.py:69
  80.3 3.1 %shard_map.83.h2_ref = bf16[160,352]{1,0:T(8,128)(2,1)S(1)} custom-call(bf16[160,2048]{1,0:T(8,128)(2,1)} %shard_map.81.rows_ref, bf16[352,2048]{1,0:T(8,128)(2,1)} %collective-permute-done.8.gate_ref, bf16[352,2048]{1,0:T(8,128)(2,1)} %collective-permute-done.9.up_ref), custom_call_target="tpu_custom_call" | custom-call | flops 461373440 | bytes 3538944 | tf_op jit(solution)/shard_map/pallas_call | solution.py:69
  83.4 2.2 %shard_map.84.own_ref = f32[160,2048]{1,0:T(8,128)S(1)} custom-call(bf16[160,352]{1,0:T(8,128)(2,1)S(1)} %shard_map.82.h_ref, bf16[352,2048]{1,0:T(8,128)(2,1)S(1)} %bitcast.67, bf16[160,352]{1,0:T(8,128)(2,1)S(1)} %shard_map.83.h2_ref, bf16[352,2048]{1,0:T(8,128)(2,1)} %collective-permute-done.10.w2_ref), custom_call_target="tpu_custom_call" | custom-call | flops 461373440 | bytes 3108864 | tf_op jit(solution)/shard_map/pallas_call | solution.py:69
  85.7 2.7 %collective-permute-start.22 = (bf16[40,2048]{1,0:T(8,128)(2,1)S(1)}, bf16[40,2048]{1,0:T(8,128)(2,1)S(1)}, u32[]{:S(2)}, u32[]{:S(2)}) collective-permute-start(bf16[40,2048]{1,0:T(8,128)(2,1)S(1)} %get-tuple-element.17), channel_id=1, source_target_pairs={{0,4},{1,5},{2,6},{3,7},{4,0},{5,1},{6,2},{7,3},{8,12},{9,13},{10,... | collective-permute-start | bytes 491528 | tf_op jit(solution)/shard_map/ppermute | solution.py:42
  88.4 2.2 %shard_map.74.h_ref = bf16[160,352]{1,0:T(8,128)(2,1)S(1)} custom-call(bf16[160,2048]{1,0:T(8,128)(2,1)} %shard_map.73.rows_ref, bf16[352,2048]{1,0:T(8,128)(2,1)S(1)} %bitcast.58, bf16[352,2048]{1,0:T(8,128)(2,1)S(1)} %bitcast.63), custom_call_target="tpu_custom_call" | custom-call | flops 461373440 | bytes 3538944 | tf_op jit(solution)/shard_map/pallas_call | solution.py:69
  90.6 3.1 %shard_map.75.h2_ref = bf16[160,352]{1,0:T(8,128)(2,1)S(1)} custom-call(bf16[160,2048]{1,0:T(8,128)(2,1)} %shard_map.73.rows_ref, bf16[352,2048]{1,0:T(8,128)(2,1)} %collective-permute-done.8.gate_ref, bf16[352,2048]{1,0:T(8,128)(2,1)} %collective-permute-done.9.up_ref), custom_call_target="tpu_custom_call" | custom-call | flops 461373440 | bytes 3538944 | tf_op jit(solution)/shard_map/pallas_call | solution.py:69
  93.7 2.2 %shard_map.76.own_ref = f32[160,2048]{1,0:T(8,128)S(1)} custom-call(bf16[160,352]{1,0:T(8,128)(2,1)S(1)} %shard_map.74.h_ref, bf16[352,2048]{1,0:T(8,128)(2,1)S(1)} %bitcast.68, bf16[160,352]{1,0:T(8,128)(2,1)S(1)} %shard_map.75.h2_ref, bf16[352,2048]{1,0:T(8,128)(2,1)} %collective-permute-done.10.w2_ref), custom_call_target="tpu_custom_call" | custom-call | flops 461373440 | bytes 3108864 | tf_op jit(solution)/shard_map/pallas_call | solution.py:69
  95.9 1.4 %collective-permute-start.24 = (bf16[40,2048]{1,0:T(8,128)(2,1)S(1)}, bf16[40,2048]{1,0:T(8,128)(2,1)S(1)}, u32[]{:S(2)}, u32[]{:S(2)}) collective-permute-start(bf16[40,2048]{1,0:T(8,128)(2,1)S(1)} %get-tuple-element.19), channel_id=1, source_target_pairs={{0,6},{1,7},{2,4},{3,5},{4,2},{5,3},{6,0},{7,1},{8,14},{9,15},{10,... | collective-permute-start | bytes 491528 | tf_op jit(solution)/shard_map/ppermute | solution.py:42
  97.3 2.4 %collective-permute-start.25 = (bf16[40,2048]{1,0:T(8,128)(2,1)S(1)}, bf16[40,2048]{1,0:T(8,128)(2,1)S(1)}, u32[]{:S(2)}, u32[]{:S(2)}) collective-permute-start(bf16[40,2048]{1,0:T(8,128)(2,1)S(1)} %get-tuple-element.20), channel_id=1, source_target_pairs={{0,7},{1,6},{2,5},{3,4},{4,3},{5,2},{6,1},{7,0},{8,15},{9,14},{10,... | collective-permute-start | bytes 491528 | tf_op jit(solution)/shard_map/ppermute | solution.py:42
  100.1 0.5 collective-permute-done.23.refs_5_
  100.6 1.1 collective-permute-start.15
  101.9 3.1 %collective-permute-done.24.refs_6_ = bf16[40,2048]{1,0:T(8,128)(2,1)S(1)} collective-permute-done((bf16[40,2048]{1,0:T(8,128)(2,1)S(1)}, bf16[40,2048]{1,0:T(8,128)(2,1)S(1)}, u32[]{:S(2)}, u32[]{:S(2)}) %collective-permute-start.24) | collective-permute-done | bytes 163872 | tf_op jit(solution)/shard_map/ppermute | solution.py:42
  105.0 2.6 %collective-permute-done.25.refs_7_ = bf16[40,2048]{1,0:T(8,128)(2,1)S(1)} collective-permute-done((bf16[40,2048]{1,0:T(8,128)(2,1)S(1)}, bf16[40,2048]{1,0:T(8,128)(2,1)S(1)}, u32[]{:S(2)}, u32[]{:S(2)}) %collective-permute-start.25) | collective-permute-done | bytes 163872 | tf_op jit(solution)/shard_map/ppermute | solution.py:42
  107.6 4.7 %collective-permute-done.14.refs_2_ = bf16[40,2048]{1,0:T(8,128)(2,1)S(1)} collective-permute-done((bf16[40,2048]{1,0:T(8,128)(2,1)S(1)}, bf16[40,2048]{1,0:T(8,128)(2,1)S(1)}, u32[]{:S(2)}, u32[]{:S(2)}) %collective-permute-start.14) | collective-permute-done | bytes 163872 | tf_op jit(solution)/shard_map/ppermute | solution.py:42
  112.3 3.1 %collective-permute-done.15.refs_3_ = bf16[40,2048]{1,0:T(8,128)(2,1)S(1)} collective-permute-done((bf16[40,2048]{1,0:T(8,128)(2,1)S(1)}, bf16[40,2048]{1,0:T(8,128)(2,1)S(1)}, u32[]{:S(2)}, u32[]{:S(2)}) %collective-permute-start.15) | collective-permute-done | bytes 163872 | tf_op jit(solution)/shard_map/ppermute | solution.py:42
  115.5 1.5 %mix.1 = bf16[128,2048]{1,0:T(8,128)(2,1)} custom-call(bf16[320,128]{1,0:T(8,128)(2,1)S(1)} %get-tuple-element.30.high_ref, bf16[320,128]{1,0:T(8,128)(2,1)S(1)} %get-tuple-element.29.low_ref, bf16[40,2048]{1,0:T(8,128)(2,1)S(1)} %get-tuple-element.13.refs_0_, bf16[40,2048]{1,0:T(8,128)(2,1)S(1)} %collective-permute-done.13.refs_1_, ...), custom_call_target="tpu_custom_call" | custom-call | tf_op jit(solution)/shard_map/mix/pallas_call | solution.py:204
  (56 shorter events, 1.5 us)
Async XLA Ops:
  0.0 6.1 %copy-start = (bf16[128,2048]{1,0:T(8,128)(2,1)S(1)}, bf16[128,2048]{1,0:T(8,128)(2,1)}, u32[]{:S(2)}) copy-start(bf16[128,2048]{1,0:T(8,128)(2,1)} %param.7) | copy-start | bytes 1572868
  0.0 62.9 %collective-permute-start.8 = (bf16[352,2048]{1,0:T(8,128)(2,1)}, bf16[352,2048]{1,0:T(8,128)(2,1)}, u32[]{:S(2)}, u32[]{:S(2)}) collective-permute-start(bf16[352,2048]{1,0:T(8,128)(2,1)} %bitcast.54), channel_id=1, source_target_pairs={{0,16},{1,9},{2,18},{3,11},{4,20},{5,13},{6,22},{7,15},{8,24},{9,1... | collective-permute-start | bytes 4325384 | tf_op jit(solution)/shard_map/ppermute | solution.py:31
  3.0 59.9 %collective-permute-start.9 = (bf16[352,2048]{1,0:T(8,128)(2,1)}, bf16[352,2048]{1,0:T(8,128)(2,1)}, u32[]{:S(2)}, u32[]{:S(2)}) collective-permute-start(bf16[352,2048]{1,0:T(8,128)(2,1)} %bitcast.59), channel_id=1, source_target_pairs={{0,16},{1,9},{2,18},{3,11},{4,20},{5,13},{6,22},{7,15},{8,24},{9,1... | collective-permute-start | bytes 4325384 | tf_op jit(solution)/shard_map/ppermute | solution.py:31
  3.1 63.0 %collective-permute-start.10 = (bf16[352,2048]{1,0:T(8,128)(2,1)}, bf16[352,2048]{1,0:T(8,128)(2,1)}, u32[]{:S(2)}, u32[]{:S(2)}) collective-permute-start(bf16[352,2048]{1,0:T(8,128)(2,1)} %bitcast.64), channel_id=1, source_target_pairs={{0,16},{1,9},{2,18},{3,11},{4,20},{5,13},{6,22},{7,15},{8,24},{9,1... | collective-permute-start | bytes 4325384 | tf_op jit(solution)/shard_map/ppermute | solution.py:31
  6.6 2.4 %copy-start.4 = (s32[128,2]{0,1:T(2,128)S(1)}, s32[128,2]{0,1:T(2,128)}, u32[]{:S(2)}) copy-start(s32[128,2]{0,1:T(2,128)} %param.8) | copy-start | bytes 3076
  6.6 54.1 %copy-start.2 = (bf16[1,2048,352]{1,2,0:T(8,128)(2,1)S(1)}, bf16[1,2048,352]{1,2,0:T(8,128)(2,1)}, u32[]{:S(2)}) copy-start(bf16[1,2048,352]{1,2,0:T(8,128)(2,1)} %param.12) | copy-start | bytes 4325380
  6.8 53.9 %copy-start.1 = (bf16[1,2048,352]{1,2,0:T(8,128)(2,1)S(1)}, bf16[1,2048,352]{1,2,0:T(8,128)(2,1)}, u32[]{:S(2)}) copy-start(bf16[1,2048,352]{1,2,0:T(8,128)(2,1)} %param.11) | copy-start | bytes 4325380
  6.8 9.0 %collective-permute-start.19 = (bf16[40,2048]{1,0:T(8,128)(2,1)S(1)}, bf16[40,2048]{1,0:T(8,128)(2,1)S(1)}, u32[]{:S(2)}, u32[]{:S(2)}) collective-permute-start(bf16[40,2048]{1,0:T(8,128)(2,1)S(1)} %get-tuple-element.21), channel_id=1, source_target_pairs={{0,7},{1,6},{2,5},{3,4},{4,3},{5,2},{6,1},{7,0},{8,15},{9,14},{10,... | collective-permute-start | bytes 491528 | tf_op jit(solution)/shard_map/ppermute | solution.py:42
  9.1 2.4 %collective-permute-start = (s32[8]{0:T(128)S(1)}, s32[8]{0:T(128)S(1)}, u32[]{:S(2)}, u32[]{:S(2)}) collective-permute-start(s32[8]{0:T(128)S(1)} %convert_reduce_fusion), channel_id=1, source_target_pairs={{0,1},{1,0},{2,3},{3,2},{4,5},{5,4},{6,7},{7,6},{8,9},{9,8},{10,11... | collective-permute-start | bytes 104 | tf_op jit(solution)/shard_map/ppermute | solution.py:54
  11.6 3.6 %collective-permute-start.1 = (s32[8]{0:T(128)S(1)}, s32[8]{0:T(128)S(1)}, u32[]{:S(2)}, u32[]{:S(2)}) collective-permute-start(s32[8]{0:T(128)S(1)} %add.37), channel_id=1, source_target_pairs={{0,2},{1,3},{2,0},{3,1},{4,6},{5,7},{6,4},{7,5},{8,10},{9,11},{10,... | collective-permute-start | bytes 104 | tf_op jit(solution)/shard_map/ppermute | solution.py:54
  15.1 8.7 %collective-permute-start.18 = (bf16[40,2048]{1,0:T(8,128)(2,1)S(1)}, bf16[40,2048]{1,0:T(8,128)(2,1)S(1)}, u32[]{:S(2)}, u32[]{:S(2)}) collective-permute-start(bf16[40,2048]{1,0:T(8,128)(2,1)S(1)} %get-tuple-element.22), channel_id=1, source_target_pairs={{0,6},{1,7},{2,4},{3,5},{4,2},{5,3},{6,0},{7,1},{8,14},{9,15},{10,... | collective-permute-start | bytes 491528 | tf_op jit(solution)/shard_map/ppermute | solution.py:42
  15.8 16.7 %collective-permute-start.17 = (bf16[40,2048]{1,0:T(8,128)(2,1)S(1)}, bf16[40,2048]{1,0:T(8,128)(2,1)S(1)}, u32[]{:S(2)}, u32[]{:S(2)}) collective-permute-start(bf16[40,2048]{1,0:T(8,128)(2,1)S(1)} %get-tuple-element.23), channel_id=1, source_target_pairs={{0,5},{1,4},{2,7},{3,6},{4,1},{5,0},{6,3},{7,2},{8,13},{9,12},{10,... | collective-permute-start | bytes 491528 | tf_op jit(solution)/shard_map/ppermute | solution.py:42
  23.9 15.5 %collective-permute-start.16 = (bf16[40,2048]{1,0:T(8,128)(2,1)S(1)}, bf16[40,2048]{1,0:T(8,128)(2,1)S(1)}, u32[]{:S(2)}, u32[]{:S(2)}) collective-permute-start(bf16[40,2048]{1,0:T(8,128)(2,1)S(1)} %get-tuple-element.24), channel_id=1, source_target_pairs={{0,4},{1,5},{2,6},{3,7},{4,0},{5,1},{6,2},{7,3},{8,12},{9,13},{10,... | collective-permute-start | bytes 491528 | tf_op jit(solution)/shard_map/ppermute | solution.py:42
  32.4 12.6 %collective-permute-start.7 = (bf16[40,2048]{1,0:T(8,128)(2,1)S(1)}, bf16[40,2048]{1,0:T(8,128)(2,1)S(1)}, u32[]{:S(2)}, u32[]{:S(2)}) collective-permute-start(bf16[40,2048]{1,0:T(8,128)(2,1)S(1)} %get-tuple-element.25), channel_id=1, source_target_pairs={{0,3},{1,2},{2,1},{3,0},{4,7},{5,6},{6,5},{7,4},{8,11},{9,10},{10,... | collective-permute-start | bytes 491528 | tf_op jit(solution)/shard_map/ppermute | solution.py:42
  39.4 4.5 %collective-permute-start.2 = (s32[8]{0:T(128)S(1)}, s32[8]{0:T(128)S(1)}, u32[]{:S(2)}, u32[]{:S(2)}) collective-permute-start(s32[8]{0:T(128)S(1)} %add.39), channel_id=1, source_target_pairs={{0,4},{1,5},{2,6},{3,7},{4,0},{5,1},{6,2},{7,3},{8,12},{9,13},{10,... | collective-permute-start | bytes 104 | tf_op jit(solution)/shard_map/ppermute | solution.py:54
  43.8 15.3 %collective-permute-start.20 = (bf16[160,2048]{1,0:T(8,128)(2,1)}, bf16[160,2048]{1,0:T(8,128)(2,1)}, u32[]{:S(2)}, u32[]{:S(2)}) collective-permute-start(bf16[160,2048]{1,0:T(8,128)(2,1)} %shard_map.81.rows_ref), channel_id=1, source_target_pairs={{0,8},{1,17},{2,10},{3,19},{4,12},{5,21},{6,14},{7,23},{8,0},{9,25... | collective-permute-start | bytes 1966088 | tf_op jit(solution)/shard_map/ppermute | solution.py:31
  45.0 5.3 %collective-permute-start.6 = (bf16[40,2048]{1,0:T(8,128)(2,1)S(1)}, bf16[40,2048]{1,0:T(8,128)(2,1)S(1)}, u32[]{:S(2)}, u32[]{:S(2)}) collective-permute-start(bf16[40,2048]{1,0:T(8,128)(2,1)S(1)} %get-tuple-element.26), channel_id=1, source_target_pairs={{0,2},{1,3},{2,0},{3,1},{4,6},{5,7},{6,4},{7,5},{8,10},{9,11},{10,... | collective-permute-start | bytes 491528 | tf_op jit(solution)/shard_map/ppermute | solution.py:42
  50.3 1.4 %collective-permute-start.5 = (bf16[40,2048]{1,0:T(8,128)(2,1)S(1)}, bf16[40,2048]{1,0:T(8,128)(2,1)S(1)}, u32[]{:S(2)}, u32[]{:S(2)}) collective-permute-start(bf16[40,2048]{1,0:T(8,128)(2,1)S(1)} %get-tuple-element.27), channel_id=1, source_target_pairs={{0,1},{1,0},{2,3},{3,2},{4,5},{5,4},{6,7},{7,6},{8,9},{9,8},{10,11... | collective-permute-start | bytes 491528 | tf_op jit(solution)/shard_map/ppermute | solution.py:42
  51.7 5.6 %collective-permute-start.3 = (s32[8]{0:T(128)S(1)}, s32[8]{0:T(128)S(1)}, u32[]{:S(2)}, u32[]{:S(2)}) collective-permute-start(s32[8]{0:T(128)S(1)} %add.41), channel_id=1, source_target_pairs={{0,8},{1,9},{2,10},{3,11},{4,12},{5,13},{6,14},{7,15},{8,0},{9,1},... | collective-permute-start | bytes 104 | tf_op jit(solution)/shard_map/ppermute | solution.py:54
  57.3 11.6 %collective-permute-start.11 = (bf16[160,2048]{1,0:T(8,128)(2,1)}, bf16[160,2048]{1,0:T(8,128)(2,1)}, u32[]{:S(2)}, u32[]{:S(2)}) collective-permute-start(bf16[160,2048]{1,0:T(8,128)(2,1)} %shard_map.73.rows_ref), channel_id=1, source_target_pairs={{0,8},{1,17},{2,10},{3,19},{4,12},{5,21},{6,14},{7,23},{8,0},{9,25... | collective-permute-start | bytes 1966088 | tf_op jit(solution)/shard_map/ppermute | solution.py:31
  59.1 9.8 %collective-permute-start.4 = (s32[8]{0:T(128)S(1)}, s32[8]{0:T(128)S(1)}, u32[]{:S(2)}, u32[]{:S(2)}) collective-permute-start(s32[8]{0:T(128)S(1)} %add.43), channel_id=1, source_target_pairs={{0,16},{1,17},{2,18},{3,19},{4,20},{5,21},{6,22},{7,23},{8,24},{9,... | collective-permute-start | bytes 104 | tf_op jit(solution)/shard_map/ppermute | solution.py:54
  62.9 3.2 %copy-start.3 = (bf16[1,2048,352]{1,2,0:T(8,128)(2,1)S(1)}, bf16[1,2048,352]{1,2,0:T(8,128)(2,1)}, u32[]{:S(2)}) copy-start(bf16[1,2048,352]{1,2,0:T(8,128)(2,1)} %param.13) | copy-start | bytes 4325380
  66.1 2.9 %copy-start.6 = (s32[8]{0:T(128)S(1)}, s32[8]{0:T(128)}, u32[]{:S(2)}) copy-start(s32[8]{0:T(128)} %param.10) | copy-start | bytes 100
  68.4 17.2 %collective-permute-start.21 = (bf16[160,2048]{1,0:T(8,128)(2,1)S(1)}, bf16[160,2048]{1,0:T(8,128)(2,1)S(1)}, u32[]{:S(2)}, u32[]{:S(2)}) collective-permute-start(bf16[160,2048]{1,0:T(8,128)(2,1)S(1)} %shard_map.87), channel_id=1, source_target_pairs={{0,8},{1,17},{2,10},{3,19},{4,12},{5,21},{6,14},{7,23},{8,0},{9,25... | collective-permute-start | bytes 1966088 | tf_op jit(solution)/shard_map/ppermute | solution.py:31
  74.2 3.9 %copy-start.5 = (s32[128,2]{0,1:T(2,128)S(1)}, s32[128,2]{0,1:T(2,128)}, u32[]{:S(2)}) copy-start(s32[128,2]{0,1:T(2,128)} %param.9) | copy-start | bytes 3076
  76.5 23.2 %collective-permute-start.12 = (bf16[160,2048]{1,0:T(8,128)(2,1)S(1)}, bf16[160,2048]{1,0:T(8,128)(2,1)S(1)}, u32[]{:S(2)}, u32[]{:S(2)}) collective-permute-start(bf16[160,2048]{1,0:T(8,128)(2,1)S(1)} %shard_map.79), channel_id=1, source_target_pairs={{0,8},{1,17},{2,10},{3,19},{4,12},{5,21},{6,14},{7,23},{8,0},{9,25... | collective-permute-start | bytes 1966088 | tf_op jit(solution)/shard_map/ppermute | solution.py:31
  85.7 14.3 %collective-permute-start.22 = (bf16[40,2048]{1,0:T(8,128)(2,1)S(1)}, bf16[40,2048]{1,0:T(8,128)(2,1)S(1)}, u32[]{:S(2)}, u32[]{:S(2)}) collective-permute-start(bf16[40,2048]{1,0:T(8,128)(2,1)S(1)} %get-tuple-element.17), channel_id=1, source_target_pairs={{0,4},{1,5},{2,6},{3,7},{4,0},{5,1},{6,2},{7,3},{8,12},{9,13},{10,... | collective-permute-start | bytes 491528 | tf_op jit(solution)/shard_map/ppermute | solution.py:42
  88.4 12.2 %collective-permute-start.23 = (bf16[40,2048]{1,0:T(8,128)(2,1)S(1)}, bf16[40,2048]{1,0:T(8,128)(2,1)S(1)}, u32[]{:S(2)}, u32[]{:S(2)}) collective-permute-start(bf16[40,2048]{1,0:T(8,128)(2,1)S(1)} %get-tuple-element.18), channel_id=1, source_target_pairs={{0,5},{1,4},{2,7},{3,6},{4,1},{5,0},{6,3},{7,2},{8,13},{9,12},{10,... | collective-permute-start | bytes 491528 | tf_op jit(solution)/shard_map/ppermute | solution.py:42
  95.9 9.1 %collective-permute-start.24 = (bf16[40,2048]{1,0:T(8,128)(2,1)S(1)}, bf16[40,2048]{1,0:T(8,128)(2,1)S(1)}, u32[]{:S(2)}, u32[]{:S(2)}) collective-permute-start(bf16[40,2048]{1,0:T(8,128)(2,1)S(1)} %get-tuple-element.19), channel_id=1, source_target_pairs={{0,6},{1,7},{2,4},{3,5},{4,2},{5,3},{6,0},{7,1},{8,14},{9,15},{10,... | collective-permute-start | bytes 491528 | tf_op jit(solution)/shard_map/ppermute | solution.py:42
  97.3 10.3 %collective-permute-start.25 = (bf16[40,2048]{1,0:T(8,128)(2,1)S(1)}, bf16[40,2048]{1,0:T(8,128)(2,1)S(1)}, u32[]{:S(2)}, u32[]{:S(2)}) collective-permute-start(bf16[40,2048]{1,0:T(8,128)(2,1)S(1)} %get-tuple-element.20), channel_id=1, source_target_pairs={{0,7},{1,6},{2,5},{3,4},{4,3},{5,2},{6,1},{7,0},{8,15},{9,14},{10,... | collective-permute-start | bytes 491528 | tf_op jit(solution)/shard_map/ppermute | solution.py:42
  99.8 7.8 %collective-permute-start.13 = (bf16[40,2048]{1,0:T(8,128)(2,1)S(1)}, bf16[40,2048]{1,0:T(8,128)(2,1)S(1)}, u32[]{:S(2)}, u32[]{:S(2)}) collective-permute-start(bf16[40,2048]{1,0:T(8,128)(2,1)S(1)} %get-tuple-element.14), channel_id=1, source_target_pairs={{0,1},{1,0},{2,3},{3,2},{4,5},{5,4},{6,7},{7,6},{8,9},{9,8},{10,11... | collective-permute-start | bytes 491528 | tf_op jit(solution)/shard_map/ppermute | solution.py:42
  100.1 12.3 %collective-permute-start.14 = (bf16[40,2048]{1,0:T(8,128)(2,1)S(1)}, bf16[40,2048]{1,0:T(8,128)(2,1)S(1)}, u32[]{:S(2)}, u32[]{:S(2)}) collective-permute-start(bf16[40,2048]{1,0:T(8,128)(2,1)S(1)} %get-tuple-element.15), channel_id=1, source_target_pairs={{0,2},{1,3},{2,0},{3,1},{4,6},{5,7},{6,4},{7,5},{8,10},{9,11},{10,... | collective-permute-start | bytes 491528 | tf_op jit(solution)/shard_map/ppermute | solution.py:42
  100.6 14.9 %collective-permute-start.15 = (bf16[40,2048]{1,0:T(8,128)(2,1)S(1)}, bf16[40,2048]{1,0:T(8,128)(2,1)S(1)}, u32[]{:S(2)}, u32[]{:S(2)}) collective-permute-start(bf16[40,2048]{1,0:T(8,128)(2,1)S(1)} %get-tuple-element.16), channel_id=1, source_target_pairs={{0,3},{1,2},{2,1},{3,0},{4,7},{5,6},{6,5},{7,4},{8,11},{9,10},{10,... | collective-permute-start | bytes 491528 | tf_op jit(solution)/shard_map/ppermute | solution.py:42

commit v3 on v2

v3 whole, which is shorter than its diff:
```python
import functools

import jax
import jax.numpy as jnp
from jax import lax
from jax.experimental import pallas as pl
from jax.experimental.pallas import tpu as pltpu
from jax.sharding import PartitionSpec as P

BF16 = jnp.bfloat16
F32 = jnp.float32
AXES = ("dp", "expert")
VMEM_LIMIT = 8 << 20
BOTH_LAST = (((1,), (1,)), ((), ()))
BOTH_FIRST = (((0,), (0,)), ((), ()))


def few(n):
    return n - 1 <= 16


def near_far(n):
    return list(range(n // 2)), list(range(n // 2, n))


def pair_permute(values, n_dp, n_exp, weights_side):
    pairs = []
    for d in range(n_dp):
        for e in range(n_exp):
            high = (e % 2 == 0) == weights_side
            partner = d ^ (n_dp // 2) if high else d ^ 1
            pairs.append((d * n_exp + e, partner * n_exp + e))
    return lax.ppermute(values, AXES, pairs)


def expert_exchange(blocks):
    n = lax.axis_size("expert")
    if not few(n):
        place = jnp.arange(n, dtype=jnp.int32) ^ lax.axis_index("expert")
        there = lax.all_to_all(jnp.stack(blocks)[place], "expert", 0, 0, tiled=True)[place]
        return [there[k] for k in range(n)]
    return expert_send(blocks, range(n))


def expert_send(blocks, places):
    n, out = lax.axis_size("expert"), []
    for k, block in zip(places, blocks):
        if k:
            block = lax.ppermute(block, "expert", [(i, i ^ k) for i in range(n)])
        out.append(block)
    return out


def exchanged_counts(counts, late):
    n = lax.axis_size("dp") * lax.axis_size("expert")
    total, others = counts, []
    step = 1
    while step < n:
        if step == lax.axis_size("expert"):
            total, _ = lax.optimization_barrier((total, late))
        others.append(lax.ppermute(total, AXES, [(i, i ^ step) for i in range(n)]))
        total = total + others[-1]
        step *= 2
    return others


def dot(a, b):
    return jnp.dot(a, b, preferred_element_type=F32)


def kernel_call(body, shapes, operands, flops):
    spec = pl.BlockSpec(memory_space=pltpu.VMEM)
    single = not isinstance(shapes, (list, tuple))
    moved = sum(x.size * x.dtype.itemsize for x in operands)
    return pl.pallas_call(
        body,
        out_shape=shapes if single else tuple(shapes),
        in_specs=[spec] * len(operands),
        out_specs=spec if single else tuple([spec] * len(shapes)),
        compiler_params=pltpu.CompilerParams(vmem_limit_bytes=VMEM_LIMIT),
        cost_estimate=pl.CostEstimate(flops=flops, bytes_accessed=moved, transcendentals=0),
    )(*operands)


def join(blocks):
    if len(blocks) > 16:
        return jnp.concatenate(blocks, axis=0)
    rows, width = blocks[0].shape

    def body(*refs):
        for i, ref in enumerate(refs[:-1]):
            refs[-1][i * rows : (i + 1) * rows, :] = ref[...]

    shape = jax.ShapeDtypeStruct((rows * len(blocks), width), blocks[0].dtype)
    return kernel_call(body, shape, blocks, 0)


def hidden_of(rows, gate_t, up_t):
    def body(rows_ref, gate_ref, up_ref, out_ref):
        gate = lax.dot_general(rows_ref[...], gate_ref[...], BOTH_LAST, preferred_element_type=F32)
        up = lax.dot_general(rows_ref[...], up_ref[...], BOTH_LAST, preferred_element_type=F32)
        out_ref[...] = (gate / (1.0 + jnp.exp(-gate)) * up).astype(BF16)

    units = gate_t.shape[0]
    shape = jax.ShapeDtypeStruct((rows.shape[0], units), BF16)
    return kernel_call(body, shape, (rows, gate_t, up_t), 4 * rows.size * units)


def down(hidden, down_t, hidden2, down2_t, dtype, start=0):
    width = sum(piece.shape[1] for piece in down2_t)
    step = min(down2_t[0].shape[1], 512)

    def body(h_ref, w_ref, h2_ref, *refs):
        at = 0
        for ref in refs[:-1]:
            for here in range(0, ref.shape[1], step):
                columns = slice(start + at, start + at + step)
                part = dot(h_ref[...], w_ref[:, columns]) + dot(h2_ref[...], ref[:, here : here + step])
                refs[-1][:, at : at + step] = part.astype(dtype)
                at += step

    shape = jax.ShapeDtypeStruct((hidden.shape[0], width), dtype)
    return kernel_call(body, shape, (hidden, down_t, hidden2, *down2_t), 4 * hidden.size * width)


def add_and_split(own, returned, count):
    rows, width = own.shape[0] // count, own.shape[1]
    if count > 16:
        total = (own + returned.astype(F32)).astype(BF16).reshape(count, rows, width)
        return [total[k] for k in range(count)]

    def body(own_ref, returned_ref, *out_refs):
        for k, ref in enumerate(out_refs):
            part = slice(k * rows, (k + 1) * rows)
            ref[...] = (own_ref[part, :] + returned_ref[part, :].astype(F32)).astype(BF16)

    shapes = [jax.ShapeDtypeStruct((rows, width), BF16)] * count
    return list(kernel_call(body, shapes, (own, returned), own.size))


def named_places(ids, me, n):
    rows = ids.shape[1]
    place = lax.broadcasted_iota(jnp.int32, (n, rows), 0)
    named = [(ids[k : k + 1, :] ^ me) == place for k in range(ids.shape[0])]
    once = functools.reduce(jnp.logical_or, named)
    first = lax.broadcasted_iota(jnp.int32, (rows, rows), 0)
    second = lax.broadcasted_iota(jnp.int32, (rows, rows), 1)
    earlier = dot(ones_at(once), ones_at(first < second))
    return named, once, earlier


def ones_at(mask):
    return jnp.where(mask, 1.0, 0.0).astype(BF16)


def dispatch(tokens, ids, here, n, most):
    tok_rows, width = tokens.shape

    def body(tokens_ref, ids_ref, here_ref, counts_ref, *out_refs):
        me = here_ref[0, 0] % n
        _, once, earlier = named_places(ids_ref[...], me, n)
        _, absolute, _ = named_places(ids_ref[...], 0, n)
        ones = jnp.ones((1, tok_rows), BF16)
        counts = lax.dot_general(ones, ones_at(absolute), BOTH_LAST, preferred_element_type=F32)
        counts_ref[...] = counts.astype(jnp.int32)
        slot = jnp.where(once, earlier, -1.0)
        row = lax.broadcasted_iota(jnp.int32, (most, tok_rows), 0).astype(F32)
        for k in range(n):
            picked = dot(ones_at(row == slot[k : k + 1, :]), tokens_ref[...]).astype(BF16)
            if few(n):
                out_refs[k][...] = picked
            else:
                out_refs[0][k] = picked

    shapes = [jax.ShapeDtypeStruct((1, n), jnp.int32)]
    if few(n):
        shapes += [jax.ShapeDtypeStruct((most, width), BF16)] * n
    else:
        shapes += [jax.ShapeDtypeStruct((n, most, width), BF16)]
    memory = [pltpu.VMEM, pltpu.VMEM, pltpu.SMEM]
    call = pl.pallas_call(
        body,
        out_shape=tuple(shapes),
        in_specs=[pl.BlockSpec(memory_space=m) for m in memory],
        out_specs=tuple(pl.BlockSpec(memory_space=pltpu.VMEM) for _ in shapes),
        compiler_params=pltpu.CompilerParams(vmem_limit_bytes=VMEM_LIMIT),
        name="dispatch",
    )
    counts, *blocks = call(tokens, ids, here)
    return [blocks[0][k] for k in range(n)] if len(blocks) < n else blocks, counts


def mix(ids, units, capacity, others, here, back, corners, most):
    n, tok_rows, width = capacity.shape[1], ids.shape[1], sum(b.shape[0] * b.shape[1] for b in back)
    width = width // (n * most)

    def body(here_ref, ids_ref, units_ref, capacity_ref, *refs):
        other_refs, back_refs = refs[: len(others)], refs[len(others) : -2]
        out_ref, joined = refs[-2:]
        me = here_ref[0, 0]
        room = capacity_ref[...]
        for i, ref in enumerate(other_refs):
            room = room - ref[...] * ((me >> i) & 1)
        place = lax.broadcasted_iota(jnp.int32, (n, n), 0)
        expert = lax.broadcasted_iota(jnp.int32, (n, n), 1)
        room = jnp.sum(jnp.where(place ^ (me % n) == expert, room, 0).astype(F32), axis=1, keepdims=True)
        named, once, earlier = named_places(ids_ref[...], me % n, n)
        unit = sum(jnp.where(named[k], units_ref[k : k + 1, :], 0) for k in range(len(named)))
        unit = jnp.where(earlier < room, unit, 0)
        high = ((unit >> 3) << 3).astype(F32) * (1.0 / 1024.0)
        low = (unit & 7).astype(F32) * (1.0 / 1024.0)
        slot = jnp.where(once, earlier, -1.0)
        row = lax.broadcasted_iota(jnp.int32, (most, tok_rows), 0).astype(F32)

        def spread(values):
            parts = [jnp.where(row == slot[k : k + 1, :], values[k : k + 1, :], 0.0) for k in range(n)]
            return jnp.concatenate(parts, axis=0).astype(BF16)

        for at, ref in zip(corners, back_refs):
            joined[at[0] : at[0] + ref.shape[0], at[1] : at[1] + ref.shape[1]] = ref[...]
        mixed = lax.dot_general(spread(high), joined[...], BOTH_FIRST, preferred_element_type=F32)
        mixed += lax.dot_general(spread(low), joined[...], BOTH_FIRST, preferred_element_type=F32)
        out_ref[...] = mixed.astype(BF16)

    operands = (here, ids, units, capacity, *others, *back)
    memory = [pltpu.SMEM] + [pltpu.VMEM] * (len(operands) - 1)
    return pl.pallas_call(
        body,
        out_shape=jax.ShapeDtypeStruct((tok_rows, width), BF16),
        in_specs=[pl.BlockSpec(memory_space=m) for m in memory],
        out_specs=pl.BlockSpec(memory_space=pltpu.VMEM),
        scratch_shapes=[pltpu.VMEM((n * most, width), BF16)],
        compiler_params=pltpu.CompilerParams(vmem_limit_bytes=VMEM_LIMIT),
        name="mix",
    )(*operands)


def layer(tokens, expert_ids, gate_units, capacity, w_gate, w_up, w_down):
    n_dp, n_exp = lax.axis_size("dp"), lax.axis_size("expert")
    tok_rows, width = tokens.shape
    n_experts = capacity.shape[0]
    most = max(2, 5 * tok_rows // (2 * n_experts))
    here = jnp.full((1, 1), lax.axis_index(AXES), jnp.int32)
    near, far = near_far(n_experts)
    wg, wu, wd = w_gate[0].T, w_up[0].T, w_down[0].T
    here, wg, wu, wd = lax.optimization_barrier((here, wg, wu, wd))
    wg2 = pair_permute(wg, n_dp, n_exp, True)
    wu2 = pair_permute(wu, n_dp, n_exp, True)
    half = width // 2
    wd2_a = pair_permute(wd[:, :half], n_dp, n_exp, True)
    wd2_b = pair_permute(wd[:, half:], n_dp, n_exp, True)

    ids = expert_ids.T
    blocks, counts = dispatch(tokens, ids, here, n_experts, most)
    arrived = expert_exchange(blocks)
    own_near = join([arrived[k] for k in near])
    theirs_near = pair_permute(own_near, n_dp, n_exp, False)
    own_far = join([arrived[k] for k in far])
    theirs_far = pair_permute(own_far, n_dp, n_exp, False)

    def hidden_pair(rows):
        return hidden_of(rows, wg, wu), hidden_of(rows, wg2, wu2)

    def partial(pair, w2, dtype, start=0):
        return down(pair[0], wd, pair[1], w2, dtype, start)

    h_own_near = hidden_pair(own_near)
    h_own_far = hidden_pair(own_far)
    h_near = hidden_pair(theirs_near)
    h_far = hidden_pair(theirs_far)
    far_a = pair_permute(partial(h_far, [wd2_a], BF16), n_dp, n_exp, False)
    far_b = pair_permute(partial(h_far, [wd2_b], BF16, half), n_dp, n_exp, False)
    own_far_a = partial(h_own_far, [wd2_a], F32)
    own_far_b = partial(h_own_far, [wd2_b], F32, half)
    near_part = pair_permute(partial(h_near, [wd2_a, wd2_b], BF16), n_dp, n_exp, False)
    own_near_part = partial(h_own_near, [wd2_a, wd2_b], F32)
    answer_a = add_and_split(own_far_a, far_a, len(far))
    answer_b = add_and_split(own_far_b, far_b, len(far))
    answer_near = add_and_split(own_near_part, near_part, len(near))
    if few(n_experts):
        back = expert_send(answer_near, near)
        back += expert_send(answer_a, far) + expert_send(answer_b, far)
    else:
        answer_far = [jnp.concatenate(pair, axis=1) for pair in zip(answer_a, answer_b)]
        back = [jnp.concatenate(expert_exchange(answer_near + answer_far), axis=0)]

    counts, _ = lax.optimization_barrier((counts, own_far[0, 0]))
    others = exchanged_counts(counts, answer_a[0][0, 0])
    corners = [(0, 0)]
    if few(n_experts):
        corners = [(k * most, 0) for k in near + far] + [(k * most, half) for k in far]
    return mix(ids, gate_units.T, capacity[None, :], others, here, back, corners, most)


def solution(mesh):
    return jax.shard_map(
        layer,
        mesh=mesh,
        in_specs=(
            P(AXES, None),
            P(AXES, None),
            P(AXES, None),
            P(),
            P("expert", None, "dp"),
            P("expert", None, "dp"),
            P("expert", None, "dp"),
        ),
        out_specs=P(AXES, None),
        check_vma=False,
    )
```

time: 117 us -> 125 us (1.068)
  Pallas kernels: 33.5 us -> 15.2 us
  starting transfers between devices: 32.2 us -> 47.9 us
  waiting for transfers between devices: 49 us -> 59.9 us
  local copies, waits for them, and re-layouts: 0.28 us -> 1.87 us
    pallas_call x16 -> x19, Pallas kernels: 31.9 us -> 12.7 us  [kernel_call(): pl.pallas_call(body, out_shape=shapes if single else tuple(shapes), in_sp...]
    ppermute x7 -> x9, waiting for transfers between devices: 0.02 us -> 19.2 us  [pair_permute(): return lax.ppermute(values, AXES, pairs)]
    ppermute x19 -> x23, starting transfers between devices: 22.1 us -> 34.4 us  [the longest x18 28.5 us: expert_send(): block = lax.ppermute(block, 'expert', [(i, i ^ k) for i in range(n)])]
    ppermute x19 -> x23, waiting for transfers between devices: 49 us -> 40.7 us  [the longest x18 30.3 us: expert_send(): block = lax.ppermute(block, 'expert', [(i, i ^ k) for i in range(n)])]
    ppermute x7 -> x9, starting transfers between devices: 10.1 us -> 13.5 us  [pair_permute(): return lax.ppermute(values, AXES, pairs)]
    unnamed x14 -> x16, local copies, waits for them, and re-layouts: 0.04 us -> 1.75 us
    pallas_call x1 -> x2, Pallas kernels: 1.53 us -> 2.51 us  [the longest x1 1.7 us: mix(): pl.pallas_call(body, out_shape=jax.ShapeDtypeStruct((tok_rows, width), BF...]
  transfers between devices with their start and end apart: 26 -> 32, of which waited for: 14 -> 14; matrix products, arithmetic and copies ran while one was open for 2% -> 0% of each run, Pallas kernels for 27% -> 11%
where the time goes in v3:
time: 125 us
  waiting for transfers between devices  59.9 us (48%)
  starting transfers between devices  47.9 us (38%)
  Pallas kernels  15.2 us (12%)
  local copies, waits for them, and re-layouts  1.87 us (1%)
    ppermute x18, waiting for transfers between devices, expert_send(): block = lax.ppermute(block, 'expert', [(i, i ^ k) for i in range(n)])  30.3 us
    ppermute x18, starting transfers between devices, expert_send(): block = lax.ppermute(block, 'expert', [(i, i ^ k) for i in range(n)])  28.5 us
    ppermute x9, waiting for transfers between devices, pair_permute(): return lax.ppermute(values, AXES, pairs)  19.2 us
    ppermute x9, starting transfers between devices, pair_permute(): return lax.ppermute(values, AXES, pairs)  13.5 us
    pallas_call x19, Pallas kernels, kernel_call(): pl.pallas_call(body, out_shape=shapes if single else tuple(shapes), in_sp...  12.7 us
    ppermute x5, waiting for transfers between devices, exchanged_counts(): others.append(lax.ppermute(total, AXES, [(i, i ^ step) for i in range(n)]))  10.3 us
    ppermute x5, starting transfers between devices, exchanged_counts(): others.append(lax.ppermute(total, AXES, [(i, i ^ step) for i in range(n)]))  5.96 us
  transfers between devices with their start and end apart: 32, of which 14 were waited for; matrix products, arithmetic and copies ran while one was open for 0% of the time, Pallas kernels for 11%

profile of v3, /device:TPU:0, one launch (start us, length us, event | category | flops | bytes accessed | tf_op | source)
XLA Modules:
  0.0 125.2 jit_solution(9765666956692068409)
XLA Ops:
  0.0 3.0 %collective-permute-start.8 = (bf16[352,2048]{1,0:T(8,128)(2,1)}, bf16[352,2048]{1,0:T(8,128)(2,1)S(1)}, u32[]{:S(2)}, u32[]{:S(2)}) collective-permute-start(bf16[352,2048]{1,0:T(8,128)(2,1)} %bitcast.20), channel_id=1, source_target_pairs={{0,16},{1,9},{2,18},{3,11},{4,20},{5,13},{6,22},{7,15},{8,24},{9,1... | collective-permute-start | bytes 4325384 | tf_op jit(solution)/shard_map/ppermute | solution.py:33
  3.1 1.0 copy-done.3
  4.8 0.8 dispatch.1
  5.7 2.1 %collective-permute-start.6 = (bf16[40,2048]{1,0:T(8,128)(2,1)S(1)}, bf16[40,2048]{1,0:T(8,128)(2,1)S(1)}, u32[]{:S(2)}, u32[]{:S(2)}) collective-permute-start(bf16[40,2048]{1,0:T(8,128)(2,1)S(1)} %get-tuple-element.34), channel_id=1, source_target_pairs={{0,2},{1,3},{2,0},{3,1},{4,6},{5,7},{6,4},{7,5},{8,10},{9,11},{10,... | collective-permute-start | bytes 491528 | tf_op jit(solution)/shard_map/ppermute | solution.py:49
  7.8 2.8 %collective-permute-start.17 = (bf16[40,2048]{1,0:T(8,128)(2,1)S(1)}, bf16[40,2048]{1,0:T(8,128)(2,1)S(1)}, u32[]{:S(2)}, u32[]{:S(2)}) collective-permute-start(bf16[40,2048]{1,0:T(8,128)(2,1)S(1)} %get-tuple-element.43), channel_id=1, source_target_pairs={{0,4},{1,5},{2,6},{3,7},{4,0},{5,1},{6,2},{7,3},{8,12},{9,13},{10,... | collective-permute-start | bytes 491528 | tf_op jit(solution)/shard_map/ppermute | solution.py:49
  10.6 5.8 %collective-permute-done.6.refs_2_ = bf16[40,2048]{1,0:T(8,128)(2,1)S(1)} collective-permute-done((bf16[40,2048]{1,0:T(8,128)(2,1)S(1)}, bf16[40,2048]{1,0:T(8,128)(2,1)S(1)}, u32[]{:S(2)}, u32[]{:S(2)}) %collective-permute-start.6) | collective-permute-done | bytes 163872 | tf_op jit(solution)/shard_map/ppermute | solution.py:49
  16.3 3.0 %collective-permute-done.7.refs_3_ = bf16[40,2048]{1,0:T(8,128)(2,1)S(1)} collective-permute-done((bf16[40,2048]{1,0:T(8,128)(2,1)S(1)}, bf16[40,2048]{1,0:T(8,128)(2,1)S(1)}, u32[]{:S(2)}, u32[]{:S(2)}) %collective-permute-start.7) | collective-permute-done | bytes 163872 | tf_op jit(solution)/shard_map/ppermute | solution.py:49
  19.4 1.4 %collective-permute-start.12 = (bf16[160,2048]{1,0:T(8,128)(2,1)S(1)}, bf16[160,2048]{1,0:T(8,128)(2,1)S(1)}, u32[]{:S(2)}, u32[]{:S(2)}) collective-permute-start(bf16[160,2048]{1,0:T(8,128)(2,1)S(1)} %shard_map.73.rows_ref), channel_id=1, source_target_pairs={{0,8},{1,17},{2,10},{3,19},{4,12},{5,21},{6,14},{7,23},{8,0},{9,25... | collective-permute-start | bytes 1966088 | tf_op jit(solution)/shard_map/ppermute | solution.py:33
  20.8 3.6 %collective-permute-start.19 = (bf16[40,2048]{1,0:T(8,128)(2,1)S(1)}, bf16[40,2048]{1,0:T(8,128)(2,1)S(1)}, u32[]{:S(2)}, u32[]{:S(2)}) collective-permute-start(bf16[40,2048]{1,0:T(8,128)(2,1)S(1)} %get-tuple-element.45), channel_id=1, source_target_pairs={{0,6},{1,7},{2,4},{3,5},{4,2},{5,3},{6,0},{7,1},{8,14},{9,15},{10,... | collective-permute-start | bytes 491528 | tf_op jit(solution)/shard_map/ppermute | solution.py:49
  24.4 7.9 %collective-permute-done.18.refs_1_ = bf16[40,2048]{1,0:T(8,128)(2,1)S(1)} collective-permute-done((bf16[40,2048]{1,0:T(8,128)(2,1)S(1)}, bf16[40,2048]{1,0:T(8,128)(2,1)S(1)}, u32[]{:S(2)}, u32[]{:S(2)}) %collective-permute-start.18) | collective-permute-done | bytes 163872 | tf_op jit(solution)/shard_map/ppermute | solution.py:49
  32.3 1.0 collective-permute-start.20
  33.4 1.6 %collective-permute-start.11 = (bf16[352,1024]{1,0:T(8,128)(2,1)S(1)}, bf16[352,1024]{1,0:T(8,128)(2,1)S(1)}, u32[]{:S(2)}, u32[]{:S(2)}) collective-permute-start(bf16[352,1024]{1,0:T(8,128)(2,1)S(1)} %get-tuple-element.55), channel_id=1, source_target_pairs={{0,16},{1,9},{2,18},{3,11},{4,20},{5,13},{6,22},{7,15},{8,24},{9,1... | collective-permute-start | bytes 2162696 | tf_op jit(solution)/shard_map/ppermute | solution.py:33
  35.0 5.4 %collective-permute-done.20.refs_3_ = bf16[40,2048]{1,0:T(8,128)(2,1)S(1)} collective-permute-done((bf16[40,2048]{1,0:T(8,128)(2,1)S(1)}, bf16[40,2048]{1,0:T(8,128)(2,1)S(1)}, u32[]{:S(2)}, u32[]{:S(2)}) %collective-permute-start.20) | collective-permute-done | bytes 163872 | tf_op jit(solution)/shard_map/ppermute | solution.py:49
  40.5 1.7 %collective-permute-start.10 = (bf16[352,1024]{1,0:T(8,128)(2,1)S(1)}, bf16[352,1024]{1,0:T(8,128)(2,1)S(1)}, u32[]{:S(2)}, u32[]{:S(2)}) collective-permute-start(bf16[352,1024]{1,0:T(8,128)(2,1)S(1)} %get-tuple-element.56), channel_id=1, source_target_pairs={{0,16},{1,9},{2,18},{3,11},{4,20},{5,13},{6,22},{7,15},{8,24},{9,1... | collective-permute-start | bytes 2162696 | tf_op jit(solution)/shard_map/ppermute | solution.py:33
  42.2 1.6 %collective-permute-start.21 = (bf16[160,2048]{1,0:T(8,128)(2,1)S(1)}, bf16[160,2048]{1,0:T(8,128)(2,1)S(1)}, u32[]{:S(2)}, u32[]{:S(2)}) collective-permute-start(bf16[160,2048]{1,0:T(8,128)(2,1)S(1)} %shard_map.81.rows_ref), channel_id=1, source_target_pairs={{0,8},{1,17},{2,10},{3,19},{4,12},{5,21},{6,14},{7,23},{8,0},{9,25... | collective-permute-start | bytes 1966088 | tf_op jit(solution)/shard_map/ppermute | solution.py:33
  43.7 1.1 shard_map.77.h_ref
  44.9 1.1 shard_map.78.h2_ref
  45.9 10.3 %collective-permute-done.11.refs_1_.refs_0_ = bf16[352,1024]{1,0:T(8,128)(2,1)S(1)} collective-permute-done((bf16[352,1024]{1,0:T(8,128)(2,1)S(1)}, bf16[352,1024]{1,0:T(8,128)(2,1)S(1)}, u32[]{:S(2)}, u32[]{:S(2)}) %collective-permute-start.11) | collective-permute-done | bytes 720928 | tf_op jit(solution)/shard_map/ppermute | solution.py:33
  56.2 8.9 %collective-permute-done.10.refs_0_ = bf16[352,1024]{1,0:T(8,128)(2,1)S(1)} collective-permute-done((bf16[352,1024]{1,0:T(8,128)(2,1)S(1)}, bf16[352,1024]{1,0:T(8,128)(2,1)S(1)}, u32[]{:S(2)}, u32[]{:S(2)}) %collective-permute-start.10) | collective-permute-done | bytes 720928 | tf_op jit(solution)/shard_map/ppermute | solution.py:33
  65.1 0.9 shard_map.79
  66.0 2.1 %collective-permute-start.13 = (bf16[160,2048]{1,0:T(8,128)(2,1)S(1)}, bf16[160,2048]{1,0:T(8,128)(2,1)S(1)}, u32[]{:S(2)}, u32[]{:S(2)}) collective-permute-start(bf16[160,2048]{1,0:T(8,128)(2,1)S(1)} %shard_map.79), channel_id=1, source_target_pairs={{0,8},{1,17},{2,10},{3,19},{4,12},{5,21},{6,14},{7,23},{8,0},{9,25... | collective-permute-start | bytes 1966088 | tf_op jit(solution)/shard_map/ppermute | solution.py:33
  68.1 1.1 shard_map.85.h_ref
  69.2 1.1 shard_map.86.h2_ref
  71.4 2.1 %collective-permute-start.22 = (bf16[160,1024]{1,0:T(8,128)(2,1)S(1)}, bf16[160,1024]{1,0:T(8,128)(2,1)S(1)}, u32[]{:S(2)}, u32[]{:S(2)}) collective-permute-start(bf16[160,1024]{1,0:T(8,128)(2,1)S(1)} %shard_map.87), channel_id=1, source_target_pairs={{0,8},{1,17},{2,10},{3,19},{4,12},{5,21},{6,14},{7,23},{8,0},{9,25... | collective-permute-start | bytes 983048 | tf_op jit(solution)/shard_map/ppermute | solution.py:33
  73.4 1.2 collective-permute-done.refs_0_
  74.6 1.6 %collective-permute-start.1 = (s32[1,8]{1,0:T(1,128)S(1)}, s32[1,8]{1,0:T(1,128)S(1)}, u32[]{:S(2)}, u32[]{:S(2)}) collective-permute-start(s32[1,8]{1,0:T(1,128)S(1)} %add.16), channel_id=1, source_target_pairs={{0,2},{1,3},{2,0},{3,1},{4,6},{5,7},{6,4},{7,5},{8,10},{9,11},{10,... | collective-permute-start | bytes 104 | tf_op jit(solution)/shard_map/ppermute | solution.py:61
  76.2 2.0 %collective-permute-done.1.refs_1_ = s32[1,8]{1,0:T(1,128)S(1)} collective-permute-done((s32[1,8]{1,0:T(1,128)S(1)}, s32[1,8]{1,0:T(1,128)S(1)}, u32[]{:S(2)}, u32[]{:S(2)}) %collective-permute-start.1) | collective-permute-done | bytes 64 | tf_op jit(solution)/shard_map/ppermute | solution.py:61
  78.2 2.6 %collective-permute-start.2 = (s32[1,8]{1,0:T(1,128)S(1)}, s32[1,8]{1,0:T(1,128)S(1)}, u32[]{:S(2)}, u32[]{:S(2)}) collective-permute-start(s32[1,8]{1,0:T(1,128)S(1)} %add.17), channel_id=1, source_target_pairs={{0,4},{1,5},{2,6},{3,7},{4,0},{5,1},{6,2},{7,3},{8,12},{9,13},{10,... | collective-permute-start | bytes 104 | tf_op jit(solution)/shard_map/ppermute | solution.py:61
  80.8 1.9 %collective-permute-done.2.refs_2_ = s32[1,8]{1,0:T(1,128)S(1)} collective-permute-done((s32[1,8]{1,0:T(1,128)S(1)}, s32[1,8]{1,0:T(1,128)S(1)}, u32[]{:S(2)}, u32[]{:S(2)}) %collective-permute-start.2) | collective-permute-done | bytes 64 | tf_op jit(solution)/shard_map/ppermute | solution.py:61
  82.8 3.4 %collective-permute-done.3.refs_3_ = s32[1,8]{1,0:T(1,128)S(1)} collective-permute-done((s32[1,8]{1,0:T(1,128)S(1)}, s32[1,8]{1,0:T(1,128)S(1)}, u32[]{:S(2)}, u32[]{:S(2)}) %collective-permute-start.3) | collective-permute-done | bytes 64 | tf_op jit(solution)/shard_map/ppermute | solution.py:61
  86.2 1.1 shard_map.82.h_ref
  87.3 1.1 shard_map.74.h_ref
  88.4 1.1 shard_map.83.h2_ref
  90.6 2.7 %collective-permute-start.28 = (bf16[40,1024]{1,0:T(8,128)(2,1)S(1)}, bf16[40,1024]{1,0:T(8,128)(2,1)S(1)}, u32[]{:S(2)}, u32[]{:S(2)}) collective-permute-start(bf16[40,1024]{1,0:T(8,128)(2,1)S(1)} %get-tuple-element.51), channel_id=1, source_target_pairs={{0,4},{1,5},{2,6},{3,7},{4,0},{5,1},{6,2},{7,3},{8,12},{9,13},{10,... | collective-permute-start | bytes 245768 | tf_op jit(solution)/shard_map/ppermute | solution.py:49
  93.2 1.3 %collective-permute-start.30 = (bf16[40,1024]{1,0:T(8,128)(2,1)S(1)}, bf16[40,1024]{1,0:T(8,128)(2,1)S(1)}, u32[]{:S(2)}, u32[]{:S(2)}) collective-permute-start(bf16[40,1024]{1,0:T(8,128)(2,1)S(1)} %get-tuple-element.53), channel_id=1, source_target_pairs={{0,6},{1,7},{2,4},{3,5},{4,2},{5,3},{6,0},{7,1},{8,14},{9,15},{10,... | collective-permute-start | bytes 245768 | tf_op jit(solution)/shard_map/ppermute | solution.py:49
  94.6 2.3 %collective-permute-start.31 = (bf16[40,1024]{1,0:T(8,128)(2,1)S(1)}, bf16[40,1024]{1,0:T(8,128)(2,1)S(1)}, u32[]{:S(2)}, u32[]{:S(2)}) collective-permute-start(bf16[40,1024]{1,0:T(8,128)(2,1)S(1)} %get-tuple-element.54), channel_id=1, source_target_pairs={{0,7},{1,6},{2,5},{3,4},{4,3},{5,2},{6,1},{7,0},{8,15},{9,14},{10,... | collective-permute-start | bytes 245768 | tf_op jit(solution)/shard_map/ppermute | solution.py:49
  96.9 1.1 shard_map.75.h2_ref
  98.0 0.8 shard_map.76.own_ref
  98.9 1.6 %collective-permute-start.4 = (s32[1,8]{1,0:T(1,128)S(1)}, s32[1,8]{1,0:T(1,128)S(1)}, u32[]{:S(2)}, u32[]{:S(2)}) collective-permute-start(s32[1,8]{1,0:T(1,128)S(1)} %add.19), channel_id=1, source_target_pairs={{0,16},{1,17},{2,18},{3,19},{4,20},{5,21},{6,22},{7,23},{8,24},{9,... | collective-permute-start | bytes 104 | tf_op jit(solution)/shard_map/ppermute | solution.py:61
  100.6 1.9 %collective-permute-done.4.refs_4_ = s32[1,8]{1,0:T(1,128)S(1)} collective-permute-done((s32[1,8]{1,0:T(1,128)S(1)}, s32[1,8]{1,0:T(1,128)S(1)}, u32[]{:S(2)}, u32[]{:S(2)}) %collective-permute-start.4) | collective-permute-done | bytes 64 | tf_op jit(solution)/shard_map/ppermute | solution.py:61
  103.3 0.9 collective-permute-start.24
  104.3 1.4 %collective-permute-start.14 = (bf16[40,2048]{1,0:T(8,128)(2,1)S(1)}, bf16[40,2048]{1,0:T(8,128)(2,1)S(1)}, u32[]{:S(2)}, u32[]{:S(2)}) collective-permute-start(bf16[40,2048]{1,0:T(8,128)(2,1)S(1)} %get-tuple-element.40), channel_id=1, source_target_pairs={{0,1},{1,0},{2,3},{3,2},{4,5},{5,4},{6,7},{7,6},{8,9},{9,8},{10,11... | collective-permute-start | bytes 491528 | tf_op jit(solution)/shard_map/ppermute | solution.py:49
  105.6 4.9 %collective-permute-start.15 = (bf16[40,2048]{1,0:T(8,128)(2,1)S(1)}, bf16[40,2048]{1,0:T(8,128)(2,1)S(1)}, u32[]{:S(2)}, u32[]{:S(2)}) collective-permute-start(bf16[40,2048]{1,0:T(8,128)(2,1)S(1)} %get-tuple-element.41), channel_id=1, source_target_pairs={{0,2},{1,3},{2,0},{3,1},{4,6},{5,7},{6,4},{7,5},{8,10},{9,11},{10,... | collective-permute-start | bytes 491528 | tf_op jit(solution)/shard_map/ppermute | solution.py:49
  110.5 2.0 %collective-permute-done.23.refs_9_ = bf16[40,1024]{1,0:T(8,128)(2,1)S(1)} collective-permute-done((bf16[40,1024]{1,0:T(8,128)(2,1)S(1)}, bf16[40,1024]{1,0:T(8,128)(2,1)S(1)}, u32[]{:S(2)}, u32[]{:S(2)}) %collective-permute-start.23) | collective-permute-done | bytes 81952 | tf_op jit(solution)/shard_map/ppermute | solution.py:49
  112.5 4.4 %collective-permute-start.25 = (bf16[40,1024]{1,0:T(8,128)(2,1)S(1)}, bf16[40,1024]{1,0:T(8,128)(2,1)S(1)}, u32[]{:S(2)}, u32[]{:S(2)}) collective-permute-start(bf16[40,1024]{1,0:T(8,128)(2,1)S(1)} %get-tuple-element.49), channel_id=1, source_target_pairs={{0,6},{1,7},{2,4},{3,5},{4,2},{5,3},{6,0},{7,1},{8,14},{9,15},{10,... | collective-permute-start | bytes 245768 | tf_op jit(solution)/shard_map/ppermute | solution.py:49
  117.2 4.8 %collective-permute-done.25.refs_11_ = bf16[40,1024]{1,0:T(8,128)(2,1)S(1)} collective-permute-done((bf16[40,1024]{1,0:T(8,128)(2,1)S(1)}, bf16[40,1024]{1,0:T(8,128)(2,1)S(1)}, u32[]{:S(2)}, u32[]{:S(2)}) %collective-permute-start.25) | collective-permute-done | bytes 81952 | tf_op jit(solution)/shard_map/ppermute | solution.py:49
  122.0 1.4 %collective-permute-done.26.refs_12_ = bf16[40,1024]{1,0:T(8,128)(2,1)S(1)} collective-permute-done((bf16[40,1024]{1,0:T(8,128)(2,1)S(1)}, bf16[40,1024]{1,0:T(8,128)(2,1)S(1)}, u32[]{:S(2)}, u32[]{:S(2)}) %collective-permute-start.26) | collective-permute-done | bytes 81952 | tf_op jit(solution)/shard_map/ppermute | solution.py:49
  123.5 1.7 %mix.1 = bf16[128,2048]{1,0:T(8,128)(2,1)} custom-call(s32[1,1]{1,0:T(1,128)} %bitcast.here_ref, s32[2,128]{1,0:T(2,128)S(1)} %bitcast.31, s32[2,128]{1,0:T(2,128)S(1)} %bitcast.32, s32[1,8]{1,0:T(1,128)S(1)} %bitcast.33, s32[1,8]{1,0:T(1,128)S(1)} %collective-permute-done.refs_0_, s32[1,8]{1,0:T(1,128)S(1)} %collective-permute-done.1.refs_1_, ...), custom_call_target="tpu_custom_call" | custom-call | tf_op jit(solution)/shard_map/mix/pallas_call | solution.py:227
  (58 shorter events, 4.7 us)
Async XLA Ops:
  0.0 33.3 %copy-start = (bf16[1,2048,352]{1,2,0:T(8,128)(2,1)S(1)}, bf16[1,2048,352]{1,2,0:T(8,128)(2,1)}, u32[]{:S(2)}) copy-start(bf16[1,2048,352]{1,2,0:T(8,128)(2,1)} %param.13) | copy-start | bytes 4325380
  0.0 44.8 %collective-permute-start.8 = (bf16[352,2048]{1,0:T(8,128)(2,1)}, bf16[352,2048]{1,0:T(8,128)(2,1)S(1)}, u32[]{:S(2)}, u32[]{:S(2)}) collective-permute-start(bf16[352,2048]{1,0:T(8,128)(2,1)} %bitcast.20), channel_id=1, source_target_pairs={{0,16},{1,9},{2,18},{3,11},{4,20},{5,13},{6,22},{7,15},{8,24},{9,1... | collective-permute-start | bytes 4325384 | tf_op jit(solution)/shard_map/ppermute | solution.py:33
  3.0 41.8 %collective-permute-start.9 = (bf16[352,2048]{1,0:T(8,128)(2,1)}, bf16[352,2048]{1,0:T(8,128)(2,1)S(1)}, u32[]{:S(2)}, u32[]{:S(2)}) collective-permute-start(bf16[352,2048]{1,0:T(8,128)(2,1)} %bitcast.25), channel_id=1, source_target_pairs={{0,16},{1,9},{2,18},{3,11},{4,20},{5,13},{6,22},{7,15},{8,24},{9,1... | collective-permute-start | bytes 4325384 | tf_op jit(solution)/shard_map/ppermute | solution.py:33
  3.1 1.0 copy-start.3
  4.1 0.7 copy-start.4
  5.6 2.2 %collective-permute-start.5 = (bf16[40,2048]{1,0:T(8,128)(2,1)S(1)}, bf16[40,2048]{1,0:T(8,128)(2,1)S(1)}, u32[]{:S(2)}, u32[]{:S(2)}) collective-permute-start(bf16[40,2048]{1,0:T(8,128)(2,1)S(1)} %get-tuple-element.33), channel_id=1, source_target_pairs={{0,1},{1,0},{2,3},{3,2},{4,5},{5,4},{6,7},{7,6},{8,9},{9,8},{10,11... | collective-permute-start | bytes 491528 | tf_op jit(solution)/shard_map/ppermute | solution.py:49
  5.7 10.6 %collective-permute-start.6 = (bf16[40,2048]{1,0:T(8,128)(2,1)S(1)}, bf16[40,2048]{1,0:T(8,128)(2,1)S(1)}, u32[]{:S(2)}, u32[]{:S(2)}) collective-permute-start(bf16[40,2048]{1,0:T(8,128)(2,1)S(1)} %get-tuple-element.34), channel_id=1, source_target_pairs={{0,2},{1,3},{2,0},{3,1},{4,6},{5,7},{6,4},{7,5},{8,10},{9,11},{10,... | collective-permute-start | bytes 491528 | tf_op jit(solution)/shard_map/ppermute | solution.py:49
  7.8 11.6 %collective-permute-start.7 = (bf16[40,2048]{1,0:T(8,128)(2,1)S(1)}, bf16[40,2048]{1,0:T(8,128)(2,1)S(1)}, u32[]{:S(2)}, u32[]{:S(2)}) collective-permute-start(bf16[40,2048]{1,0:T(8,128)(2,1)S(1)} %get-tuple-element.35), channel_id=1, source_target_pairs={{0,3},{1,2},{2,1},{3,0},{4,7},{5,6},{6,5},{7,4},{8,11},{9,10},{10,... | collective-permute-start | bytes 491528 | tf_op jit(solution)/shard_map/ppermute | solution.py:49
  7.8 13.0 %collective-permute-start.17 = (bf16[40,2048]{1,0:T(8,128)(2,1)S(1)}, bf16[40,2048]{1,0:T(8,128)(2,1)S(1)}, u32[]{:S(2)}, u32[]{:S(2)}) collective-permute-start(bf16[40,2048]{1,0:T(8,128)(2,1)S(1)} %get-tuple-element.43), channel_id=1, source_target_pairs={{0,4},{1,5},{2,6},{3,7},{4,0},{5,1},{6,2},{7,3},{8,12},{9,13},{10,... | collective-permute-start | bytes 491528 | tf_op jit(solution)/shard_map/ppermute | solution.py:49
  16.3 16.0 %collective-permute-start.18 = (bf16[40,2048]{1,0:T(8,128)(2,1)S(1)}, bf16[40,2048]{1,0:T(8,128)(2,1)S(1)}, u32[]{:S(2)}, u32[]{:S(2)}) collective-permute-start(bf16[40,2048]{1,0:T(8,128)(2,1)S(1)} %get-tuple-element.44), channel_id=1, source_target_pairs={{0,5},{1,4},{2,7},{3,6},{4,1},{5,0},{6,3},{7,2},{8,13},{9,12},{10,... | collective-permute-start | bytes 491528 | tf_op jit(solution)/shard_map/ppermute | solution.py:49
  19.4 22.8 %collective-permute-start.12 = (bf16[160,2048]{1,0:T(8,128)(2,1)S(1)}, bf16[160,2048]{1,0:T(8,128)(2,1)S(1)}, u32[]{:S(2)}, u32[]{:S(2)}) collective-permute-start(bf16[160,2048]{1,0:T(8,128)(2,1)S(1)} %shard_map.73.rows_ref), channel_id=1, source_target_pairs={{0,8},{1,17},{2,10},{3,19},{4,12},{5,21},{6,14},{7,23},{8,0},{9,25... | collective-permute-start | bytes 1966088 | tf_op jit(solution)/shard_map/ppermute | solution.py:33
  20.8 12.6 %collective-permute-start.19 = (bf16[40,2048]{1,0:T(8,128)(2,1)S(1)}, bf16[40,2048]{1,0:T(8,128)(2,1)S(1)}, u32[]{:S(2)}, u32[]{:S(2)}) collective-permute-start(bf16[40,2048]{1,0:T(8,128)(2,1)S(1)} %get-tuple-element.45), channel_id=1, source_target_pairs={{0,6},{1,7},{2,4},{3,5},{4,2},{5,3},{6,0},{7,1},{8,14},{9,15},{10,... | collective-permute-start | bytes 491528 | tf_op jit(solution)/shard_map/ppermute | solution.py:49
  32.3 11.4 %copy-start.1 = (bf16[1,2048,352]{1,2,0:T(8,128)(2,1)S(1)}, bf16[1,2048,352]{1,2,0:T(8,128)(2,1)}, u32[]{:S(2)}) copy-start(bf16[1,2048,352]{1,2,0:T(8,128)(2,1)} %param.11) | copy-start | bytes 4325380
  32.3 11.4 %copy-start.2 = (bf16[1,2048,352]{1,2,0:T(8,128)(2,1)S(1)}, bf16[1,2048,352]{1,2,0:T(8,128)(2,1)}, u32[]{:S(2)}) copy-start(bf16[1,2048,352]{1,2,0:T(8,128)(2,1)} %param.12) | copy-start | bytes 4325380
  32.3 8.1 %collective-permute-start.20 = (bf16[40,2048]{1,0:T(8,128)(2,1)S(1)}, bf16[40,2048]{1,0:T(8,128)(2,1)S(1)}, u32[]{:S(2)}, u32[]{:S(2)}) collective-permute-start(bf16[40,2048]{1,0:T(8,128)(2,1)S(1)} %get-tuple-element.46), channel_id=1, source_target_pairs={{0,7},{1,6},{2,5},{3,4},{4,3},{5,2},{6,1},{7,0},{8,15},{9,14},{10,... | collective-permute-start | bytes 491528 | tf_op jit(solution)/shard_map/ppermute | solution.py:49
  33.4 22.8 %collective-permute-start.11 = (bf16[352,1024]{1,0:T(8,128)(2,1)S(1)}, bf16[352,1024]{1,0:T(8,128)(2,1)S(1)}, u32[]{:S(2)}, u32[]{:S(2)}) collective-permute-start(bf16[352,1024]{1,0:T(8,128)(2,1)S(1)} %get-tuple-element.55), channel_id=1, source_target_pairs={{0,16},{1,9},{2,18},{3,11},{4,20},{5,13},{6,22},{7,15},{8,24},{9,1... | collective-permute-start | bytes 2162696 | tf_op jit(solution)/shard_map/ppermute | solution.py:33
  40.5 24.7 %collective-permute-start.10 = (bf16[352,1024]{1,0:T(8,128)(2,1)S(1)}, bf16[352,1024]{1,0:T(8,128)(2,1)S(1)}, u32[]{:S(2)}, u32[]{:S(2)}) collective-permute-start(bf16[352,1024]{1,0:T(8,128)(2,1)S(1)} %get-tuple-element.56), channel_id=1, source_target_pairs={{0,16},{1,9},{2,18},{3,11},{4,20},{5,13},{6,22},{7,15},{8,24},{9,1... | collective-permute-start | bytes 2162696 | tf_op jit(solution)/shard_map/ppermute | solution.py:33
  42.2 25.9 %collective-permute-start.21 = (bf16[160,2048]{1,0:T(8,128)(2,1)S(1)}, bf16[160,2048]{1,0:T(8,128)(2,1)S(1)}, u32[]{:S(2)}, u32[]{:S(2)}) collective-permute-start(bf16[160,2048]{1,0:T(8,128)(2,1)S(1)} %shard_map.81.rows_ref), channel_id=1, source_target_pairs={{0,8},{1,17},{2,10},{3,19},{4,12},{5,21},{6,14},{7,23},{8,0},{9,25... | collective-permute-start | bytes 1966088 | tf_op jit(solution)/shard_map/ppermute | solution.py:33
  66.0 32.9 %collective-permute-start.13 = (bf16[160,2048]{1,0:T(8,128)(2,1)S(1)}, bf16[160,2048]{1,0:T(8,128)(2,1)S(1)}, u32[]{:S(2)}, u32[]{:S(2)}) collective-permute-start(bf16[160,2048]{1,0:T(8,128)(2,1)S(1)} %shard_map.79), channel_id=1, source_target_pairs={{0,8},{1,17},{2,10},{3,19},{4,12},{5,21},{6,14},{7,23},{8,0},{9,25... | collective-permute-start | bytes 1966088 | tf_op jit(solution)/shard_map/ppermute | solution.py:33
  70.8 19.7 %collective-permute-start.27 = (bf16[160,1024]{1,0:T(8,128)(2,1)S(1)}, bf16[160,1024]{1,0:T(8,128)(2,1)S(1)}, u32[]{:S(2)}, u32[]{:S(2)}) collective-permute-start(bf16[160,1024]{1,0:T(8,128)(2,1)S(1)} %shard_map.90), channel_id=1, source_target_pairs={{0,8},{1,17},{2,10},{3,19},{4,12},{5,21},{6,14},{7,23},{8,0},{9,25... | collective-permute-start | bytes 983048 | tf_op jit(solution)/shard_map/ppermute | solution.py:33
  71.4 23.2 %collective-permute-start.22 = (bf16[160,1024]{1,0:T(8,128)(2,1)S(1)}, bf16[160,1024]{1,0:T(8,128)(2,1)S(1)}, u32[]{:S(2)}, u32[]{:S(2)}) collective-permute-start(bf16[160,1024]{1,0:T(8,128)(2,1)S(1)} %shard_map.87), channel_id=1, source_target_pairs={{0,8},{1,17},{2,10},{3,19},{4,12},{5,21},{6,14},{7,23},{8,0},{9,25... | collective-permute-start | bytes 983048 | tf_op jit(solution)/shard_map/ppermute | solution.py:33
  73.4 1.2 collective-permute-start
  74.6 3.6 %collective-permute-start.1 = (s32[1,8]{1,0:T(1,128)S(1)}, s32[1,8]{1,0:T(1,128)S(1)}, u32[]{:S(2)}, u32[]{:S(2)}) collective-permute-start(s32[1,8]{1,0:T(1,128)S(1)} %add.16), channel_id=1, source_target_pairs={{0,2},{1,3},{2,0},{3,1},{4,6},{5,7},{6,4},{7,5},{8,10},{9,11},{10,... | collective-permute-start | bytes 104 | tf_op jit(solution)/shard_map/ppermute | solution.py:61
  78.2 4.5 %collective-permute-start.2 = (s32[1,8]{1,0:T(1,128)S(1)}, s32[1,8]{1,0:T(1,128)S(1)}, u32[]{:S(2)}, u32[]{:S(2)}) collective-permute-start(s32[1,8]{1,0:T(1,128)S(1)} %add.17), channel_id=1, source_target_pairs={{0,4},{1,5},{2,6},{3,7},{4,0},{5,1},{6,2},{7,3},{8,12},{9,13},{10,... | collective-permute-start | bytes 104 | tf_op jit(solution)/shard_map/ppermute | solution.py:61
  82.6 3.6 %collective-permute-start.3 = (s32[1,8]{1,0:T(1,128)S(1)}, s32[1,8]{1,0:T(1,128)S(1)}, u32[]{:S(2)}, u32[]{:S(2)}) collective-permute-start(s32[1,8]{1,0:T(1,128)S(1)} %add.18), channel_id=1, source_target_pairs={{0,8},{1,9},{2,10},{3,11},{4,12},{5,13},{6,14},{7,15},{8,0},{9,1},... | collective-permute-start | bytes 104 | tf_op jit(solution)/shard_map/ppermute | solution.py:61
  90.6 12.7 %collective-permute-start.28 = (bf16[40,1024]{1,0:T(8,128)(2,1)S(1)}, bf16[40,1024]{1,0:T(8,128)(2,1)S(1)}, u32[]{:S(2)}, u32[]{:S(2)}) collective-permute-start(bf16[40,1024]{1,0:T(8,128)(2,1)S(1)} %get-tuple-element.51), channel_id=1, source_target_pairs={{0,4},{1,5},{2,6},{3,7},{4,0},{5,1},{6,2},{7,3},{8,12},{9,13},{10,... | collective-permute-start | bytes 245768 | tf_op jit(solution)/shard_map/ppermute | solution.py:49
  93.2 11.0 %collective-permute-start.29 = (bf16[40,1024]{1,0:T(8,128)(2,1)S(1)}, bf16[40,1024]{1,0:T(8,128)(2,1)S(1)}, u32[]{:S(2)}, u32[]{:S(2)}) collective-permute-start(bf16[40,1024]{1,0:T(8,128)(2,1)S(1)} %get-tuple-element.52), channel_id=1, source_target_pairs={{0,5},{1,4},{2,7},{3,6},{4,1},{5,0},{6,3},{7,2},{8,13},{9,12},{10,... | collective-permute-start | bytes 245768 | tf_op jit(solution)/shard_map/ppermute | solution.py:49
  93.2 12.4 %collective-permute-start.30 = (bf16[40,1024]{1,0:T(8,128)(2,1)S(1)}, bf16[40,1024]{1,0:T(8,128)(2,1)S(1)}, u32[]{:S(2)}, u32[]{:S(2)}) collective-permute-start(bf16[40,1024]{1,0:T(8,128)(2,1)S(1)} %get-tuple-element.53), channel_id=1, source_target_pairs={{0,6},{1,7},{2,4},{3,5},{4,2},{5,3},{6,0},{7,1},{8,14},{9,15},{10,... | collective-permute-start | bytes 245768 | tf_op jit(solution)/shard_map/ppermute | solution.py:49
  94.6 15.9 %collective-permute-start.31 = (bf16[40,1024]{1,0:T(8,128)(2,1)S(1)}, bf16[40,1024]{1,0:T(8,128)(2,1)S(1)}, u32[]{:S(2)}, u32[]{:S(2)}) collective-permute-start(bf16[40,1024]{1,0:T(8,128)(2,1)S(1)} %get-tuple-element.54), channel_id=1, source_target_pairs={{0,7},{1,6},{2,5},{3,4},{4,3},{5,2},{6,1},{7,0},{8,15},{9,14},{10,... | collective-permute-start | bytes 245768 | tf_op jit(solution)/shard_map/ppermute | solution.py:49
  98.8 24.6 %copy-start.5 = (s32[128,2]{0,1:T(2,128)S(1)}, s32[128,2]{0,1:T(2,128)}, u32[]{:S(2)}) copy-start(s32[128,2]{0,1:T(2,128)} %param.8) | copy-start | bytes 3076
  98.8 24.6 %copy-start.6 = (s32[128,2]{0,1:T(2,128)S(1)}, s32[128,2]{0,1:T(2,128)}, u32[]{:S(2)}) copy-start(s32[128,2]{0,1:T(2,128)} %param.9) | copy-start | bytes 3076
  98.8 24.6 %copy-start.7 = (s32[8]{0:T(128)S(1)}, s32[8]{0:T(128)}, u32[]{:S(2)}) copy-start(s32[8]{0:T(128)} %param.10) | copy-start | bytes 100
  98.9 3.6 %collective-permute-start.4 = (s32[1,8]{1,0:T(1,128)S(1)}, s32[1,8]{1,0:T(1,128)S(1)}, u32[]{:S(2)}, u32[]{:S(2)}) collective-permute-start(s32[1,8]{1,0:T(1,128)S(1)} %add.19), channel_id=1, source_target_pairs={{0,16},{1,17},{2,18},{3,19},{4,20},{5,21},{6,22},{7,23},{8,24},{9,... | collective-permute-start | bytes 104 | tf_op jit(solution)/shard_map/ppermute | solution.py:61
  102.6 9.9 %collective-permute-start.23 = (bf16[40,1024]{1,0:T(8,128)(2,1)S(1)}, bf16[40,1024]{1,0:T(8,128)(2,1)S(1)}, u32[]{:S(2)}, u32[]{:S(2)}) collective-permute-start(bf16[40,1024]{1,0:T(8,128)(2,1)S(1)} %get-tuple-element.47), channel_id=1, source_target_pairs={{0,4},{1,5},{2,6},{3,7},{4,0},{5,1},{6,2},{7,3},{8,12},{9,13},{10,... | collective-permute-start | bytes 245768 | tf_op jit(solution)/shard_map/ppermute | solution.py:49
  103.3 13.6 %collective-permute-start.24 = (bf16[40,1024]{1,0:T(8,128)(2,1)S(1)}, bf16[40,1024]{1,0:T(8,128)(2,1)S(1)}, u32[]{:S(2)}, u32[]{:S(2)}) collective-permute-start(bf16[40,1024]{1,0:T(8,128)(2,1)S(1)} %get-tuple-element.48), channel_id=1, source_target_pairs={{0,5},{1,4},{2,7},{3,6},{4,1},{5,0},{6,3},{7,2},{8,13},{9,12},{10,... | collective-permute-start | bytes 245768 | tf_op jit(solution)/shard_map/ppermute | solution.py:49
  104.3 19.2 %collective-permute-start.14 = (bf16[40,2048]{1,0:T(8,128)(2,1)S(1)}, bf16[40,2048]{1,0:T(8,128)(2,1)S(1)}, u32[]{:S(2)}, u32[]{:S(2)}) collective-permute-start(bf16[40,2048]{1,0:T(8,128)(2,1)S(1)} %get-tuple-element.40), channel_id=1, source_target_pairs={{0,1},{1,0},{2,3},{3,2},{4,5},{5,4},{6,7},{7,6},{8,9},{9,8},{10,11... | collective-permute-start | bytes 491528 | tf_op jit(solution)/shard_map/ppermute | solution.py:49
  105.6 17.8 %collective-permute-start.15 = (bf16[40,2048]{1,0:T(8,128)(2,1)S(1)}, bf16[40,2048]{1,0:T(8,128)(2,1)S(1)}, u32[]{:S(2)}, u32[]{:S(2)}) collective-permute-start(bf16[40,2048]{1,0:T(8,128)(2,1)S(1)} %get-tuple-element.41), channel_id=1, source_target_pairs={{0,2},{1,3},{2,0},{3,1},{4,6},{5,7},{6,4},{7,5},{8,10},{9,11},{10,... | collective-permute-start | bytes 491528 | tf_op jit(solution)/shard_map/ppermute | solution.py:49
  110.5 13.0 %collective-permute-start.16 = (bf16[40,2048]{1,0:T(8,128)(2,1)S(1)}, bf16[40,2048]{1,0:T(8,128)(2,1)S(1)}, u32[]{:S(2)}, u32[]{:S(2)}) collective-permute-start(bf16[40,2048]{1,0:T(8,128)(2,1)S(1)} %get-tuple-element.42), channel_id=1, source_target_pairs={{0,3},{1,2},{2,1},{3,0},{4,7},{5,6},{6,5},{7,4},{8,11},{9,10},{10,... | collective-permute-start | bytes 491528 | tf_op jit(solution)/shard_map/ppermute | solution.py:49
  112.5 9.5 %collective-permute-start.25 = (bf16[40,1024]{1,0:T(8,128)(2,1)S(1)}, bf16[40,1024]{1,0:T(8,128)(2,1)S(1)}, u32[]{:S(2)}, u32[]{:S(2)}) collective-permute-start(bf16[40,1024]{1,0:T(8,128)(2,1)S(1)} %get-tuple-element.49), channel_id=1, source_target_pairs={{0,6},{1,7},{2,4},{3,5},{4,2},{5,3},{6,0},{7,1},{8,14},{9,15},{10,... | collective-permute-start | bytes 245768 | tf_op jit(solution)/shard_map/ppermute | solution.py:49
  116.9 6.5 %collective-permute-start.26 = (bf16[40,1024]{1,0:T(8,128)(2,1)S(1)}, bf16[40,1024]{1,0:T(8,128)(2,1)S(1)}, u32[]{:S(2)}, u32[]{:S(2)}) collective-permute-start(bf16[40,1024]{1,0:T(8,128)(2,1)S(1)} %get-tuple-element.50), channel_id=1, source_target_pairs={{0,7},{1,6},{2,5},{3,4},{4,3},{5,2},{6,1},{7,0},{8,15},{9,14},{10,... | collective-permute-start | bytes 245768 | tf_op jit(solution)/shard_map/ppermute | solution.py:49

commit v4 on v3

--- a/solution.py
+++ b/solution.py
@@ -1,4 +1,5 @@
 import functools
+import math
 
 import jax
 import jax.numpy as jnp
@@ -12,7 +13,6 @@
 AXES = ("dp", "expert")
 VMEM_LIMIT = 8 << 20
 BOTH_LAST = (((1,), (1,)), ((), ()))
-BOTH_FIRST = (((0,), (0,)), ((), ()))
 
 
 def few(n):
@@ -106,21 +106,24 @@
     return kernel_call(body, shape, (rows, gate_t, up_t), 4 * rows.size * units)
 
 
-def down(hidden, down_t, hidden2, down2_t, dtype, start=0):
+def down(hidden, down_t, hidden2, down2_t, dtype, start=0, parts=1):
     width = sum(piece.shape[1] for piece in down2_t)
-    step = min(down2_t[0].shape[1], 512)
+    step = math.gcd(*(piece.shape[1] for piece in down2_t), 512)
 
     def body(h_ref, w_ref, h2_ref, *refs):
         at = 0
-        for ref in refs[:-1]:
+        for ref in refs[:-parts]:
             for here in range(0, ref.shape[1], step):
                 columns = slice(start + at, start + at + step)
                 part = dot(h_ref[...], w_ref[:, columns]) + dot(h2_ref[...], ref[:, here : here + step])
-                refs[-1][:, at : at + step] = part.astype(dtype)
+                for i, out_ref in enumerate(refs[-parts:]):
+                    out_ref[:, at : at + step] = part[i * rows : (i + 1) * rows, :].astype(dtype)
                 at += step
 
-    shape = jax.ShapeDtypeStruct((hidden.shape[0], width), dtype)
-    return kernel_call(body, shape, (hidden, down_t, hidden2, *down2_t), 4 * hidden.size * width)
+    rows = hidden.shape[0] // parts
+    shape = jax.ShapeDtypeStruct((rows, width), dtype)
+    shapes = shape if parts == 1 else [shape] * parts
+    return kernel_call(body, shapes, (hidden, down_t, hidden2, *down2_t), 4 * hidden.size * width)
 
 
 def add_and_split(own, returned, count):
@@ -190,16 +193,14 @@
     return [blocks[0][k] for k in range(n)] if len(blocks) < n else blocks, counts
 
 
-def mix(ids, units, capacity, others, here, back, corners, most):
-    n, tok_rows, width = capacity.shape[1], ids.shape[1], sum(b.shape[0] * b.shape[1] for b in back)
-    width = width // (n * most)
+def mix_weights(ids, units, capacity, others, here, most):
+    n, tok_rows = capacity.shape[1], ids.shape[1]
 
     def body(here_ref, ids_ref, units_ref, capacity_ref, *refs):
-        other_refs, back_refs = refs[: len(others)], refs[len(others) : -2]
-        out_ref, joined = refs[-2:]
+        out_ref = refs[-1]
         me = here_ref[0, 0]
         room = capacity_ref[...]
-        for i, ref in enumerate(other_refs):
+        for i, ref in enumerate(refs[:-1]):
             room = room - ref[...] * ((me >> i) & 1)
         place = lax.broadcasted_iota(jnp.int32, (n, n), 0)
         expert = lax.broadcasted_iota(jnp.int32, (n, n), 1)
@@ -211,28 +212,46 @@
         low = (unit & 7).astype(F32) * (1.0 / 1024.0)
         slot = jnp.where(once, earlier, -1.0)
         row = lax.broadcasted_iota(jnp.int32, (most, tok_rows), 0).astype(F32)
-
-        def spread(values):
+        for i, values in enumerate((high, low)):
             parts = [jnp.where(row == slot[k : k + 1, :], values[k : k + 1, :], 0.0) for k in range(n)]
-            return jnp.concatenate(parts, axis=0).astype(BF16)
-
-        for at, ref in zip(corners, back_refs):
-            joined[at[0] : at[0] + ref.shape[0], at[1] : at[1] + ref.shape[1]] = ref[...]
-        mixed = lax.dot_general(spread(high), joined[...], BOTH_FIRST, preferred_element_type=F32)
-        mixed += lax.dot_general(spread(low), joined[...], BOTH_FIRST, preferred_element_type=F32)
-        out_ref[...] = mixed.astype(BF16)
-
-    operands = (here, ids, units, capacity, *others, *back)
+            spread = jnp.concatenate(parts, axis=0)
+            out_ref[i * tok_rows : (i + 1) * tok_rows, :] = spread.T.astype(BF16)
+
+    operands = (here, ids, units, capacity, *others)
     memory = [pltpu.SMEM] + [pltpu.VMEM] * (len(operands) - 1)
     return pl.pallas_call(
         body,
-        out_shape=jax.ShapeDtypeStruct((tok_rows, width), BF16),
+        out_shape=jax.ShapeDtypeStruct((2 * tok_rows, n * most), BF16),
         in_specs=[pl.BlockSpec(memory_space=m) for m in memory],
         out_specs=pl.BlockSpec(memory_space=pltpu.VMEM),
-        scratch_shapes=[pltpu.VMEM((n * most, width), BF16)],
+        compiler_params=pltpu.CompilerParams(vmem_limit_bytes=VMEM_LIMIT),
+        name="mix_weights",
+    )(*operands)
+
+
+def mix(weights, back, corners):
+    tok_rows, choices = weights.shape[0] // 2, weights.shape[1]
+    width = sum(b.size for b in back) // choices
+
+    def body(weights_ref, *refs):
+        out_ref, joined = refs[-2:]
+        for at, ref in zip(corners, refs[:-2]):
+            joined[at[0] : at[0] + ref.shape[0], at[1] : at[1] + ref.shape[1]] = ref[...]
+        step = math.gcd(width, 256)
+        for column in range(0, width, step):
+            here = slice(column, column + step)
+            both = dot(weights_ref[...], joined[:, here])
+            out_ref[:, here] = (both[:tok_rows, :] + both[tok_rows:, :]).astype(BF16)
+
+    return pl.pallas_call(
+        body,
+        out_shape=jax.ShapeDtypeStruct((tok_rows, width), BF16),
+        in_specs=[pl.BlockSpec(memory_space=pltpu.VMEM)] * (1 + len(back)),
+        out_specs=pl.BlockSpec(memory_space=pltpu.VMEM),
+        scratch_shapes=[pltpu.VMEM((choices, width), BF16)],
         compiler_params=pltpu.CompilerParams(vmem_limit_bytes=VMEM_LIMIT),
         name="mix",
-    )(*operands)
+    )(weights, *back)
 
 
 def layer(tokens, expert_ids, gate_units, capacity, w_gate, w_up, w_down):
@@ -246,7 +265,7 @@
     here, wg, wu, wd = lax.optimization_barrier((here, wg, wu, wd))
     wg2 = pair_permute(wg, n_dp, n_exp, True)
     wu2 = pair_permute(wu, n_dp, n_exp, True)
-    half = width // 2
+    half = width * 3 // 8
     wd2_a = pair_permute(wd[:, :half], n_dp, n_exp, True)
     wd2_b = pair_permute(wd[:, half:], n_dp, n_exp, True)
 
@@ -261,8 +280,8 @@
     def hidden_pair(rows):
         return hidden_of(rows, wg, wu), hidden_of(rows, wg2, wu2)
 
-    def partial(pair, w2, dtype, start=0):
-        return down(pair[0], wd, pair[1], w2, dtype, start)
+    def partial(pair, w2, dtype, start=0, parts=1):
+        return down(pair[0], wd, pair[1], w2, dtype, start, parts)
 
     h_own_near = hidden_pair(own_near)
     h_own_far = hidden_pair(own_far)
@@ -272,11 +291,13 @@
     far_b = pair_permute(partial(h_far, [wd2_b], BF16, half), n_dp, n_exp, False)
     own_far_a = partial(h_own_far, [wd2_a], F32)
     own_far_b = partial(h_own_far, [wd2_b], F32, half)
-    near_part = pair_permute(partial(h_near, [wd2_a, wd2_b], BF16), n_dp, n_exp, False)
-    own_near_part = partial(h_own_near, [wd2_a, wd2_b], F32)
+    near_part = partial(h_near, [wd2_a, wd2_b], BF16, parts=2)
+    near_part = [pair_permute(p, n_dp, n_exp, False) for p in near_part]
+    own_near_part = partial(h_own_near, [wd2_a, wd2_b], F32, parts=2)
     answer_a = add_and_split(own_far_a, far_a, len(far))
     answer_b = add_and_split(own_far_b, far_b, len(far))
-    answer_near = add_and_split(own_near_part, near_part, len(near))
+    answer_near = add_and_split(own_near_part[0], near_part[0], len(near) // 2)
+    answer_near += add_and_split(own_near_part[1], near_part[1], len(near) // 2)
     if few(n_experts):
         back = expert_send(answer_near, near)
         back += expert_send(answer_a, far) + expert_send(answer_b, far)
@@ -289,7 +310,8 @@
     corners = [(0, 0)]
     if few(n_experts):
         corners = [(k * most, 0) for k in near + far] + [(k * most, half) for k in far]
-    return mix(ids, gate_units.T, capacity[None, :], others, here, back, corners, most)
+    weights = mix_weights(ids, gate_units.T, capacity[None, :], others, here, most)
+    return mix(weights, back, corners)
 
 
 def solution(mesh):

time: 125 us -> 135 us (1.080); the launches traced: 125 us -> 133 us
  waiting for transfers between devices: 59.9 us -> 68.2 us
    ppermute x18, waiting for transfers between devices: 30.3 us -> 39.7 us  [expert_send(): block = lax.ppermute(block, 'expert', [(i, i ^ k) for i in range(n)])]
    ppermute x9 -> x10, starting transfers between devices: 13.5 us -> 11.2 us  [pair_permute(): return lax.ppermute(values, AXES, pairs)]
    ppermute x18, starting transfers between devices: 28.5 us -> 30.2 us  [expert_send(): block = lax.ppermute(block, 'expert', [(i, i ^ k) for i in range(n)])]
    ppermute x5, waiting for transfers between devices: 10.3 us -> 8.82 us  [exchanged_counts(): others.append(lax.ppermute(total, AXES, [(i, i ^ step) for i in range(n)]))]
    ppermute x9 -> x10, waiting for transfers between devices: 19.2 us -> 19.7 us  [pair_permute(): return lax.ppermute(values, AXES, pairs)]
    pallas_call x19 -> x20, Pallas kernels: 12.7 us -> 12.7 us  [kernel_call(): pl.pallas_call(body, out_shape=shapes if single else tuple(shapes), in_sp...]
  transfers between devices with their start and end apart: 32 -> 33, of which waited for: 14 -> 15; matrix products, arithmetic and copies ran while one was open for 0% -> 0% of each run, Pallas kernels for 11% -> 9%
where the time goes in v4:
time: 135 us; the launch traced here: 133 us
  waiting for transfers between devices  68.2 us (51%)
  starting transfers between devices  46.9 us (35%)
  Pallas kernels  15.3 us (11%)
  local copies, waits for them, and re-layouts  1.98 us (1%)
    ppermute x18, waiting for transfers between devices, expert_send(): block = lax.ppermute(block, 'expert', [(i, i ^ k) for i in range(n)])  39.7 us
    ppermute x18, starting transfers between devices, expert_send(): block = lax.ppermute(block, 'expert', [(i, i ^ k) for i in range(n)])  30.2 us
    ppermute x10, waiting for transfers between devices, pair_permute(): return lax.ppermute(values, AXES, pairs)  19.7 us
    pallas_call x20, Pallas kernels, kernel_call(): pl.pallas_call(body, out_shape=shapes if single else tuple(shapes), in_sp...  12.7 us
    ppermute x10, starting transfers between devices, pair_permute(): return lax.ppermute(values, AXES, pairs)  11.2 us
    ppermute x5, waiting for transfers between devices, exchanged_counts(): others.append(lax.ppermute(total, AXES, [(i, i ^ step) for i in range(n)]))  8.82 us
    ppermute x5, starting transfers between devices, exchanged_counts(): others.append(lax.ppermute(total, AXES, [(i, i ^ step) for i in range(n)]))  5.48 us
  transfers between devices with their start and end apart: 33, of which 15 were waited for; matrix products, arithmetic and copies ran while one was open for 0% of the time, Pallas kernels for 9%

profile of v4, /device:TPU:0, one launch (start us, length us, event | category | flops | bytes accessed | tf_op | source)
XLA Modules:
  0.0 132.6 jit_solution(5980557402109699728)
XLA Ops:
  0.0 1.2 copy-done.3
  1.8 0.8 dispatch.1
  2.7 4.1 %collective-permute-start.18 = (bf16[40,2048]{1,0:T(8,128)(2,1)S(1)}, bf16[40,2048]{1,0:T(8,128)(2,1)S(1)}, u32[]{:S(2)}, u32[]{:S(2)}) collective-permute-start(bf16[40,2048]{1,0:T(8,128)(2,1)S(1)} %get-tuple-element.51), channel_id=1, source_target_pairs={{0,4},{1,5},{2,6},{3,7},{4,0},{5,1},{6,2},{7,3},{8,12},{9,13},{10,... | collective-permute-start | bytes 491528 | tf_op jit(solution)/shard_map/ppermute | solution.py:49
  6.8 1.5 %collective-permute-start.8 = (bf16[352,2048]{1,0:T(8,128)(2,1)}, bf16[352,2048]{1,0:T(8,128)(2,1)S(1)}, u32[]{:S(2)}, u32[]{:S(2)}) collective-permute-start(bf16[352,2048]{1,0:T(8,128)(2,1)} %bitcast.21), channel_id=1, source_target_pairs={{0,16},{1,9},{2,18},{3,11},{4,20},{5,13},{6,22},{7,15},{8,24},{9,1... | collective-permute-start | bytes 4325384 | tf_op jit(solution)/shard_map/ppermute | solution.py:33
  8.8 2.5 %collective-permute-start.20 = (bf16[40,2048]{1,0:T(8,128)(2,1)S(1)}, bf16[40,2048]{1,0:T(8,128)(2,1)S(1)}, u32[]{:S(2)}, u32[]{:S(2)}) collective-permute-start(bf16[40,2048]{1,0:T(8,128)(2,1)S(1)} %get-tuple-element.53), channel_id=1, source_target_pairs={{0,6},{1,7},{2,4},{3,5},{4,2},{5,3},{6,0},{7,1},{8,14},{9,15},{10,... | collective-permute-start | bytes 491528 | tf_op jit(solution)/shard_map/ppermute | solution.py:49
  11.3 11.0 %collective-permute-done.18.refs_0_ = bf16[40,2048]{1,0:T(8,128)(2,1)S(1)} collective-permute-done((bf16[40,2048]{1,0:T(8,128)(2,1)S(1)}, bf16[40,2048]{1,0:T(8,128)(2,1)S(1)}, u32[]{:S(2)}, u32[]{:S(2)}) %collective-permute-start.18) | collective-permute-done | bytes 163872 | tf_op jit(solution)/shard_map/ppermute | solution.py:49
  22.4 2.3 %collective-permute-start.21 = (bf16[40,2048]{1,0:T(8,128)(2,1)S(1)}, bf16[40,2048]{1,0:T(8,128)(2,1)S(1)}, u32[]{:S(2)}, u32[]{:S(2)}) collective-permute-start(bf16[40,2048]{1,0:T(8,128)(2,1)S(1)} %get-tuple-element.54), channel_id=1, source_target_pairs={{0,7},{1,6},{2,5},{3,4},{4,3},{5,2},{6,1},{7,0},{8,15},{9,14},{10,... | collective-permute-start | bytes 491528 | tf_op jit(solution)/shard_map/ppermute | solution.py:49
  24.7 5.6 %collective-permute-done.21.refs_3_ = bf16[40,2048]{1,0:T(8,128)(2,1)S(1)} collective-permute-done((bf16[40,2048]{1,0:T(8,128)(2,1)S(1)}, bf16[40,2048]{1,0:T(8,128)(2,1)S(1)}, u32[]{:S(2)}, u32[]{:S(2)}) %collective-permute-start.21) | collective-permute-done | bytes 163872 | tf_op jit(solution)/shard_map/ppermute | solution.py:49
  30.3 1.6 %collective-permute-start.22 = (bf16[160,2048]{1,0:T(8,128)(2,1)S(1)}, bf16[160,2048]{1,0:T(8,128)(2,1)S(1)}, u32[]{:S(2)}, u32[]{:S(2)}) collective-permute-start(bf16[160,2048]{1,0:T(8,128)(2,1)S(1)} %shard_map.82.rows_ref), channel_id=1, source_target_pairs={{0,8},{1,17},{2,10},{3,19},{4,12},{5,21},{6,14},{7,23},{8,0},{9,25... | collective-permute-start | bytes 1966088 | tf_op jit(solution)/shard_map/ppermute | solution.py:33
  31.9 6.0 %collective-permute-start.6 = (bf16[40,2048]{1,0:T(8,128)(2,1)S(1)}, bf16[40,2048]{1,0:T(8,128)(2,1)S(1)}, u32[]{:S(2)}, u32[]{:S(2)}) collective-permute-start(bf16[40,2048]{1,0:T(8,128)(2,1)S(1)} %get-tuple-element.38), channel_id=1, source_target_pairs={{0,2},{1,3},{2,0},{3,1},{4,6},{5,7},{6,4},{7,5},{8,10},{9,11},{10,... | collective-permute-start | bytes 491528 | tf_op jit(solution)/shard_map/ppermute | solution.py:49
  37.9 1.1 collective-permute-start.7
  39.1 3.8 %collective-permute-done.6.refs_2_ = bf16[40,2048]{1,0:T(8,128)(2,1)S(1)} collective-permute-done((bf16[40,2048]{1,0:T(8,128)(2,1)S(1)}, bf16[40,2048]{1,0:T(8,128)(2,1)S(1)}, u32[]{:S(2)}, u32[]{:S(2)}) %collective-permute-start.6) | collective-permute-done | bytes 163872 | tf_op jit(solution)/shard_map/ppermute | solution.py:49
  42.9 1.5 %collective-permute-start.11 = (bf16[352,1280]{1,0:T(8,128)(2,1)S(1)}, bf16[352,1280]{1,0:T(8,128)(2,1)S(1)}, u32[]{:S(2)}, u32[]{:S(2)}) collective-permute-start(bf16[352,1280]{1,0:T(8,128)(2,1)S(1)} %slice.9), channel_id=1, source_target_pairs={{0,16},{1,9},{2,18},{3,11},{4,20},{5,13},{6,22},{7,15},{8,24},{9,1... | collective-permute-start | bytes 2703368 | tf_op jit(solution)/shard_map/ppermute | solution.py:33
  44.5 1.6 %collective-permute-done.7.refs_3_ = bf16[40,2048]{1,0:T(8,128)(2,1)S(1)} collective-permute-done((bf16[40,2048]{1,0:T(8,128)(2,1)S(1)}, bf16[40,2048]{1,0:T(8,128)(2,1)S(1)}, u32[]{:S(2)}, u32[]{:S(2)}) %collective-permute-start.7) | collective-permute-done | bytes 163872 | tf_op jit(solution)/shard_map/ppermute | solution.py:49
  46.5 1.5 %collective-permute-done.22.rows_ref = bf16[160,2048]{1,0:T(8,128)(2,1)S(1)} collective-permute-done((bf16[160,2048]{1,0:T(8,128)(2,1)S(1)}, bf16[160,2048]{1,0:T(8,128)(2,1)S(1)}, u32[]{:S(2)}, u32[]{:S(2)}) %collective-permute-start.22) | collective-permute-done | bytes 655392 | tf_op jit(solution)/shard_map/ppermute | solution.py:33
  48.0 1.5 %collective-permute-start.10 = (bf16[352,768]{1,0:T(8,128)(2,1)S(1)}, bf16[352,768]{1,0:T(8,128)(2,1)S(1)}, u32[]{:S(2)}, u32[]{:S(2)}) collective-permute-start(bf16[352,768]{1,0:T(8,128)(2,1)S(1)} %slice.8), channel_id=1, source_target_pairs={{0,16},{1,9},{2,18},{3,11},{4,20},{5,13},{6,22},{7,15},{8,24},{9,1... | collective-permute-start | bytes 1622024 | tf_op jit(solution)/shard_map/ppermute | solution.py:33
  49.5 1.1 shard_map.86.h_ref
  50.6 13.2 %collective-permute-done.12.rows_ref = bf16[160,2048]{1,0:T(8,128)(2,1)S(1)} collective-permute-done((bf16[160,2048]{1,0:T(8,128)(2,1)S(1)}, bf16[160,2048]{1,0:T(8,128)(2,1)S(1)}, u32[]{:S(2)}, u32[]{:S(2)}) %collective-permute-start.12) | collective-permute-done | bytes 655392 | tf_op jit(solution)/shard_map/ppermute | solution.py:33
  63.8 1.1 shard_map.77.h_ref
  64.9 1.1 shard_map.78.h2_ref
  66.0 4.9 %collective-permute-done.10.refs_0_ = bf16[352,768]{1,0:T(8,128)(2,1)S(1)} collective-permute-done((bf16[352,768]{1,0:T(8,128)(2,1)S(1)}, bf16[352,768]{1,0:T(8,128)(2,1)S(1)}, u32[]{:S(2)}, u32[]{:S(2)}) %collective-permute-start.10) | collective-permute-done | bytes 540704 | tf_op jit(solution)/shard_map/ppermute | solution.py:33
  71.0 0.8 shard_map.79
  71.8 1.6 %collective-permute-start.15 = (bf16[80,2048]{1,0:T(8,128)(2,1)S(1)}, bf16[80,2048]{1,0:T(8,128)(2,1)S(1)}, u32[]{:S(2)}, u32[]{:S(2)}) collective-permute-start(bf16[80,2048]{1,0:T(8,128)(2,1)S(1)} %get-tuple-element.48), channel_id=1, source_target_pairs={{0,8},{1,17},{2,10},{3,19},{4,12},{5,21},{6,14},{7,23},{8,0},{9,25... | collective-permute-start | bytes 983048 | tf_op jit(solution)/shard_map/ppermute | solution.py:33
  73.4 1.1 shard_map.87.h2_ref
  76.0 1.6 %collective-permute-start.23 = (bf16[160,768]{1,0:T(8,128)(2,1)S(1)}, bf16[160,768]{1,0:T(8,128)(2,1)S(1)}, u32[]{:S(2)}, u32[]{:S(2)}) collective-permute-start(bf16[160,768]{1,0:T(8,128)(2,1)S(1)} %shard_map.88), channel_id=1, source_target_pairs={{0,8},{1,17},{2,10},{3,19},{4,12},{5,21},{6,14},{7,23},{8,0},{9,25... | collective-permute-start | bytes 737288 | tf_op jit(solution)/shard_map/ppermute | solution.py:33
  77.6 1.2 collective-permute-done.refs_0_
  78.8 1.6 %collective-permute-start.1 = (s32[1,8]{1,0:T(1,128)S(1)}, s32[1,8]{1,0:T(1,128)S(1)}, u32[]{:S(2)}, u32[]{:S(2)}) collective-permute-start(s32[1,8]{1,0:T(1,128)S(1)} %add.16), channel_id=1, source_target_pairs={{0,2},{1,3},{2,0},{3,1},{4,6},{5,7},{6,4},{7,5},{8,10},{9,11},{10,... | collective-permute-start | bytes 104 | tf_op jit(solution)/shard_map/ppermute | solution.py:61
  80.3 2.0 %collective-permute-done.1.refs_1_ = s32[1,8]{1,0:T(1,128)S(1)} collective-permute-done((s32[1,8]{1,0:T(1,128)S(1)}, s32[1,8]{1,0:T(1,128)S(1)}, u32[]{:S(2)}, u32[]{:S(2)}) %collective-permute-start.1) | collective-permute-done | bytes 64 | tf_op jit(solution)/shard_map/ppermute | solution.py:61
  82.3 1.8 %collective-permute-start.2 = (s32[1,8]{1,0:T(1,128)S(1)}, s32[1,8]{1,0:T(1,128)S(1)}, u32[]{:S(2)}, u32[]{:S(2)}) collective-permute-start(s32[1,8]{1,0:T(1,128)S(1)} %add.17), channel_id=1, source_target_pairs={{0,4},{1,5},{2,6},{3,7},{4,0},{5,1},{6,2},{7,3},{8,12},{9,13},{10,... | collective-permute-start | bytes 104 | tf_op jit(solution)/shard_map/ppermute | solution.py:61
  84.2 2.6 %collective-permute-done.2.refs_2_ = s32[1,8]{1,0:T(1,128)S(1)} collective-permute-done((s32[1,8]{1,0:T(1,128)S(1)}, s32[1,8]{1,0:T(1,128)S(1)}, u32[]{:S(2)}, u32[]{:S(2)}) %collective-permute-start.2) | collective-permute-done | bytes 64 | tf_op jit(solution)/shard_map/ppermute | solution.py:61
  87.4 3.0 %collective-permute-done.3.refs_3_ = s32[1,8]{1,0:T(1,128)S(1)} collective-permute-done((s32[1,8]{1,0:T(1,128)S(1)}, s32[1,8]{1,0:T(1,128)S(1)}, u32[]{:S(2)}, u32[]{:S(2)}) %collective-permute-start.3) | collective-permute-done | bytes 64 | tf_op jit(solution)/shard_map/ppermute | solution.py:61
  90.4 1.5 %collective-permute-start.4 = (s32[1,8]{1,0:T(1,128)S(1)}, s32[1,8]{1,0:T(1,128)S(1)}, u32[]{:S(2)}, u32[]{:S(2)}) collective-permute-start(s32[1,8]{1,0:T(1,128)S(1)} %add.19), channel_id=1, source_target_pairs={{0,16},{1,17},{2,18},{3,19},{4,20},{5,21},{6,22},{7,23},{8,24},{9,... | collective-permute-start | bytes 104 | tf_op jit(solution)/shard_map/ppermute | solution.py:61
  92.4 1.1 shard_map.83.h_ref
  93.5 1.1 shard_map.74.h_ref
  94.6 1.1 shard_map.84.h2_ref
  96.1 1.1 shard_map.75.h2_ref
  97.3 1.9 %collective-permute-start.24 = (bf16[40,768]{1,0:T(8,128)(2,1)S(1)}, bf16[40,768]{1,0:T(8,128)(2,1)S(1)}, u32[]{:S(2)}, u32[]{:S(2)}) collective-permute-start(bf16[40,768]{1,0:T(8,128)(2,1)S(1)} %get-tuple-element.55), channel_id=1, source_target_pairs={{0,4},{1,5},{2,6},{3,7},{4,0},{5,1},{6,2},{7,3},{8,12},{9,13},{10,... | collective-permute-start | bytes 184328 | tf_op jit(solution)/shard_map/ppermute | solution.py:49
  99.2 0.8 shard_map.76
  100.3 2.2 %collective-permute-done.24.refs_4_ = bf16[40,768]{1,0:T(8,128)(2,1)S(1)} collective-permute-done((bf16[40,768]{1,0:T(8,128)(2,1)S(1)}, bf16[40,768]{1,0:T(8,128)(2,1)S(1)}, u32[]{:S(2)}, u32[]{:S(2)}) %collective-permute-start.24) | collective-permute-done | bytes 61472 | tf_op jit(solution)/shard_map/ppermute | solution.py:49
  103.0 4.9 %collective-permute-done.25.refs_5_ = bf16[40,768]{1,0:T(8,128)(2,1)S(1)} collective-permute-done((bf16[40,768]{1,0:T(8,128)(2,1)S(1)}, bf16[40,768]{1,0:T(8,128)(2,1)S(1)}, u32[]{:S(2)}, u32[]{:S(2)}) %collective-permute-start.25) | collective-permute-done | bytes 61472 | tf_op jit(solution)/shard_map/ppermute | solution.py:49
  107.9 2.5 %collective-permute-start.26 = (bf16[40,768]{1,0:T(8,128)(2,1)S(1)}, bf16[40,768]{1,0:T(8,128)(2,1)S(1)}, u32[]{:S(2)}, u32[]{:S(2)}) collective-permute-start(bf16[40,768]{1,0:T(8,128)(2,1)S(1)} %get-tuple-element.57), channel_id=1, source_target_pairs={{0,6},{1,7},{2,4},{3,5},{4,2},{5,3},{6,0},{7,1},{8,14},{9,15},{10,... | collective-permute-start | bytes 184328 | tf_op jit(solution)/shard_map/ppermute | solution.py:49
  111.0 1.0 collective-permute-start.14
  112.7 1.3 collective-permute-done.26.refs_6_
  114.0 3.4 %collective-permute-start.29 = (bf16[40,1280]{1,0:T(8,128)(2,1)S(1)}, bf16[40,1280]{1,0:T(8,128)(2,1)S(1)}, u32[]{:S(2)}, u32[]{:S(2)}) collective-permute-start(bf16[40,1280]{1,0:T(8,128)(2,1)S(1)} %get-tuple-element.59), channel_id=1, source_target_pairs={{0,4},{1,5},{2,6},{3,7},{4,0},{5,1},{6,2},{7,3},{8,12},{9,13},{10,... | collective-permute-start | bytes 307208 | tf_op jit(solution)/shard_map/ppermute | solution.py:49
  118.0 2.4 %collective-permute-start.31 = (bf16[40,1280]{1,0:T(8,128)(2,1)S(1)}, bf16[40,1280]{1,0:T(8,128)(2,1)S(1)}, u32[]{:S(2)}, u32[]{:S(2)}) collective-permute-start(bf16[40,1280]{1,0:T(8,128)(2,1)S(1)} %get-tuple-element.61), channel_id=1, source_target_pairs={{0,6},{1,7},{2,4},{3,5},{4,2},{5,3},{6,0},{7,1},{8,14},{9,15},{10,... | collective-permute-start | bytes 307208 | tf_op jit(solution)/shard_map/ppermute | solution.py:49
  120.4 1.1 collective-permute-start.32
  121.8 9.3 %collective-permute-done.30.refs_9_ = bf16[40,1280]{1,0:T(8,128)(2,1)S(1)} collective-permute-done((bf16[40,1280]{1,0:T(8,128)(2,1)S(1)}, bf16[40,1280]{1,0:T(8,128)(2,1)S(1)}, u32[]{:S(2)}, u32[]{:S(2)}) %collective-permute-start.30) | collective-permute-done | bytes 102432 | tf_op jit(solution)/shard_map/ppermute | solution.py:49
  131.1 1.5 %mix.1 = bf16[128,2048]{1,0:T(8,128)(2,1)} custom-call(bf16[256,320]{1,0:T(8,128)(2,1)S(1)} %mix_weights.1.weights_ref, bf16[40,2048]{1,0:T(8,128)(2,1)S(1)} %get-tuple-element.45.refs_0_, bf16[40,2048]{1,0:T(8,128)(2,1)S(1)} %collective-permute-done.14.refs_1_, bf16[40,2048]{1,0:T(8,128)(2,1)S(1)} %collective-permute-done.16.refs_2_, ...), custom_call_target="tpu_custom_call" | custom-call | tf_op jit(solution)/shard_map/mix/pallas_call | solution.py:246
  (63 shorter events, 7.7 us)
Async XLA Ops:
  0.0 39.0 %copy-start = (bf16[1,2048,352]{1,2,0:T(8,128)(2,1)S(1)}, bf16[1,2048,352]{1,2,0:T(8,128)(2,1)}, u32[]{:S(2)}) copy-start(bf16[1,2048,352]{1,2,0:T(8,128)(2,1)} %param.13) | copy-start | bytes 4325380
  0.0 1.2 copy-start.3
  1.2 0.7 copy-start.4
  2.7 19.7 %collective-permute-start.18 = (bf16[40,2048]{1,0:T(8,128)(2,1)S(1)}, bf16[40,2048]{1,0:T(8,128)(2,1)S(1)}, u32[]{:S(2)}, u32[]{:S(2)}) collective-permute-start(bf16[40,2048]{1,0:T(8,128)(2,1)S(1)} %get-tuple-element.51), channel_id=1, source_target_pairs={{0,4},{1,5},{2,6},{3,7},{4,0},{5,1},{6,2},{7,3},{8,12},{9,13},{10,... | collective-permute-start | bytes 491528 | tf_op jit(solution)/shard_map/ppermute | solution.py:49
  6.8 58.1 %collective-permute-start.8 = (bf16[352,2048]{1,0:T(8,128)(2,1)}, bf16[352,2048]{1,0:T(8,128)(2,1)S(1)}, u32[]{:S(2)}, u32[]{:S(2)}) collective-permute-start(bf16[352,2048]{1,0:T(8,128)(2,1)} %bitcast.21), channel_id=1, source_target_pairs={{0,16},{1,9},{2,18},{3,11},{4,20},{5,13},{6,22},{7,15},{8,24},{9,1... | collective-permute-start | bytes 4325384 | tf_op jit(solution)/shard_map/ppermute | solution.py:33
  8.3 56.6 %collective-permute-start.9 = (bf16[352,2048]{1,0:T(8,128)(2,1)}, bf16[352,2048]{1,0:T(8,128)(2,1)S(1)}, u32[]{:S(2)}, u32[]{:S(2)}) collective-permute-start(bf16[352,2048]{1,0:T(8,128)(2,1)} %bitcast.26), channel_id=1, source_target_pairs={{0,16},{1,9},{2,18},{3,11},{4,20},{5,13},{6,22},{7,15},{8,24},{9,1... | collective-permute-start | bytes 4325384 | tf_op jit(solution)/shard_map/ppermute | solution.py:33
  8.8 15.9 %collective-permute-start.19 = (bf16[40,2048]{1,0:T(8,128)(2,1)S(1)}, bf16[40,2048]{1,0:T(8,128)(2,1)S(1)}, u32[]{:S(2)}, u32[]{:S(2)}) collective-permute-start(bf16[40,2048]{1,0:T(8,128)(2,1)S(1)} %get-tuple-element.52), channel_id=1, source_target_pairs={{0,5},{1,4},{2,7},{3,6},{4,1},{5,0},{6,3},{7,2},{8,13},{9,12},{10,... | collective-permute-start | bytes 491528 | tf_op jit(solution)/shard_map/ppermute | solution.py:49
  8.8 15.9 %collective-permute-start.20 = (bf16[40,2048]{1,0:T(8,128)(2,1)S(1)}, bf16[40,2048]{1,0:T(8,128)(2,1)S(1)}, u32[]{:S(2)}, u32[]{:S(2)}) collective-permute-start(bf16[40,2048]{1,0:T(8,128)(2,1)S(1)} %get-tuple-element.53), channel_id=1, source_target_pairs={{0,6},{1,7},{2,4},{3,5},{4,2},{5,3},{6,0},{7,1},{8,14},{9,15},{10,... | collective-permute-start | bytes 491528 | tf_op jit(solution)/shard_map/ppermute | solution.py:49
  22.4 7.9 %collective-permute-start.21 = (bf16[40,2048]{1,0:T(8,128)(2,1)S(1)}, bf16[40,2048]{1,0:T(8,128)(2,1)S(1)}, u32[]{:S(2)}, u32[]{:S(2)}) collective-permute-start(bf16[40,2048]{1,0:T(8,128)(2,1)S(1)} %get-tuple-element.54), channel_id=1, source_target_pairs={{0,7},{1,6},{2,5},{3,4},{4,3},{5,2},{6,1},{7,0},{8,15},{9,14},{10,... | collective-permute-start | bytes 491528 | tf_op jit(solution)/shard_map/ppermute | solution.py:49
  30.3 17.7 %collective-permute-start.22 = (bf16[160,2048]{1,0:T(8,128)(2,1)S(1)}, bf16[160,2048]{1,0:T(8,128)(2,1)S(1)}, u32[]{:S(2)}, u32[]{:S(2)}) collective-permute-start(bf16[160,2048]{1,0:T(8,128)(2,1)S(1)} %shard_map.82.rows_ref), channel_id=1, source_target_pairs={{0,8},{1,17},{2,10},{3,19},{4,12},{5,21},{6,14},{7,23},{8,0},{9,25... | collective-permute-start | bytes 1966088 | tf_op jit(solution)/shard_map/ppermute | solution.py:33
  31.9 6.0 %collective-permute-start.5 = (bf16[40,2048]{1,0:T(8,128)(2,1)S(1)}, bf16[40,2048]{1,0:T(8,128)(2,1)S(1)}, u32[]{:S(2)}, u32[]{:S(2)}) collective-permute-start(bf16[40,2048]{1,0:T(8,128)(2,1)S(1)} %get-tuple-element.37), channel_id=1, source_target_pairs={{0,1},{1,0},{2,3},{3,2},{4,5},{5,4},{6,7},{7,6},{8,9},{9,8},{10,11... | collective-permute-start | bytes 491528 | tf_op jit(solution)/shard_map/ppermute | solution.py:49
  31.9 11.0 %collective-permute-start.6 = (bf16[40,2048]{1,0:T(8,128)(2,1)S(1)}, bf16[40,2048]{1,0:T(8,128)(2,1)S(1)}, u32[]{:S(2)}, u32[]{:S(2)}) collective-permute-start(bf16[40,2048]{1,0:T(8,128)(2,1)S(1)} %get-tuple-element.38), channel_id=1, source_target_pairs={{0,2},{1,3},{2,0},{3,1},{4,6},{5,7},{6,4},{7,5},{8,10},{9,11},{10,... | collective-permute-start | bytes 491528 | tf_op jit(solution)/shard_map/ppermute | solution.py:49
  37.9 8.2 %collective-permute-start.7 = (bf16[40,2048]{1,0:T(8,128)(2,1)S(1)}, bf16[40,2048]{1,0:T(8,128)(2,1)S(1)}, u32[]{:S(2)}, u32[]{:S(2)}) collective-permute-start(bf16[40,2048]{1,0:T(8,128)(2,1)S(1)} %get-tuple-element.39), channel_id=1, source_target_pairs={{0,3},{1,2},{2,1},{3,0},{4,7},{5,6},{6,5},{7,4},{8,11},{9,10},{10,... | collective-permute-start | bytes 491528 | tf_op jit(solution)/shard_map/ppermute | solution.py:49
  39.0 10.5 %copy-start.2 = (bf16[1,2048,352]{1,2,0:T(8,128)(2,1)S(1)}, bf16[1,2048,352]{1,2,0:T(8,128)(2,1)}, u32[]{:S(2)}) copy-start(bf16[1,2048,352]{1,2,0:T(8,128)(2,1)} %param.12) | copy-start | bytes 4325380
  39.1 10.4 %copy-start.1 = (bf16[1,2048,352]{1,2,0:T(8,128)(2,1)S(1)}, bf16[1,2048,352]{1,2,0:T(8,128)(2,1)}, u32[]{:S(2)}) copy-start(bf16[1,2048,352]{1,2,0:T(8,128)(2,1)} %param.11) | copy-start | bytes 4325380
  42.9 28.0 %collective-permute-start.11 = (bf16[352,1280]{1,0:T(8,128)(2,1)S(1)}, bf16[352,1280]{1,0:T(8,128)(2,1)S(1)}, u32[]{:S(2)}, u32[]{:S(2)}) collective-permute-start(bf16[352,1280]{1,0:T(8,128)(2,1)S(1)} %slice.9), channel_id=1, source_target_pairs={{0,16},{1,9},{2,18},{3,11},{4,20},{5,13},{6,22},{7,15},{8,24},{9,1... | collective-permute-start | bytes 2703368 | tf_op jit(solution)/shard_map/ppermute | solution.py:33
  46.1 17.7 %collective-permute-start.12 = (bf16[160,2048]{1,0:T(8,128)(2,1)S(1)}, bf16[160,2048]{1,0:T(8,128)(2,1)S(1)}, u32[]{:S(2)}, u32[]{:S(2)}) collective-permute-start(bf16[160,2048]{1,0:T(8,128)(2,1)S(1)} %shard_map.73.rows_ref), channel_id=1, source_target_pairs={{0,8},{1,17},{2,10},{3,19},{4,12},{5,21},{6,14},{7,23},{8,0},{9,25... | collective-permute-start | bytes 1966088 | tf_op jit(solution)/shard_map/ppermute | solution.py:33
  48.0 22.9 %collective-permute-start.10 = (bf16[352,768]{1,0:T(8,128)(2,1)S(1)}, bf16[352,768]{1,0:T(8,128)(2,1)S(1)}, u32[]{:S(2)}, u32[]{:S(2)}) collective-permute-start(bf16[352,768]{1,0:T(8,128)(2,1)S(1)} %slice.8), channel_id=1, source_target_pairs={{0,16},{1,9},{2,18},{3,11},{4,20},{5,13},{6,22},{7,15},{8,24},{9,1... | collective-permute-start | bytes 1622024 | tf_op jit(solution)/shard_map/ppermute | solution.py:33
  71.8 28.3 %collective-permute-start.15 = (bf16[80,2048]{1,0:T(8,128)(2,1)S(1)}, bf16[80,2048]{1,0:T(8,128)(2,1)S(1)}, u32[]{:S(2)}, u32[]{:S(2)}) collective-permute-start(bf16[80,2048]{1,0:T(8,128)(2,1)S(1)} %get-tuple-element.48), channel_id=1, source_target_pairs={{0,8},{1,17},{2,10},{3,19},{4,12},{5,21},{6,14},{7,23},{8,0},{9,25... | collective-permute-start | bytes 983048 | tf_op jit(solution)/shard_map/ppermute | solution.py:33
  75.0 36.0 %collective-permute-start.28 = (bf16[160,1280]{1,0:T(8,128)(2,1)S(1)}, bf16[160,1280]{1,0:T(8,128)(2,1)S(1)}, u32[]{:S(2)}, u32[]{:S(2)}) collective-permute-start(bf16[160,1280]{1,0:T(8,128)(2,1)S(1)} %shard_map.91), channel_id=1, source_target_pairs={{0,8},{1,17},{2,10},{3,19},{4,12},{5,21},{6,14},{7,23},{8,0},{9,25... | collective-permute-start | bytes 1228808 | tf_op jit(solution)/shard_map/ppermute | solution.py:33
  76.0 21.2 %collective-permute-start.23 = (bf16[160,768]{1,0:T(8,128)(2,1)S(1)}, bf16[160,768]{1,0:T(8,128)(2,1)S(1)}, u32[]{:S(2)}, u32[]{:S(2)}) collective-permute-start(bf16[160,768]{1,0:T(8,128)(2,1)S(1)} %shard_map.88), channel_id=1, source_target_pairs={{0,8},{1,17},{2,10},{3,19},{4,12},{5,21},{6,14},{7,23},{8,0},{9,25... | collective-permute-start | bytes 737288 | tf_op jit(solution)/shard_map/ppermute | solution.py:33
  77.6 1.2 collective-permute-start
  78.8 3.6 %collective-permute-start.1 = (s32[1,8]{1,0:T(1,128)S(1)}, s32[1,8]{1,0:T(1,128)S(1)}, u32[]{:S(2)}, u32[]{:S(2)}) collective-permute-start(s32[1,8]{1,0:T(1,128)S(1)} %add.16), channel_id=1, source_target_pairs={{0,2},{1,3},{2,0},{3,1},{4,6},{5,7},{6,4},{7,5},{8,10},{9,11},{10,... | collective-permute-start | bytes 104 | tf_op jit(solution)/shard_map/ppermute | solution.py:61
  82.3 4.5 %collective-permute-start.2 = (s32[1,8]{1,0:T(1,128)S(1)}, s32[1,8]{1,0:T(1,128)S(1)}, u32[]{:S(2)}, u32[]{:S(2)}) collective-permute-start(s32[1,8]{1,0:T(1,128)S(1)} %add.17), channel_id=1, source_target_pairs={{0,4},{1,5},{2,6},{3,7},{4,0},{5,1},{6,2},{7,3},{8,12},{9,13},{10,... | collective-permute-start | bytes 104 | tf_op jit(solution)/shard_map/ppermute | solution.py:61
  86.8 3.6 %collective-permute-start.3 = (s32[1,8]{1,0:T(1,128)S(1)}, s32[1,8]{1,0:T(1,128)S(1)}, u32[]{:S(2)}, u32[]{:S(2)}) collective-permute-start(s32[1,8]{1,0:T(1,128)S(1)} %add.18), channel_id=1, source_target_pairs={{0,8},{1,9},{2,10},{3,11},{4,12},{5,13},{6,14},{7,15},{8,0},{9,1},... | collective-permute-start | bytes 104 | tf_op jit(solution)/shard_map/ppermute | solution.py:61
  90.4 9.9 %collective-permute-start.4 = (s32[1,8]{1,0:T(1,128)S(1)}, s32[1,8]{1,0:T(1,128)S(1)}, u32[]{:S(2)}, u32[]{:S(2)}) collective-permute-start(s32[1,8]{1,0:T(1,128)S(1)} %add.19), channel_id=1, source_target_pairs={{0,16},{1,17},{2,18},{3,19},{4,20},{5,21},{6,22},{7,23},{8,24},{9,... | collective-permute-start | bytes 104 | tf_op jit(solution)/shard_map/ppermute | solution.py:61
  91.9 18.5 %collective-permute-start.13 = (bf16[80,2048]{1,0:T(8,128)(2,1)S(1)}, bf16[80,2048]{1,0:T(8,128)(2,1)S(1)}, u32[]{:S(2)}, u32[]{:S(2)}) collective-permute-start(bf16[80,2048]{1,0:T(8,128)(2,1)S(1)} %get-tuple-element.44), channel_id=1, source_target_pairs={{0,8},{1,17},{2,10},{3,19},{4,12},{5,21},{6,14},{7,23},{8,0},{9,25... | collective-permute-start | bytes 983048 | tf_op jit(solution)/shard_map/ppermute | solution.py:33
  97.3 5.2 %collective-permute-start.24 = (bf16[40,768]{1,0:T(8,128)(2,1)S(1)}, bf16[40,768]{1,0:T(8,128)(2,1)S(1)}, u32[]{:S(2)}, u32[]{:S(2)}) collective-permute-start(bf16[40,768]{1,0:T(8,128)(2,1)S(1)} %get-tuple-element.55), channel_id=1, source_target_pairs={{0,4},{1,5},{2,6},{3,7},{4,0},{5,1},{6,2},{7,3},{8,12},{9,13},{10,... | collective-permute-start | bytes 184328 | tf_op jit(solution)/shard_map/ppermute | solution.py:49
  100.1 17.8 %collective-permute-start.16 = (bf16[40,2048]{1,0:T(8,128)(2,1)S(1)}, bf16[40,2048]{1,0:T(8,128)(2,1)S(1)}, u32[]{:S(2)}, u32[]{:S(2)}) collective-permute-start(bf16[40,2048]{1,0:T(8,128)(2,1)S(1)} %get-tuple-element.49), channel_id=1, source_target_pairs={{0,2},{1,3},{2,0},{3,1},{4,6},{5,7},{6,4},{7,5},{8,10},{9,11},{10,... | collective-permute-start | bytes 491528 | tf_op jit(solution)/shard_map/ppermute | solution.py:49
  100.3 20.1 %collective-permute-start.17 = (bf16[40,2048]{1,0:T(8,128)(2,1)S(1)}, bf16[40,2048]{1,0:T(8,128)(2,1)S(1)}, u32[]{:S(2)}, u32[]{:S(2)}) collective-permute-start(bf16[40,2048]{1,0:T(8,128)(2,1)S(1)} %get-tuple-element.50), channel_id=1, source_target_pairs={{0,3},{1,2},{2,1},{3,0},{4,7},{5,6},{6,5},{7,4},{8,11},{9,10},{10,... | collective-permute-start | bytes 491528 | tf_op jit(solution)/shard_map/ppermute | solution.py:49
  102.5 5.4 %collective-permute-start.25 = (bf16[40,768]{1,0:T(8,128)(2,1)S(1)}, bf16[40,768]{1,0:T(8,128)(2,1)S(1)}, u32[]{:S(2)}, u32[]{:S(2)}) collective-permute-start(bf16[40,768]{1,0:T(8,128)(2,1)S(1)} %get-tuple-element.56), channel_id=1, source_target_pairs={{0,5},{1,4},{2,7},{3,6},{4,1},{5,0},{6,3},{7,2},{8,13},{9,12},{10,... | collective-permute-start | bytes 184328 | tf_op jit(solution)/shard_map/ppermute | solution.py:49
  107.9 6.1 %collective-permute-start.26 = (bf16[40,768]{1,0:T(8,128)(2,1)S(1)}, bf16[40,768]{1,0:T(8,128)(2,1)S(1)}, u32[]{:S(2)}, u32[]{:S(2)}) collective-permute-start(bf16[40,768]{1,0:T(8,128)(2,1)S(1)} %get-tuple-element.57), channel_id=1, source_target_pairs={{0,6},{1,7},{2,4},{3,5},{4,2},{5,3},{6,0},{7,1},{8,14},{9,15},{10,... | collective-permute-start | bytes 184328 | tf_op jit(solution)/shard_map/ppermute | solution.py:49
  110.4 7.1 %collective-permute-start.27 = (bf16[40,768]{1,0:T(8,128)(2,1)S(1)}, bf16[40,768]{1,0:T(8,128)(2,1)S(1)}, u32[]{:S(2)}, u32[]{:S(2)}) collective-permute-start(bf16[40,768]{1,0:T(8,128)(2,1)S(1)} %get-tuple-element.58), channel_id=1, source_target_pairs={{0,7},{1,6},{2,5},{3,4},{4,3},{5,2},{6,1},{7,0},{8,15},{9,14},{10,... | collective-permute-start | bytes 184328 | tf_op jit(solution)/shard_map/ppermute | solution.py:49
  111.0 10.5 %copy-start.5 = (s32[128,2]{0,1:T(2,128)S(1)}, s32[128,2]{0,1:T(2,128)}, u32[]{:S(2)}) copy-start(s32[128,2]{0,1:T(2,128)} %param.8) | copy-start | bytes 3076
  111.0 10.5 %copy-start.6 = (s32[128,2]{0,1:T(2,128)S(1)}, s32[128,2]{0,1:T(2,128)}, u32[]{:S(2)}) copy-start(s32[128,2]{0,1:T(2,128)} %param.9) | copy-start | bytes 3076
  111.0 10.5 %copy-start.7 = (s32[8]{0:T(128)S(1)}, s32[8]{0:T(128)}, u32[]{:S(2)}) copy-start(s32[8]{0:T(128)} %param.10) | copy-start | bytes 100
  111.0 10.8 %collective-permute-start.14 = (bf16[40,2048]{1,0:T(8,128)(2,1)S(1)}, bf16[40,2048]{1,0:T(8,128)(2,1)S(1)}, u32[]{:S(2)}, u32[]{:S(2)}) collective-permute-start(bf16[40,2048]{1,0:T(8,128)(2,1)S(1)} %get-tuple-element.46), channel_id=1, source_target_pairs={{0,1},{1,0},{2,3},{3,2},{4,5},{5,4},{6,7},{7,6},{8,9},{9,8},{10,11... | collective-permute-start | bytes 491528 | tf_op jit(solution)/shard_map/ppermute | solution.py:49
  114.0 7.8 %collective-permute-start.29 = (bf16[40,1280]{1,0:T(8,128)(2,1)S(1)}, bf16[40,1280]{1,0:T(8,128)(2,1)S(1)}, u32[]{:S(2)}, u32[]{:S(2)}) collective-permute-start(bf16[40,1280]{1,0:T(8,128)(2,1)S(1)} %get-tuple-element.59), channel_id=1, source_target_pairs={{0,4},{1,5},{2,6},{3,7},{4,0},{5,1},{6,2},{7,3},{8,12},{9,13},{10,... | collective-permute-start | bytes 307208 | tf_op jit(solution)/shard_map/ppermute | solution.py:49
  117.5 13.6 %collective-permute-start.30 = (bf16[40,1280]{1,0:T(8,128)(2,1)S(1)}, bf16[40,1280]{1,0:T(8,128)(2,1)S(1)}, u32[]{:S(2)}, u32[]{:S(2)}) collective-permute-start(bf16[40,1280]{1,0:T(8,128)(2,1)S(1)} %get-tuple-element.60), channel_id=1, source_target_pairs={{0,5},{1,4},{2,7},{3,6},{4,1},{5,0},{6,3},{7,2},{8,13},{9,12},{10,... | collective-permute-start | bytes 307208 | tf_op jit(solution)/shard_map/ppermute | solution.py:49
  118.0 13.1 %collective-permute-start.31 = (bf16[40,1280]{1,0:T(8,128)(2,1)S(1)}, bf16[40,1280]{1,0:T(8,128)(2,1)S(1)}, u32[]{:S(2)}, u32[]{:S(2)}) collective-permute-start(bf16[40,1280]{1,0:T(8,128)(2,1)S(1)} %get-tuple-element.61), channel_id=1, source_target_pairs={{0,6},{1,7},{2,4},{3,5},{4,2},{5,3},{6,0},{7,1},{8,14},{9,15},{10,... | collective-permute-start | bytes 307208 | tf_op jit(solution)/shard_map/ppermute | solution.py:49
  120.4 10.7 %collective-permute-start.32 = (bf16[40,1280]{1,0:T(8,128)(2,1)S(1)}, bf16[40,1280]{1,0:T(8,128)(2,1)S(1)}, u32[]{:S(2)}, u32[]{:S(2)}) collective-permute-start(bf16[40,1280]{1,0:T(8,128)(2,1)S(1)} %get-tuple-element.62), channel_id=1, source_target_pairs={{0,7},{1,6},{2,5},{3,4},{4,3},{5,2},{6,1},{7,0},{8,15},{9,14},{10,... | collective-permute-start | bytes 307208 | tf_op jit(solution)/shard_map/ppermute | solution.py:49
